TPU v7x, 32 devices: a whole 2x2x4 slice. The times are simulated.
32 devices in a mesh: band: 4 (over x, core), grid: 8 (over z, y).
Axes of the slice: x: 2, y: 2, z: 4, core: 2. Of those that a mesh axis runs over, the one named last changes fastest.
Arguments:
- orbitals: bfloat16 [16384, 2048], P('grid', 'band'), may hold values from -6 to 6
- projectors: bfloat16 [64, 8, 128], replicated, may hold values from -0.5 to 0.5
- sphere_start: int32 [64], replicated, may hold values from 0 to 1920, as said below
- proj_count: int32 [64], replicated, may hold values from 1 to 8
- owner_slab: int32 [64], replicated, may hold values from 0 to 7, as said below
- correlation_coef: float32 [64, 8, 8], replicated, as said below
Outputs:
- rotated: bfloat16 [16384, 2048], P(('grid', 'band'))
Inputs may be any that keep to these rules, and one draw needn't show every extreme that they name: `sphere_start`: a multiple of 128. `owner_slab`: every slab owns exactly 8 atoms. `correlation_coef`: each atom's matrix is symmetric positive definite.
All inputs are finite; a program needn't handle non-finite values.
Results may differ from a plain program's by a relative error of at most 0.0049.
Values may be sent and summed in bfloat16 or wider, within the bound.
No kernel may reach another device: no remote copies, remote signals or barrier semaphores. Data moves between devices by JAX's collectives and lax.ppermute only.
A program may use at most 128 MiB of HBM per device.

v0:
```python
import jax
import jax.numpy as jnp
from jax import lax
from jax.sharding import PartitionSpec as P

SPH = 128
NPMAX = 8
A_SLAB = 8


def inverse_factor(matrix):
    order = matrix.shape[0]
    if order <= 512 or order % 2 != 0:
        lower = jnp.linalg.cholesky(matrix)
        identity = jnp.eye(order, dtype=matrix.dtype)
        return lax.linalg.triangular_solve(lower, identity, left_side=True, lower=True)
    half = order // 2
    upper_inv = inverse_factor(matrix[:half, :half])
    below = jnp.dot(matrix[half:, :half], upper_inv.T, precision=lax.Precision.HIGHEST)
    schur = matrix[half:, half:] - jnp.dot(below, below.T, precision=lax.Precision.HIGHEST)
    lower_inv = inverse_factor(schur)
    corner = -jnp.dot(
        lower_inv,
        jnp.dot(below, upper_inv, precision=lax.Precision.HIGHEST),
        precision=lax.Precision.HIGHEST,
    )
    top = jnp.concatenate([upper_inv, jnp.zeros((half, order - half), matrix.dtype)], axis=1)
    bottom = jnp.concatenate([corner, lower_inv], axis=1)
    return jnp.concatenate([top, bottom], axis=0)


def slab_atoms(owner_slab, slab):
    atoms = owner_slab.shape[0]
    keyed = jnp.where(owner_slab == slab, 0, 1) * atoms + jnp.arange(atoms, dtype=jnp.int32)
    return jnp.argsort(keyed, stable=True)[:A_SLAB]


def atom_terms(source, weights, starts, counts, coefs, valid):

    def take_rows(offset):
        return lax.dynamic_slice_in_dim(source, offset, SPH, 0)

    sphere_rows = jax.vmap(take_rows)(starts)
    correlations = jnp.einsum(
        "aij,ajn->ain", weights, sphere_rows, preferred_element_type=jnp.float32
    )
    active = (jnp.arange(NPMAX)[None, :] < counts[:, None]) & valid[:, None]
    correlations = jnp.where(active[:, :, None], correlations, jnp.zeros_like(correlations))
    weighted = jnp.einsum("aij,ajn->ain", coefs, correlations, precision=lax.Precision.HIGHEST)
    return (correlations, weighted)


def shards(orbitals, projectors, sphere_start, proj_count, owner_slab, correlation_coef):
    band_index = lax.axis_index("band")
    slab = lax.axis_index("grid")
    total_rows = orbitals.shape[0] * lax.axis_size("grid")
    chosen = slab_atoms(owner_slab, slab)
    weights = projectors[chosen]
    counts = proj_count[chosen]
    coefs = correlation_coef[chosen]
    mine = lax.all_to_all(orbitals, "band", split_axis=0, concat_axis=1, tiled=True)
    height = mine.shape[0]
    width_all = mine.shape[1]
    gram = jnp.dot(mine.T, mine, preferred_element_type=jnp.float32) * (1.0 / total_rows)
    offsets = sphere_start[chosen] - band_index * height
    valid = (offsets >= 0) & (offsets < height)
    offsets = jnp.clip(offsets, 0, height - SPH)
    correlations, weighted = atom_terms(mine, weights, offsets, counts, coefs, valid)
    paw = jnp.dot(
        weighted.reshape(-1, width_all).T,
        correlations.reshape(-1, width_all),
        precision=lax.Precision.HIGHEST,
    )
    metric = lax.psum(gram + paw, ("band", "grid"))
    inverse = inverse_factor(metric).astype(jnp.bfloat16)
    return jnp.dot(mine, inverse.T, preferred_element_type=jnp.float32).astype(jnp.bfloat16)


def solution(mesh):
    in_specs = (P("grid", "band"), P(), P(), P(), P(), P())
    out_specs = P(("grid", "band"), None)
    return jax.shard_map(shards, mesh=mesh, in_specs=in_specs, out_specs=out_specs, check_vma=False)
```

profile of v0, /device:TPU:0, one launch (start us, length us, event | category | flops | bytes accessed | tf_op | source)
XLA Modules:
  0.0 1109.8 jit_solution(1387231611529632680)
XLA Ops:
  6.5 4.6 all-to-all-start
  16.0 21.5 %all-to-all-done = bf16[4,512,512]{2,1,0:T(8,128)(2,1)} async-done(((bf16[4,512,512]{2,1,0:T(8,128)(2,1)}), bf16[4,512,512]{2,1,0:T(8,128)(2,1)}, u32[]{:S(2)}, u32[]{:S(2)}) %all-to-all-start) | async-done | bytes 2097184 | tf_op jit(solution)/shard_map/all_to_all | solution.py:61
  37.6 2.8 copy.48
  40.3 20.2 %while.9 = (s32[]{:T(128)}, bf16[512,2048]{0,1:T(8,128)(2,1)S(1)}, s32[8,2]{0,1:T(2,128)S(1)}, bf16[8,128,2048]{2,1,0:T(8,128)(2,1)}, s32[]{:T(128)}) while((s32[]{:T(128)}, bf16[512,2048]{0,1:T(8,128)(2,1)S(1)}, s32[8,2]{0,1:T(2,128)S(1)}, bf16[8,128,2048]{2,1,0:T(8,128)(2,1)}, s32[]{:T(128)}) %tuple.122), condition=%wide.while_cond.1, body=%wide.while_body.1.sunk | while | flops 2 | bytes 3146333 | solution.py:41
  60.5 3.6 convolution_select_fusion
  64.7 14.1 %fusion.178 = f32[2048,2048,1]{0,1,2:T(8,128)S(1)} fusion(f32[8,8,2048]{2,1,0:T(8,128)S(1)} %fusion.177, f32[8,8,2048]{2,1,0:T(8,128)S(1)} %convolution_select_fusion), kind=kOutput, calls=%fused_computation.329 | convolution fusion | flops 3221225472 | bytes 17825792 | tf_op jit(solution)/shard_map/dot_general | solution.py:69
  78.8 12.9 %bitcast_add_fusion = f32[2048,2048]{0,1:T(8,128)} fusion(f32[2048,2048,1]{0,1,2:T(8,128)S(1)} %fusion.178, bf16[512,2048]{0,1:T(8,128)(2,1)} %copy-done.4), kind=kOutput, calls=%fused_computation.16 | convolution fusion | flops 4303355904 | bytes 35651584 | tf_op jit(solution)/shard_map/dot_general | solution.py:64
  91.9 279.4 %all-reduce.7.cloned.1.call-done = f32[2048,2048]{0,1:T(8,128)} async-done(((f32[2048,2048]{0,1:T(8,128)}), f32[2048,2048]{0,1:T(8,128)}) %all-reduce.7.cloned.1.call-update) | async-done | bytes 16777232 | tf_op jit(solution)/shard_map/psum | solution.py:74
  374.4 11.7 %cholesky.462 = f32[128,128]{1,0:T(8,128)S(1)} custom-call(f32[128,128]{1,0:T(8,128)S(1)} %cholesky.746), custom_call_target="Cholesky" | custom-call | tf_op jit(solution)/shard_map/jit(cholesky)/cholesky | solution.py:14
  386.1 9.9 custom-call.35
  396.9 11.7 %cholesky.481 = f32[128,128]{1,0:T(8,128)S(1)} custom-call(f32[128,128]{1,0:T(8,128)S(1)} %cholesky.750), custom_call_target="Cholesky" | custom-call | tf_op jit(solution)/shard_map/jit(cholesky)/cholesky | solution.py:14
  408.6 9.8 custom-call.36
  419.1 11.9 %cholesky.502 = f32[128,128]{1,0:T(8,128)S(1)} custom-call(f32[128,128]{1,0:T(8,128)S(1)} %cholesky.755), custom_call_target="Cholesky" | custom-call | tf_op jit(solution)/shard_map/jit(cholesky)/cholesky | solution.py:14
  431.7 9.8 custom-call.37
  442.1 11.7 %cholesky.519 = f32[128,128]{1,0:T(8,128)S(1)} custom-call(f32[128,128]{1,0:T(8,128)S(1)} %convolution_subtract_fusion.25), custom_call_target="Cholesky" | custom-call | tf_op jit(solution)/shard_map/jit(cholesky)/cholesky | solution.py:14
  457.9 8.1 while.10
  466.0 39.7 %custom-call.38 = f32[4,128,128]{1,2,0:T(8,128)S(1)} custom-call(f32[4,128,128]{2,1,0:T(8,128)S(1)} %get-tuple-element.43), custom_call_target="InvertDiagBlocksLowerTriangular" | custom-call | tf_op jit(solution)/shard_map/triangular_solve/custom-call.3 | solution.py:16
  509.9 4.7 fusion.21
  516.5 3.1 convolution_subtract_fusion.1
  523.4 11.9 %cholesky.534 = f32[128,128]{1,0:T(8,128)S(1)} custom-call(f32[128,128]{1,0:T(8,128)S(1)} %cholesky.759), custom_call_target="Cholesky" | custom-call | tf_op jit(solution)/shard_map/jit(cholesky)/cholesky | solution.py:14
  535.5 9.8 custom-call.39
  547.8 11.7 %cholesky.553 = f32[128,128]{1,0:T(8,128)S(1)} custom-call(f32[128,128]{1,0:T(8,128)S(1)} %cholesky.763), custom_call_target="Cholesky" | custom-call | tf_op jit(solution)/shard_map/jit(cholesky)/cholesky | solution.py:14
  560.9 9.8 custom-call.40
  572.3 12.1 %cholesky.574 = f32[128,128]{1,0:T(8,128)S(1)} custom-call(f32[128,128]{1,0:T(8,128)S(1)} %cholesky.768), custom_call_target="Cholesky" | custom-call | tf_op jit(solution)/shard_map/jit(cholesky)/cholesky | solution.py:14
  585.1 9.8 custom-call.41
  596.4 11.7 %cholesky.591 = f32[128,128]{1,0:T(8,128)S(1)} custom-call(f32[128,128]{1,0:T(8,128)S(1)} %convolution_subtract_fusion.24), custom_call_target="Cholesky" | custom-call | tf_op jit(solution)/shard_map/jit(cholesky)/cholesky | solution.py:14
  612.4 11.7 %while.11 = (s32[]{:T(128)}, f32[512,512]{1,0:T(8,128)}, s32[4,2]{0,1:T(2,128)S(1)}, f32[4,128,128]{2,1,0:T(8,128)S(1)}, s32[]{:T(128)}) while((s32[]{:T(128)}, f32[512,512]{1,0:T(8,128)}, s32[4,2]{0,1:T(2,128)S(1)}, f32[4,128,128]{2,1,0:T(8,128)S(1)}, s32[]{:T(128)}) %tuple.123), condition=%wide.while_cond.clone, body=%wide.while_body.clone.sunk | while | flops 2 | bytes 131181 | solution.py:16
  613.0 2.2 bitcast_dynamic-update-slice_fusion.12
  616.0 2.2 bitcast_dynamic-update-slice_fusion.12
  624.0 39.3 %custom-call.42 = f32[4,128,128]{1,2,0:T(8,128)S(1)} custom-call(f32[4,128,128]{2,1,0:T(8,128)S(1)} %get-tuple-element.44), custom_call_target="InvertDiagBlocksLowerTriangular" | custom-call | tf_op jit(solution)/shard_map/triangular_solve/custom-call.3 | solution.py:16
  672.0 28.8 %fusion.9 = f32[1024,1024]{1,0:T(8,128)S(1)} fusion(f32[2048,2048]{0,1:T(8,128)} %all-reduce.7.cloned.1.call-done, f32[512,512]{1,0:T(8,128)S(1)} %copy-done.9, f32[128,512]{1,0:T(8,128)S(1)} %fusion.126, f32[128,512]{1,0:T(8,128)S(1)} %fusion.127, f32[128,512]{1,0:T(8,128)S(1)} %fusion.129, f32[128,512]{1,0:T(8,128)S(1)} %fusion.82, ...), kind=kOutput, calls=%fused_computation.26 | convolution fusion | flops 12892241920 | bytes 11534336 | tf_op jit(solution)/shard_map/dot_general | solution.py:19
  700.9 16.8 %fusion.171 = f32[1024,1024]{1,0:T(8,128)} fusion(f32[1024,1024]{1,0:T(8,128)S(1)} %fusion.9, f32[512,512]{1,0:T(8,128)S(1)} %copy-done.9, f32[128,512]{1,0:T(8,128)S(1)} %fusion.126, f32[128,512]{1,0:T(8,128)S(1)} %fusion.127, f32[128,512]{1,0:T(8,128)S(1)} %fusion.129, f32[128,512]{1,0:T(8,128)S(1)} %fusion.82, f32[512,512]{1,0:T(8,128)S(1)} %convolution_negate_fusion.1), kind=kOutput, calls=%fused_computation.322 | convolution fusion | flops 12892241920 | bytes 11534336 | tf_op jit(solution)/shard_map/dot_general | solution.py:24
  717.7 15.8 %slice_subtract_fusion = f32[1024,1024]{0,1:T(8,128)S(1)} fusion(f32[2048,2048]{0,1:T(8,128)} %all-reduce.7.cloned.1.call-done, f32[1024,1024]{1,0:T(8,128)S(1)} %fusion.9), kind=kOutput, calls=%fused_computation.28 | convolution fusion | flops 12885950464 | bytes 16777216 | tf_op jit(solution)/shard_map/dot_general | solution.py:20
  740.4 11.7 %cholesky.606 = f32[128,128]{1,0:T(8,128)S(1)} custom-call(f32[128,128]{1,0:T(8,128)S(1)} %cholesky.772), custom_call_target="Cholesky" | custom-call | tf_op jit(solution)/shard_map/jit(cholesky)/cholesky | solution.py:14
  752.3 9.8 custom-call.43
  764.7 11.7 %cholesky.625 = f32[128,128]{1,0:T(8,128)S(1)} custom-call(f32[128,128]{1,0:T(8,128)S(1)} %cholesky.776), custom_call_target="Cholesky" | custom-call | tf_op jit(solution)/shard_map/jit(cholesky)/cholesky | solution.py:14
  777.8 10.2 custom-call.44
  789.5 11.7 %cholesky.646 = f32[128,128]{1,0:T(8,128)S(1)} custom-call(f32[128,128]{1,0:T(8,128)S(1)} %cholesky.781), custom_call_target="Cholesky" | custom-call | tf_op jit(solution)/shard_map/jit(cholesky)/cholesky | solution.py:14
  802.0 9.8 custom-call.45
  813.2 11.7 %cholesky.663 = f32[128,128]{1,0:T(8,128)S(1)} custom-call(f32[128,128]{1,0:T(8,128)S(1)} %convolution_subtract_fusion.23), custom_call_target="Cholesky" | custom-call | tf_op jit(solution)/shard_map/jit(cholesky)/cholesky | solution.py:14
  829.4 11.7 %while.12 = (s32[]{:T(128)}, f32[512,512]{1,0:T(8,128)}, s32[4,2]{0,1:T(2,128)S(1)}, f32[4,128,128]{2,1,0:T(8,128)S(1)}, s32[]{:T(128)}) while((s32[]{:T(128)}, f32[512,512]{1,0:T(8,128)}, s32[4,2]{0,1:T(2,128)S(1)}, f32[4,128,128]{2,1,0:T(8,128)S(1)}, s32[]{:T(128)}) %tuple.124), condition=%wide.while_cond.clone.1, body=%wide.while_body.clone.1.sunk | while | flops 2 | bytes 131181 | solution.py:16
  830.0 2.3 bitcast_dynamic-update-slice_fusion.13
  833.0 2.3 bitcast_dynamic-update-slice_fusion.13
  835.9 2.3 bitcast_dynamic-update-slice_fusion.13
  841.0 39.3 %custom-call.46 = f32[4,128,128]{1,2,0:T(8,128)S(1)} custom-call(f32[4,128,128]{2,1,0:T(8,128)S(1)} %get-tuple-element.45), custom_call_target="InvertDiagBlocksLowerTriangular" | custom-call | tf_op jit(solution)/shard_map/triangular_solve/custom-call.3 | solution.py:16
  887.5 3.6 fusion.19
  891.0 2.8 fusion.169
  895.8 7.4 fusion.172
  907.0 11.7 %cholesky.678 = f32[128,128]{1,0:T(8,128)S(1)} custom-call(f32[128,128]{1,0:T(8,128)S(1)} %cholesky.785), custom_call_target="Cholesky" | custom-call | tf_op jit(solution)/shard_map/jit(cholesky)/cholesky | solution.py:14
  918.8 9.8 custom-call.47
  931.2 11.7 %cholesky.697 = f32[128,128]{1,0:T(8,128)S(1)} custom-call(f32[128,128]{1,0:T(8,128)S(1)} %cholesky.789), custom_call_target="Cholesky" | custom-call | tf_op jit(solution)/shard_map/jit(cholesky)/cholesky | solution.py:14
  944.3 10.0 custom-call.48
  955.8 11.7 %cholesky.718 = f32[128,128]{1,0:T(8,128)S(1)} custom-call(f32[128,128]{1,0:T(8,128)S(1)} %cholesky.794), custom_call_target="Cholesky" | custom-call | tf_op jit(solution)/shard_map/jit(cholesky)/cholesky | solution.py:14
  968.3 9.8 custom-call.49
  979.5 11.7 %cholesky.735 = f32[128,128]{1,0:T(8,128)S(1)} custom-call(f32[128,128]{1,0:T(8,128)S(1)} %convolution_subtract_fusion.22), custom_call_target="Cholesky" | custom-call | tf_op jit(solution)/shard_map/jit(cholesky)/cholesky | solution.py:14
  995.8 11.7 %while.13 = (s32[]{:T(128)}, f32[512,512]{1,0:T(8,128)}, s32[4,2]{0,1:T(2,128)S(1)}, f32[4,128,128]{2,1,0:T(8,128)S(1)}, s32[]{:T(128)}) while((s32[]{:T(128)}, f32[512,512]{1,0:T(8,128)}, s32[4,2]{0,1:T(2,128)S(1)}, f32[4,128,128]{2,1,0:T(8,128)S(1)}, s32[]{:T(128)}) %tuple.125), condition=%wide.while_cond.clone.2, body=%wide.while_body.clone.2.sunk | while | flops 2 | bytes 131181 | solution.py:16
  996.4 2.3 bitcast_dynamic-update-slice_fusion.14
  999.4 2.3 bitcast_dynamic-update-slice_fusion.14
  1002.3 2.3 bitcast_dynamic-update-slice_fusion.14
  1007.5 39.3 %custom-call.50 = f32[4,128,128]{1,2,0:T(8,128)S(1)} custom-call(f32[4,128,128]{2,1,0:T(8,128)S(1)} %get-tuple-element.46), custom_call_target="InvertDiagBlocksLowerTriangular" | custom-call | tf_op jit(solution)/shard_map/triangular_solve/custom-call.3 | solution.py:16
  1054.6 6.0 fusion.18
  1060.6 13.6 %negate_convert_fusion = bf16[1024,1024]{1,0:T(8,128)(2,1)S(1)} fusion(f32[1024,1024]{1,0:T(8,128)S(1)} %copy-done.23, f32[512,512]{1,0:T(8,128)S(1)} %copy-done.11, f32[128,512]{1,0:T(8,128)S(1)} %fusion.114, f32[128,512]{1,0:T(8,128)S(1)} %fusion.115, f32[128,512]{1,0:T(8,128)S(1)} %fusion.117, f32[128,512]{1,0:T(8,128)S(1)} %fusion.78, ...), kind=kOutput, calls=%fused_computation.32 | convolution fusion | flops 12894339072 | bytes 9437184 | tf_op jit(solution)/shard_map/dot_general | solution.py:22
  1074.3 25.8 %fusion.15 = bf16[512,2048]{0,1:T(8,128)(2,1)S(1)} fusion(bf16[512,2048]{0,1:T(8,128)(2,1)S(1)} %copy-done.5, bf16[1024,1024]{1,0:T(8,128)(2,1)S(1)} %copy-done.19, bf16[1024,1024]{1,0:T(8,128)(2,1)S(1)} %fusion.18, bf16[1024,1024]{1,0:T(8,128)(2,1)S(1)} %negate_convert_fusion), kind=kOutput, calls=%fused_computation.34 | convolution fusion | flops 4329570304 | bytes 10485760 | tf_op jit(solution)/shard_map/dot_general | solution.py:76
  1100.0 2.4 copy.63
  (272 shorter events, 132.3 us)
Async XLA Ops:
  6.5 8.1 copy-start
  6.5 4.7 copy-start.22
  6.5 6.8 copy-start.2
  6.5 7.4 copy-start.3
  6.5 8.7 copy-start.21
  6.5 31.0 %all-to-all-start = ((bf16[4,512,512]{2,1,0:T(8,128)(2,1)}), bf16[4,512,512]{2,1,0:T(8,128)(2,1)}, u32[]{:S(2)}, u32[]{:S(2)}) async-start(bf16[4,512,512]{2,1,0:T(8,128)(2,1)} %bitcast.231), calls=%async_computation | async-start | bytes 4194304 | tf_op jit(solution)/shard_map/all_to_all | solution.py:61
  11.1 360.1 %all-reduce.7.cloned.1.call-start = ((), (), s32[]{:S(2)}) async-start(), calls=%async_computation.1 | async-start | bytes 33554432 | tf_op jit(solution)/shard_map/psum | solution.py:74
  60.5 3.6 copy-start.4
  522.4 1.0 copy-start.14
  663.4 3.5 copy-start.20
  663.8 8.2 copy-start.9
  670.1 30.7 %copy-start.17 = (f32[128,512]{1,0:T(8,128)}, f32[128,512]{1,0:T(8,128)S(1)}, u32[]{:S(2)}) copy-start(f32[128,512]{1,0:T(8,128)S(1)} %fusion.126) | copy-start | bytes 786436
  672.0 28.9 %copy-start.6 = (f32[512,512]{1,0:T(8,128)}, f32[512,512]{1,0:T(8,128)S(1)}, u32[]{:S(2)}) copy-start(f32[512,512]{1,0:T(8,128)S(1)} %convolution_negate_fusion.1) | copy-start | bytes 3145732
  733.5 1.9 copy-start.12
  739.5 1.0 copy-start.16
  880.3 7.1 copy-start.13
  891.0 4.8 copy-start.7
  891.0 4.8 copy-start.10
  891.0 4.8 copy-start.18
  906.0 1.0 copy-start.15
  994.4 58.3 %copy-start.8 = (f32[512,512]{1,0:T(8,128)S(1)}, f32[512,512]{1,0:T(8,128)}, u32[]{:S(2)}) copy-start(f32[512,512]{1,0:T(8,128)} %fusion.169) | copy-start | bytes 3145732
  1047.2 7.4 copy-start.11
  1052.7 7.9 copy-start.23
  1060.6 13.7 %copy-start.5 = (bf16[512,2048]{0,1:T(8,128)(2,1)S(1)}, bf16[512,2048]{0,1:T(8,128)(2,1)}, u32[]{:S(2)}) copy-start(bf16[512,2048]{0,1:T(8,128)(2,1)} %copy-done.4) | copy-start | bytes 6291460
  1060.6 13.7 %copy-start.19 = (bf16[1024,1024]{1,0:T(8,128)(2,1)S(1)}, bf16[1024,1024]{1,0:T(8,128)(2,1)}, u32[]{:S(2)}) copy-start(bf16[1024,1024]{1,0:T(8,128)(2,1)} %fusion.172) | copy-start | bytes 6291460
  1074.3 28.2 %copy-start.1 = (bf16[64,8,128]{2,1,0:T(8,128)(2,1)S(1)}, bf16[64,8,128]{2,1,0:T(8,128)(2,1)}, u32[]{:S(2)}) copy-start(bf16[64,8,128]{2,1,0:T(8,128)(2,1)} %param.10) | copy-start | bytes 393220
Sparse Core Ops, SparseCore 0:
  91.8 279.3 all-reduce.6
where the time goes:
time: 1120 us; the launch traced here: 1110 us
  other arithmetic  502 us (45%)
  waiting for transfers between devices  301 us (27%)
  matrix products  194 us (17%)
  local copies, waits for them, and re-layouts  83.1 us (7%)
  between operations  25.2 us (2%)
    another operation x59, other arithmetic, inverse_factor(): lower = jnp.linalg.cholesky(matrix)  317 us
    psum x1, waiting for transfers between devices, shards(): metric = lax.psum(gram + paw, ('band', 'grid'))  279 us
    another operation x11, other arithmetic, inverse_factor(): lax.linalg.triangular_solve(lower, identity, left_side=True, lower=True)  163 us
    another operation x53, local copies, waits for them, and re-layouts, inverse_factor(): lax.linalg.triangular_solve(lower, identity, left_side=True, lower=True)  42.9 us
    dot_general x3, matrix products, inverse_factor(): jnp.dot(matrix[half:, :half], upper_inv.T, precision=lax.Precision.HIGHEST)  37.1 us
    dot_general x1, matrix products, shards(): jnp.dot(mine, inverse.T, preferred_element_type=jnp.float32)  25.8 us
  transfers between devices with their start and end apart: 2, of which 2 were waited for; matrix products, arithmetic and copies ran while one was open for 0% of the time, Pallas kernels for 0%

commit v1 on v0

v1 whole, which is shorter than its diff:
```python
import functools

import jax, jax.numpy as jnp
from jax import lax
from jax.experimental import pallas as pl
from jax.experimental.pallas import tpu as pltpu
from jax.sharding import PartitionSpec as P
f32,bf16=jnp.float32,jnp.bfloat16

def split(x):
    hi=x.astype(bf16)
    return hi,(x-hi.astype(f32)).astype(bf16)

def dotg(a,b,ca,cb):
    return lax.dot_general(a,b,(((ca,),(cb,)),((),())),preferred_element_type=f32)

def dot3(a,b,ca=1,cb=0):
    ah,al=split(a); bh,bl=split(b)
    return dotg(ah,bh,ca,cb)+(dotg(ah,bl,ca,cb)+dotg(al,bh,ca,cb))

def inverse_root(m):
    n=m.shape[0]
    lane=lax.broadcasted_iota(jnp.int32,(8,n),1)
    sub=lax.broadcasted_iota(jnp.int32,(8,n),0)
    def step(o,piv):
        k0=pl.multiple_of(o*8,8)
        rows=[jnp.broadcast_to(m[pl.ds(k0+k,1),:],(8,n)) for k in range(8)]
        idx=[jnp.full((8,n),k0+k,jnp.int32) for k in range(8)]
        s=[[None]*8 for _ in range(8)]
        for i in range(8):
            for k in range(i,8):
                s[i][k]=jnp.take_along_axis(rows[i],idx[k],axis=1)
        mult=[[None]*8 for _ in range(8)]
        inv=[None]*8
        for k in range(8):
            inv[k]=1.0/s[k][k]
            piv=jnp.where(lane==k0+k,s[k][k],piv)
            for j in range(k+1,8):
                mult[k][j]=s[k][j]*inv[k]
            for i in range(k+1,8):
                for j in range(i,8):
                    s[i][j]=s[i][j]-mult[k][i]*s[k][j]
            for j in range(k+1,8):
                rows[j]=rows[j]-mult[k][j]*rows[k]
        after=lane>k0+7
        r=[jnp.where(after,rows[k]*inv[k],jnp.where(lane==k0+k,-1.0,0.0)) for k in range(8)]
        for i in range(6,-1,-1):
            for k in range(7,i,-1):
                r[i]=r[i]-mult[i][k]*r[k]
        inside=(lane>=k0)&(lane<k0+8)
        for b in range(n//8):
            blk=m[b*8:b*8+8,:]
            new=jnp.where(inside,0.0,blk)
            for k in range(8):
                new=new-jnp.take_along_axis(blk,idx[k],axis=1)*r[k]
            m[b*8:b*8+8,:]=new
        own=-r[0]
        for k in range(1,8):
            own=jnp.where(sub==k,-r[k],own)
        m[pl.ds(k0,8),:]=own
        return piv
    return lax.fori_loop(0,n//8,step,jnp.ones((8,n),f32))

def invert_block(s,m,t):
    h=s.shape[0]//2
    m[...]=s[:h,:h]
    piv=inverse_root(m)
    t1=m[...]*lax.rsqrt(piv[0:1,:])
    low=dot3(s[h:,:h],t1)
    m[...]=s[h:,h:]-dot3(low,low,1,1)
    piv=inverse_root(m)
    t2=m[...]*lax.rsqrt(piv[0:1,:])
    t[:h,:h]=t1
    t[h:,h:]=t2
    t[h:,:h]=jnp.zeros((h,h),f32)
    t[:h,h:]=-dot3(t1,dot3(low,t2,0,0))

def factor_kernel(passes,a_ref,o_ref,y_ref,hi,lo,m,t,s,xb):
    nb=o_ref.shape[1]; B=256; n=nb//B; orow=o_ref.shape[0]
    off=0
    for p in range(n):
        K=p*B
        def upd(I,x):
            if p==0: return x
            rI=pl.ds(pl.multiple_of(I*B,B),B); rp=pl.ds(p*B,B)
            x=x-dotg(hi[rI,:K],hi[rp,:K],1,1)
            if passes==3:
                x=x-(dotg(hi[rI,:K],lo[rp,:K],1,1)+dotg(lo[rI,:K],hi[rp,:K],1,1))
            return x
        s[...]=upd(p,a_ref[off])
        invert_block(s[...],m,t)
        th,tl=split(t[...])
        def body(i,_):
            I=p+1+i
            x=upd(I,a_ref[off+1+i])
            xh,xl=split(x)
            r=dotg(xh,th,1,0)
            if passes==3:
                r=r+(dotg(xh,tl,1,0)+dotg(xl,th,1,0))
            rh=r.astype(bf16)
            hi[pl.ds(pl.multiple_of(I*B,B),B),p*B:(p+1)*B]=rh
            if passes==3:
                lo[pl.ds(pl.multiple_of(I*B,B),B),p*B:(p+1)*B]=(r-rh.astype(f32)).astype(bf16)
            return 0
        if p<n-1: lax.fori_loop(0,n-1-p,body,0)
        def obody(i,_):
            rr=pl.ds(pl.multiple_of(i*B,B),B)
            x=o_ref[rr,p*B:(p+1)*B].astype(f32)
            if p>0: x=x-dotg(y_ref[rr,:K],hi[p*B:(p+1)*B,:K],1,1)
            xh,xl=split(x)
            r=dotg(xh,th,1,0)+dotg(xl,th,1,0)
            y_ref[rr,p*B:(p+1)*B]=r.astype(bf16)
            return 0
        lax.fori_loop(0,orow//B,obody,0)
        off+=n-p

def factor_solve(a,o,passes=3,interpret=False):
    nb=o.shape[1]
    V=pl.BlockSpec(memory_space=pltpu.VMEM)
    return pl.pallas_call(functools.partial(factor_kernel,passes),
        out_shape=jax.ShapeDtypeStruct(o.shape,bf16),
        in_specs=[V,V],out_specs=V,
        scratch_shapes=[pltpu.VMEM((nb,nb),bf16),pltpu.VMEM((nb,nb) if passes==3 else (8,128),bf16),
            pltpu.VMEM((128,128),f32),pltpu.VMEM((256,256),f32),pltpu.VMEM((256,256),f32),pltpu.VMEM((256,256),f32)],
        compiler_params=pltpu.CompilerParams(vmem_limit_bytes=56*2**20),name="factor_solve",interpret=interpret)(a,o)


BLOCK = 256


def lower_blocks(count):
    return [(i, p) for p in range(count) for i in range(p, count)]


def metric_kernel(scale, ids, mine, weights, coefs, out, high, low, whigh, wlow):
    corr = jnp.dot(weights[...], mine[...], preferred_element_type=f32)
    weighted = dot3(coefs[...], corr) * (1.0 / scale)
    high[...], low[...] = split(corr)
    whigh[...], wlow[...] = split(weighted)

    def one(b, _):
        rows = pl.ds(pl.multiple_of(ids[b, 0] * BLOCK, BLOCK), BLOCK)
        cols = pl.ds(pl.multiple_of(ids[b, 1] * BLOCK, BLOCK), BLOCK)
        total = dotg(mine[:, rows], mine[:, cols], 0, 0)
        paw = dotg(whigh[:, rows], high[:, cols], 0, 0)
        paw = paw + dotg(whigh[:, rows], low[:, cols], 0, 0)
        paw = paw + dotg(wlow[:, rows], high[:, cols], 0, 0)
        out[b] = (total + paw) * scale
        return 0

    lax.fori_loop(0, out.shape[0], one, 0)


def metric_blocks(ids, mine, weights, coefs, scale):
    bands = mine.shape[1]
    terms = weights.shape[0]
    vmem = pl.BlockSpec(memory_space=pltpu.VMEM)
    return pl.pallas_call(
        functools.partial(metric_kernel, scale),
        out_shape=jax.ShapeDtypeStruct((ids.shape[0], BLOCK, BLOCK), f32),
        in_specs=[pl.BlockSpec(memory_space=pltpu.SMEM), vmem, vmem, vmem],
        out_specs=vmem,
        scratch_shapes=[pltpu.VMEM((terms, bands), bf16)] * 4,
        compiler_params=pltpu.CompilerParams(vmem_limit_bytes=56 * 2**20),
        name="metric_blocks",
    )(ids, mine, weights, coefs)


def atom_rows(projectors, sphere_start, proj_count, owner_slab, correlation_coef, first, height):
    slabs = lax.axis_size("grid")
    atoms, most, span = projectors.shape
    per_slab = atoms // slabs
    owned = owner_slab == lax.axis_index("grid")
    rank = jnp.cumsum(owned.astype(jnp.int32)) - 1
    pick = owned[None, :] & (rank[None, :] == jnp.arange(per_slab, dtype=jnp.int32)[:, None])

    def choose(values):
        shaped = pick.reshape(pick.shape + (1,) * (values.ndim - 1))
        return jnp.sum(jnp.where(shaped, values[None], jnp.zeros_like(values)[None]), axis=1, dtype=values.dtype)

    weights = choose(projectors)
    active = jnp.arange(most)[None, :] < choose(proj_count)[:, None]
    block = (choose(sphere_start) - first) // span
    spots = (block[:, None] == jnp.arange(height // span)[None, :])[:, None, :, None] & active[:, :, None, None]
    rows = jnp.where(spots, weights[:, :, None, :], jnp.zeros_like(weights)[:, :, None, :])
    coefs = choose(correlation_coef)
    same = jnp.eye(per_slab, dtype=bool)[:, None, :, None]
    square = jnp.where(same, coefs[:, :, None, :], 0.0)
    return rows.reshape(per_slab * most, height), square.reshape(per_slab * most, per_slab * most)


def shards(orbitals, projectors, sphere_start, proj_count, owner_slab, correlation_coef):
    total_rows = orbitals.shape[0] * lax.axis_size("grid")
    height = orbitals.shape[0] // lax.axis_size("band")
    first = lax.axis_index("band") * height
    weights, coefs = atom_rows(projectors, sphere_start, proj_count, owner_slab, correlation_coef, first, height)
    mine = lax.all_to_all(orbitals, "band", split_axis=0, concat_axis=1, tiled=True)
    ids = jnp.asarray(lower_blocks(mine.shape[1] // BLOCK), jnp.int32)
    metric = metric_blocks(ids, mine, weights, coefs, 1.0 / total_rows)
    metric = lax.psum(metric, ("band", "grid"))
    return factor_solve(metric, mine)


def solution(mesh):
    in_specs = (P("grid", "band"), P(), P(), P(), P(), P())
    out_specs = P(("grid", "band"), None)
    return jax.shard_map(shards, mesh=mesh, in_specs=in_specs, out_specs=out_specs, check_vma=False)
```

time: 1120 us -> 433 us (0.39)
  other arithmetic: 502 us -> 2.28 us
  Pallas kernels: 0 us -> 196 us
  matrix products: 194 us -> 0 us
  waiting for transfers between devices: 301 us -> 215 us
  local copies, waits for them, and re-layouts: 83.1 us -> 2.45 us
  between operations: 25.2 us -> 13.5 us
    another operation x72 -> x2, other arithmetic: 494 us -> 0.1 us  [the longest x59 317 us: inverse_factor(): lower = jnp.linalg.cholesky(matrix)]
    pallas_call x0 -> x2, Pallas kernels: none -> 196 us  [the longest x1 176 us: factor_solve(): pl.pallas_call(functools.partial(factor_kernel, passes), out_shape=jax.Sh...]
    dot_general x17 -> x0, matrix products: 154 us -> none  [the longest x3 37.1 us: inverse_factor(): jnp.dot(matrix[half:, :half], upper_inv.T, precision=lax.Precision.HIGHEST)]
    psum x1, waiting for transfers between devices: 279 us -> 192 us  [shards(): metric = lax.psum(metric, ('band', 'grid'))]
    another operation x69 -> x1, local copies, waits for them, and re-layouts: 43.5 us -> 0.1 us  [the longest x53 42.9 us: inverse_factor(): lax.linalg.triangular_solve(lower, identity, left_side=True, lower=True)]
    another operation x52 -> x0, matrix products: 39.9 us -> none  [the longest x28 21.7 us: inverse_factor(): lax.linalg.triangular_solve(lower, identity, left_side=True, lower=True)]
    gather x44 -> x0, local copies, waits for them, and re-layouts: 22.5 us -> none
  transfers between devices with their start and end apart: 2 -> 2, of which waited for: 2 -> 2; matrix products, arithmetic and copies ran while one was open for 0% -> 1% of each run, Pallas kernels for 0% -> 0%
where the time goes in v1:
time: 433 us
  waiting for transfers between devices  215 us (50%)
  Pallas kernels  196 us (45%)
  between operations  13.5 us (3%)
  starting transfers between devices  4.38 us (1%)
    psum x1, waiting for transfers between devices, shards(): metric = lax.psum(metric, ('band', 'grid'))  192 us
    pallas_call x1, Pallas kernels, factor_solve(): pl.pallas_call(functools.partial(factor_kernel, passes), out_shape=jax.Sh...  176 us
    all_to_all x1, waiting for transfers between devices, shards(): lax.all_to_all(orbitals, 'band', split_axis=0, concat_axis=1, tiled=True)  22.5 us
    pallas_call x1, Pallas kernels, metric_blocks(): pl.pallas_call(functools.partial(metric_kernel, scale), out_shape=jax.Sha...  19.7 us
  transfers between devices with their start and end apart: 2, of which 2 were waited for; matrix products, arithmetic and copies ran while one was open for 1% of the time, Pallas kernels for 0%

profile of v1, /device:TPU:0, one launch (start us, length us, event | category | flops | bytes accessed | tf_op | source)
XLA Modules:
  0.0 433.1 jit_solution(16183256260506417934)
XLA Ops:
  6.5 0.0 copy-start.2
  6.5 0.0 copy-start.1
  6.5 0.0 copy-start.3
  6.5 0.0 copy-start.4
  6.5 0.0 copy-start
  6.5 4.4 %all-to-all-start = ((bf16[4,512,512]{2,1,0:T(8,128)(2,1)}), bf16[4,512,512]{2,1,0:T(8,128)(2,1)S(1)}, u32[]{:S(2)}, u32[]{:S(2)}) async-start(bf16[4,512,512]{2,1,0:T(8,128)(2,1)} %bitcast.13), calls=%async_computation | async-start | bytes 4194304 | tf_op jit(solution)/shard_map/all_to_all | solution.py:197
  10.9 0.0 all-reduce.2.cloned.1.call-start
  10.9 0.0 copy-done.2
  11.0 0.1 copy.18
  11.1 0.1 reduce-window.8
  11.2 0.1 add_reduce_fusion
  11.3 0.0 copy-done.1
  11.3 0.1 select_reduce_fusion.1
  11.4 0.1 broadcast_select_fusion
  11.5 0.7 select_n.48.coefs
  12.3 0.0 copy-done.3
  12.3 0.0 copy-done.4
  12.3 0.1 select_reduce_fusion.3
  12.4 0.0 copy-done
  12.4 0.7 select_reduce_fusion
  13.2 0.1 iota_compare_fusion.2
  13.2 0.1 iota_compare_fusion.1
  13.3 0.1 broadcast_and_fusion
  13.4 0.7 select_bitcast_fusion.weights
  14.1 22.5 %all-to-all-done = bf16[4,512,512]{2,1,0:T(8,128)(2,1)S(1)} async-done(((bf16[4,512,512]{2,1,0:T(8,128)(2,1)}), bf16[4,512,512]{2,1,0:T(8,128)(2,1)S(1)}, u32[]{:S(2)}, u32[]{:S(2)}) %all-to-all-start) | async-done | bytes 2097184 | tf_op jit(solution)/shard_map/all_to_all | solution.py:197
  36.6 1.6 copy.19
  38.2 19.7 %metric_blocks.1 = f32[36,256,256]{2,1,0:T(8,128)} custom-call(s32[36,2]{1,0:T(8,128)} %constant.42.clone.ids, bf16[512,2048]{1,0:T(8,128)(2,1)} %bitcast.10, bf16[64,512]{1,0:T(8,128)(2,1)} %select_bitcast_fusion.weights, f32[64,64]{1,0:T(8,128)} %select_n.48.coefs), custom_call_target="tpu_custom_call" | custom-call | tf_op jit(solution)/shard_map/metric_blocks/pallas_call | solution.py:158
  57.9 0.0 all-reduce.2.cloned.1.call-update
  57.9 192.3 %all-reduce.2.cloned.1.call-done.a_ref = f32[36,256,256]{2,1,0:T(8,128)} async-done(((f32[36,256,256]{2,1,0:T(8,128)}), f32[36,256,256]{2,1,0:T(8,128)}) %all-reduce.2.cloned.1.call-update) | async-done | bytes 9437200 | tf_op jit(solution)/shard_map/psum | solution.py:200
  250.2 176.1 %factor_solve.1 = bf16[512,2048]{1,0:T(8,128)(2,1)} custom-call(f32[36,256,256]{2,1,0:T(8,128)} %all-reduce.2.cloned.1.call-done.a_ref, bf16[512,2048]{1,0:T(8,128)(2,1)} %bitcast.11), custom_call_target="tpu_custom_call" | custom-call | tf_op jit(solution)/shard_map/factor_solve/pallas_call | solution.py:120
  (4 shorter events, 0.0 us)
Async XLA Ops:
  6.5 4.4 %copy-start.2 = (s32[64]{0:T(128)S(1)}, s32[64]{0:T(128)}, u32[]{:S(2)}) copy-start(s32[64]{0:T(128)} %param.11) | copy-start | bytes 772
  6.5 4.7 %copy-start.1 = (f32[64,8,8]{0,2,1:T(8,128)S(1)}, f32[64,8,8]{0,2,1:T(8,128)}, u32[]{:S(2)}) copy-start(f32[64,8,8]{0,2,1:T(8,128)} %param.12) | copy-start | bytes 49156
  6.5 5.7 %copy-start.3 = (s32[64]{0:T(128)S(1)}, s32[64]{0:T(128)}, u32[]{:S(2)}) copy-start(s32[64]{0:T(128)} %param.9) | copy-start | bytes 772
  6.5 5.7 %copy-start.4 = (s32[64]{0:T(128)S(1)}, s32[64]{0:T(128)}, u32[]{:S(2)}) copy-start(s32[64]{0:T(128)} %param.10) | copy-start | bytes 772
  6.5 5.9 %copy-start = (bf16[64,8,128]{2,1,0:T(8,128)(2,1)S(1)}, bf16[64,8,128]{2,1,0:T(8,128)(2,1)}, u32[]{:S(2)}) copy-start(bf16[64,8,128]{2,1,0:T(8,128)(2,1)} %param.8) | copy-start | bytes 393220
  6.5 30.1 %all-to-all-start = ((bf16[4,512,512]{2,1,0:T(8,128)(2,1)}), bf16[4,512,512]{2,1,0:T(8,128)(2,1)S(1)}, u32[]{:S(2)}, u32[]{:S(2)}) async-start(bf16[4,512,512]{2,1,0:T(8,128)(2,1)} %bitcast.13), calls=%async_computation | async-start | bytes 4194304 | tf_op jit(solution)/shard_map/all_to_all | solution.py:197
  10.9 239.3 %all-reduce.2.cloned.1.call-start = ((), (), s32[]{:S(2)}) async-start(), calls=%async_computation.1 | async-start | bytes 18874368 | tf_op jit(solution)/shard_map/psum | solution.py:200
Sparse Core Ops, SparseCore 0:
  58.0 192.1 all-reduce.1

commit v2 on v0

v2 whole, which is shorter than its diff:
```python
import functools

import jax, jax.numpy as jnp
from jax import lax
from jax.experimental import pallas as pl
from jax.experimental.pallas import tpu as pltpu
from jax.sharding import PartitionSpec as P


f32,bf16=jnp.float32,jnp.bfloat16


def split(x):
    hi=x.astype(bf16)
    return hi,(x-hi.astype(f32)).astype(bf16)


def dotg(a,b,ca,cb):
    return lax.dot_general(a,b,(((ca,),(cb,)),((),())),preferred_element_type=f32)


def dot3(a,b,ca=1,cb=0):
    ah,al=split(a); bh,bl=split(b)
    return dotg(ah,bh,ca,cb)+(dotg(ah,bl,ca,cb)+dotg(al,bh,ca,cb))


def inverse_root(m, c, pv):
    n = m.shape[0]
    lane = lax.broadcasted_iota(jnp.int32, (8, n), 1)
    sub = lax.broadcasted_iota(jnp.int32, (8, n), 0)

    def step(o, piv):
        k0 = pl.multiple_of(o * 8, 8)
        block = m[pl.ds(k0, 8), :]
        for k in range(8):
            pv[k] = jnp.take_along_axis(block, jnp.full((8, n), k0 + k, jnp.int32), axis=1)
        rows = [jnp.broadcast_to(m[pl.ds(k0 + k, 1), :], (8, n)) for k in range(8)]
        s = [[None] * 8 for _ in range(8)]
        for k in range(8):
            for i in range(k + 1):
                s[i][k] = jnp.broadcast_to(pv[k, i : i + 1, :], (8, n))
        for k in range(8):
            c[k] = jnp.take_along_axis(m[...], jnp.full((n, n), k0 + k, jnp.int32), axis=1)
        mult = [[None] * 8 for _ in range(8)]
        inv = [None] * 8
        for k in range(8):
            inv[k] = 1.0 / s[k][k]
            piv = jnp.where(lane == k0 + k, s[k][k], piv)
            for j in range(k + 1, 8):
                mult[k][j] = s[k][j] * inv[k]
            for i in range(k + 1, 8):
                for j in range(i, 8):
                    s[i][j] = s[i][j] - mult[k][i] * s[k][j]
            for j in range(k + 1, 8):
                rows[j] = rows[j] - mult[k][j] * rows[k]
        after = lane > k0 + 7
        r = [jnp.where(after, rows[k] * inv[k], jnp.where(lane == k0 + k, -1.0, 0.0)) for k in range(8)]
        for i in range(6, -1, -1):
            for k in range(7, i, -1):
                r[i] = r[i] - mult[i][k] * r[k]
        inside = (lane >= k0) & (lane < k0 + 8)
        for b in range(0, n, 8):
            new = jnp.where(inside, 0.0, m[b : b + 8, :])
            for k in range(8):
                new = new - c[k, b : b + 8, :] * r[k]
            m[b : b + 8, :] = new
        own = -r[0]
        for k in range(1, 8):
            own = jnp.where(sub == k, -r[k], own)
        m[pl.ds(k0, 8), :] = own
        return piv

    return lax.fori_loop(0, n // 8, step, jnp.ones((8, n), f32))


def invert_block(s,m,t,c,pv):
    h=s.shape[0]//2
    m[...]=s[:h,:h]
    piv=inverse_root(m,c,pv)
    t1=m[...]*lax.rsqrt(piv[0:1,:])
    low=dot3(s[h:,:h],t1)
    m[...]=s[h:,h:]-dot3(low,low,1,1)
    piv=inverse_root(m,c,pv)
    t2=m[...]*lax.rsqrt(piv[0:1,:])
    t[:h,:h]=t1
    t[h:,h:]=t2
    t[h:,:h]=jnp.zeros((h,h),f32)
    t[:h,h:]=-dot3(t1,dot3(low,t2,0,0))


BLOCK = 256
GROUPS = (0, 1, 3)


def panel_groups(count):
    ends = GROUPS[1:] + (count,)
    return [range(a, min(b, count)) for a, b in zip(GROUPS, ends) if a < count]


def place_units(panels, count, devices):
    blocks = [(i, p) for p in panels for i in range(p, count)]
    size = -(-len(blocks) // devices)
    blocks += [blocks[-1]] * (size * devices - len(blocks))
    held = [blocks[d * size : (d + 1) * size] for d in range(devices)]
    where = {}
    for k, block in enumerate(blocks):
        where.setdefault(block, (k // size, k % size))
    return size, held, where


def fetch(band, pieces, buf, sem):
    copies = []
    for r, parts in enumerate(pieces):
        first = 0
        for part in parts:
            dst = buf.at[band ^ r, pl.ds(first, part.shape[0])]
            copies.append(pltpu.make_async_copy(part, dst, sem.at[len(copies)]))
            first += part.shape[0]
    for copy in copies:
        copy.start()
    for copy in copies:
        copy.wait()


def metric_kernel(scale, counts, with_rows, where, ids, weights, coefs, *refs):
    parts = sum(counts)
    flat, refs = refs[:parts], refs[parts:]
    pieces, at = [], 0
    for c in counts:
        pieces.append(flat[at : at + c])
        at += c
    outs, (mine, high, low, whigh, wlow, sem) = refs[:-6], refs[-6:]
    band = where[0]
    fetch(band, pieces, mine, sem)
    width = mine.shape[2]
    for j in range(mine.shape[0]):
        cols = slice(j * width, (j + 1) * width)
        corr = jnp.dot(weights[...], mine[j], preferred_element_type=f32)
        weighted = dot3(coefs[...], corr) * (1.0 / scale)
        high[:, cols], low[:, cols] = split(corr)
        whigh[:, cols], wlow[:, cols] = split(weighted)
    if with_rows:
        rows = outs[-1]
        outs = outs[:-1]
        height = rows.shape[0]
        for j in range(mine.shape[0]):
            own = pl.ds(pl.multiple_of(band * height, height), height)
            rows[:, j * width : (j + 1) * width] = mine[j, own, :]
    first = 0
    for out in outs:
        slabs, size, part, _ = out.shape

        def one(n, _, first=first, out=out, slabs=slabs, part=part):
            i, p = ids[first + n, 0], ids[first + n, 1]
            rows = pl.ds(pl.multiple_of(i * BLOCK, BLOCK), BLOCK)
            cols = pl.ds(pl.multiple_of(p * BLOCK, BLOCK), BLOCK)
            per = width // BLOCK
            left = mine[i // per, :, pl.ds(pl.multiple_of((i % per) * BLOCK, BLOCK), BLOCK)]
            right = mine[p // per, :, pl.ds(pl.multiple_of((p % per) * BLOCK, BLOCK), BLOCK)]
            total = dotg(left, right, 0, 0)
            paw = dotg(whigh[:, rows], high[:, cols], 0, 0)
            paw = paw + dotg(whigh[:, rows], low[:, cols], 0, 0)
            paw = paw + dotg(wlow[:, rows], high[:, cols], 0, 0)
            out[:, n] = ((total + paw) * scale).reshape(slabs, part, BLOCK)
            return 0

        lax.fori_loop(0, size, one, 0)
        first += size


def metric_units(band, ids, sizes, slabs, weights, coefs, pieces, scale, height):
    bands = sum(p[0].shape[1] for p in pieces)
    grid_rows = sum(part.shape[0] for part in pieces[0])
    terms = weights.shape[0]
    vmem = pl.BlockSpec(memory_space=pltpu.VMEM)
    smem = pl.BlockSpec(memory_space=pltpu.SMEM)
    hbm = pl.BlockSpec(memory_space=pl.ANY)
    flat = [part for p in pieces for part in p]
    outs = [jax.ShapeDtypeStruct((slabs, n, BLOCK // slabs, BLOCK), f32) for n in sizes]
    if height:
        outs.append(jax.ShapeDtypeStruct((height, bands), bf16))
    return pl.pallas_call(
        functools.partial(metric_kernel, scale, [len(p) for p in pieces], bool(height)),
        out_shape=outs,
        in_specs=[smem, smem, vmem, vmem] + [hbm] * len(flat),
        out_specs=[vmem] * len(outs),
        scratch_shapes=[pltpu.VMEM((len(pieces), grid_rows, bands // len(pieces)), bf16)]
        + [pltpu.VMEM((terms, bands), bf16)] * 4
        + [pltpu.SemaphoreType.DMA((len(flat),))],
        compiler_params=pltpu.CompilerParams(vmem_limit_bytes=56 * 2**20),
        cost_estimate=pl.CostEstimate(flops=sum(sizes) * 2 * grid_rows * BLOCK * BLOCK, bytes_accessed=2**23, transcendentals=0),
        name="metric_units",
    )(band, ids, weights, coefs, *flat)


def sum_kernel(got, out):
    total = got[0]
    for g in range(1, got.shape[0]):
        total = total + got[g]
    for g in range(out.shape[0]):
        out[g] = total


def sum_units(got):
    return pl.pallas_call(
        sum_kernel,
        out_shape=jax.ShapeDtypeStruct(got.shape, f32),
        in_specs=[pl.BlockSpec(memory_space=pltpu.VMEM)],
        out_specs=pl.BlockSpec(memory_space=pltpu.VMEM),
        name="sum_units",
    )(got)


def group_kernel(panels, npieces, earlier, last, where, spots, *refs):
    pieces = [[r] for r in refs[:npieces]]
    o_ref = refs[npieces]
    refs = refs[npieces + 1 :]
    olds = [refs[3 * q : 3 * q + 3] for q in range(earlier)]
    refs = refs[3 * earlier :]
    nout = 1 if last else 3
    outs, (buf, m, t, s, c, pv, sem) = refs[:nout], refs[nout : nout + 7]
    if last:
        y_out, (hi, lo) = outs[0], refs[nout + 7 :]
        base = panels[0] * BLOCK
        for q, (oh, ol, oy) in enumerate(olds):
            begin = sum(olds[k][2].shape[1] for k in range(q))
            y_out[:, begin : begin + oy.shape[1]] = oy[...]
    else:
        hi, lo, y_out = outs
        base = 0
    fetch(where[0], pieces, buf, sem)
    count = o_ref.shape[1] // BLOCK
    height = o_ref.shape[0]
    first = 0

    def block(k):
        return buf[spots[k, 0], :, spots[k, 1]].reshape(BLOCK, BLOCK)

    for step, p in enumerate(panels):
        K = step * BLOCK
        mine = slice(K, K + BLOCK)
        cp = slice(p * BLOCK, (p + 1) * BLOCK)
        stores = [(oh, ol, oy, oy.shape[1], 0) for oh, ol, oy in olds] + ([(hi, lo, y_out, K, base)] if K else [])

        def reduce_block(i, x):
            ri = pl.ds(pl.multiple_of(i * BLOCK, BLOCK), BLOCK)
            for h, l, _, k, _b in stores:
                x = x - dotg(h[ri, :k], h[cp, :k], 1, 1)
                x = x - (dotg(h[ri, :k], l[cp, :k], 1, 1) + dotg(l[ri, :k], h[cp, :k], 1, 1))
            return x

        s[...] = reduce_block(p, block(first))
        invert_block(s[...], m, t, c, pv)
        th, tl = split(t[...])

        def rows_below(n, _):
            i = p + 1 + n
            xh, xl = split(reduce_block(i, block(first + 1 + n)))
            r = dotg(xh, th, 1, 0) + (dotg(xh, tl, 1, 0) + dotg(xl, th, 1, 0))
            ri = pl.ds(pl.multiple_of(i * BLOCK, BLOCK), BLOCK)
            hi[ri, mine], lo[ri, mine] = split(r)
            return 0

        lax.fori_loop(0, count - 1 - p, rows_below, 0)

        def rows_orbital(n, _):
            ri = pl.ds(pl.multiple_of(n * BLOCK, BLOCK), BLOCK)
            x = o_ref[ri, cp].astype(f32)
            for h, _l, y, k, b in stores:
                x = x - dotg(y[ri, b : b + k], h[cp, :k], 1, 1)
            xh, xl = split(x)
            r = dotg(xh, th, 1, 0) + (dotg(xh, tl, 1, 0) + dotg(xl, th, 1, 0))
            y_out[ri, base + K : base + K + BLOCK] = r.astype(bf16)
            return 0

        lax.fori_loop(0, height // BLOCK, rows_orbital, 0)
        first += count - p


def solve_group(panels, band, spots, pieces, rows, olds):
    height, bands = rows.shape
    width = len(panels) * BLOCK
    last = panels[-1] + 1 == bands // BLOCK
    flat = [x for old in olds for x in old]
    vmem = pl.BlockSpec(memory_space=pltpu.VMEM)
    smem = pl.BlockSpec(memory_space=pltpu.SMEM)
    if last:
        outs = [jax.ShapeDtypeStruct((height, bands), bf16)]
        more = [pltpu.VMEM((bands, width), bf16)] * 2
    else:
        outs = [jax.ShapeDtypeStruct((bands, width), bf16)] * 2 + [jax.ShapeDtypeStruct((height, width), bf16)]
        more = []
    flops = len(panels) * 10 * 10**9
    return pl.pallas_call(
        functools.partial(group_kernel, list(panels), len(pieces), len(olds), last),
        out_shape=outs,
        in_specs=[smem, smem] + [pl.BlockSpec(memory_space=pl.ANY)] * len(pieces) + [vmem] * (1 + len(flat)),
        out_specs=[vmem] * len(outs),
        scratch_shapes=[
            pltpu.VMEM((len(pieces),) + pieces[0].shape, f32),
            pltpu.VMEM((BLOCK // 2, BLOCK // 2), f32),
            pltpu.VMEM((BLOCK, BLOCK), f32),
            pltpu.VMEM((BLOCK, BLOCK), f32),
            pltpu.VMEM((8, BLOCK // 2, BLOCK // 2), f32),
            pltpu.VMEM((8, 8, BLOCK // 2), f32),
            pltpu.SemaphoreType.DMA((len(pieces),)),
        ]
        + more,
        compiler_params=pltpu.CompilerParams(vmem_limit_bytes=56 * 2**20),
        cost_estimate=pl.CostEstimate(flops=flops, bytes_accessed=2**23, transcendentals=0),
        name="solve_group",
    )(band, spots, *pieces, rows, *flat)


def gather_bands(parts, size):
    held = {0: list(parts)}
    bit = size // 2
    while bit:
        swap = [(d, d ^ bit) for d in range(size)]
        for r in list(held):
            held[r | bit] = [lax.ppermute(x, "band", swap) for x in held[r]]
        bit //= 2
    return [held[r] for r in range(size)]


def atom_rows(projectors, sphere_start, proj_count, owner_slab, correlation_coef, height):
    slabs = lax.axis_size("grid")
    atoms, most, span = projectors.shape
    per_slab = atoms // slabs
    owned = owner_slab == lax.axis_index("grid")
    rank = jnp.cumsum(owned.astype(jnp.int32)) - 1
    pick = owned[None, :] & (rank[None, :] == jnp.arange(per_slab, dtype=jnp.int32)[:, None])

    def choose(values):
        shaped = pick.reshape(pick.shape + (1,) * (values.ndim - 1))
        return jnp.sum(jnp.where(shaped, values[None], jnp.zeros_like(values)[None]), axis=1, dtype=values.dtype)

    weights = choose(projectors)
    active = jnp.arange(most)[None, :] < choose(proj_count)[:, None]
    block = choose(sphere_start) // span
    spots = (block[:, None] == jnp.arange(height // span)[None, :])[:, None, :, None] & active[:, :, None, None]
    rows = jnp.where(spots, weights[:, :, None, :], jnp.zeros_like(weights)[:, :, None, :])
    coefs = choose(correlation_coef)
    same = jnp.eye(per_slab, dtype=bool)[:, None, :, None]
    square = jnp.where(same, coefs[:, :, None, :], 0.0)
    return rows.reshape(per_slab * most, height), square.reshape(per_slab * most, per_slab * most)


def shards(orbitals, projectors, sphere_start, proj_count, owner_slab, correlation_coef):
    slabs, devices = lax.axis_size("grid"), lax.axis_size("band")
    grid_rows, width = orbitals.shape
    scale = 1.0 / (grid_rows * slabs)
    height = grid_rows // devices
    count = width * devices // BLOCK
    band_index = lax.axis_index("band")
    band = band_index.reshape(1)
    half = grid_rows // 2
    pieces = gather_bands([orbitals[:half], orbitals[half:]], devices)
    pieces[0] = [orbitals]
    weights, coefs = atom_rows(projectors, sphere_start, proj_count, owner_slab, correlation_coef, grid_rows)

    groups = panel_groups(count)
    plans = [place_units(panels, count, devices) for panels in groups]
    tables = [jnp.asarray(held, jnp.int32)[band_index] for _, held, _ in plans]
    sizes = [size for size, _, _ in plans]
    lead, rows = metric_units(band, tables[0], sizes[:1], slabs, weights, coefs, pieces, scale, height)
    rest = metric_units(band, jnp.concatenate(tables[1:]), sizes[1:], slabs, weights, coefs, pieces, scale, 0)
    olds = []
    for panels, (_, _, where), units in zip(groups, plans, [lead] + list(rest)):
        got = lax.all_to_all(units, "grid", split_axis=0, concat_axis=0, tiled=True)
        part = sum_units(got)
        part = lax.all_to_all(part, "grid", split_axis=0, concat_axis=0, tiled=True)
        all_parts = [x[0] for x in gather_bands([part], devices)]
        runs = [list(panels)] if panels[-1] + 1 == count else [[p] for p in panels]
        for run in runs:
            order = [where[i, p] for p in run for i in range(p, count)]
            olds.append(solve_group(run, band, jnp.asarray(order, jnp.int32), all_parts, rows, olds))
    return olds[-1][0]


def solution(mesh):
    in_specs = (P("grid", "band"), P(), P(), P(), P(), P())
    out_specs = P(("grid", "band"), None)
    return jax.shard_map(shards, mesh=mesh, in_specs=in_specs, out_specs=out_specs, check_vma=False)
```

time: 1120 us -> 379 us (0.34)
  other arithmetic: 502 us -> 3.23 us
  matrix products: 194 us -> 0 us
  waiting for transfers between devices: 301 us -> 131 us
  Pallas kernels: 0 us -> 159 us
  local copies, waits for them, and re-layouts: 83.1 us -> 10.2 us
  blocking collectives: 0 us -> 52 us
  between operations: 25.2 us -> 0.47 us
  starting transfers between devices: 4.63 us -> 22.4 us
    another operation x72 -> x2, other arithmetic: 494 us -> 0.1 us  [the longest x59 317 us: inverse_factor(): lower = jnp.linalg.cholesky(matrix)]
    psum x1 -> x0, waiting for transfers between devices: 279 us -> none  [shards(): metric = lax.psum(gram + paw, ('band', 'grid'))]
    pallas_call x0 -> x9, Pallas kernels: none -> 159 us  [the longest x4 131 us: solve_group(): pl.pallas_call(functools.partial(group_kernel, list(panels), len(pieces),...]
    dot_general x17 -> x0, matrix products: 154 us -> none  [the longest x3 37.1 us: inverse_factor(): jnp.dot(matrix[half:, :half], upper_inv.T, precision=lax.Precision.HIGHEST)]
    ppermute x0 -> x15, waiting for transfers between devices: none -> 83.7 us  [gather_bands(): held[r | bit] = [lax.ppermute(x, 'band', swap) for x in held[r]]]
    all_to_all x0 -> x2, blocking collectives: none -> 52 us  [shards(): got = lax.all_to_all(units, 'grid', split_axis=0, concat_axis=0, tiled=True)]
    another operation x69 -> x1, local copies, waits for them, and re-layouts: 43.5 us -> 0.1 us  [the longest x53 42.9 us: inverse_factor(): lax.linalg.triangular_solve(lower, identity, left_side=True, lower=True)]
    another operation x52 -> x0, matrix products: 39.9 us -> none  [the longest x28 21.7 us: inverse_factor(): lax.linalg.triangular_solve(lower, identity, left_side=True, lower=True)]
  transfers between devices with their start and end apart: 2 -> 19, of which waited for: 2 -> 8; matrix products, arithmetic and copies ran while one was open for 0% -> 2% of each run, Pallas kernels for 0% -> 19%
where the time goes in v2:
time: 379 us; the launch traced here: 378 us
  Pallas kernels  159 us (42%)
  waiting for transfers between devices  131 us (35%)
  blocking collectives  52 us (14%)
  starting transfers between devices  22.4 us (6%)
  local copies, waits for them, and re-layouts  10.2 us (3%)
    pallas_call x4, Pallas kernels, solve_group(): pl.pallas_call(functools.partial(group_kernel, list(panels), len(pieces),...  131 us
    ppermute x15, waiting for transfers between devices, gather_bands(): held[r | bit] = [lax.ppermute(x, 'band', swap) for x in held[r]]  83.7 us
    all_to_all x2, blocking collectives, shards(): got = lax.all_to_all(units, 'grid', split_axis=0, concat_axis=0, tiled=True)  52 us
    all_to_all x3, waiting for transfers between devices, shards(): part = lax.all_to_all(part, 'grid', split_axis=0, concat_axis=0, tiled=True)  24.1 us
    all_to_all x1, waiting for transfers between devices, shards(): got = lax.all_to_all(units, 'grid', split_axis=0, concat_axis=0, tiled=True)  23.2 us
    pallas_call x2, Pallas kernels, metric_units(): pl.pallas_call(functools.partial(metric_kernel, scale, [len(p) for p in p...  21.9 us
    all_to_all x3, starting transfers between devices, shards(): part = lax.all_to_all(part, 'grid', split_axis=0, concat_axis=0, tiled=True)  10.9 us
    ppermute x15, starting transfers between devices, gather_bands(): held[r | bit] = [lax.ppermute(x, 'band', swap) for x in held[r]]  7.88 us
  transfers between devices with their start and end apart: 19, of which 8 were waited for; matrix products, arithmetic and copies ran while one was open for 2% of the time, Pallas kernels for 19%

profile of v2, /device:TPU:0, one launch (start us, length us, event | category | flops | bytes accessed | tf_op | source)
XLA Modules:
  0.0 378.4 jit_solution(6562825722909836317)
XLA Ops:
  0.0 3.0 fusion.1
  3.0 3.0 collective-permute-start.2
  6.0 0.1 collective-permute-start.3
  6.1 0.4 collective-permute-start.1
  6.5 0.1 copy.25
  6.6 0.1 reduce-window.8
  6.7 0.1 add_reduce_fusion
  6.9 0.1 select_reduce_fusion.1
  7.0 0.1 broadcast_select_fusion
  7.1 0.7 select_n.54.coefs
  7.9 1.2 dynamic-slice_bitcast_fusion.ids
  9.1 0.8 select_reduce_fusion.3
  9.9 0.1 iota_compare_fusion.2
  10.0 20.3 %collective-permute-done.2.refs_3_ = bf16[1024,512]{1,0:T(8,128)(2,1)S(1)} collective-permute-done((bf16[1024,512]{1,0:T(8,128)(2,1)}, bf16[1024,512]{1,0:T(8,128)(2,1)S(1)}, u32[]{:S(2)}, u32[]{:S(2)}) %collective-permute-start.2) | collective-permute-done | bytes 1048608 | tf_op jit(solution)/shard_map/ppermute | solution.py:321
  30.2 21.6 %collective-permute-done.3.refs_4_ = bf16[1024,512]{1,0:T(8,128)(2,1)S(1)} collective-permute-done((bf16[1024,512]{1,0:T(8,128)(2,1)}, bf16[1024,512]{1,0:T(8,128)(2,1)S(1)}, u32[]{:S(2)}, u32[]{:S(2)}) %collective-permute-start.3) | collective-permute-done | bytes 1048608 | tf_op jit(solution)/shard_map/ppermute | solution.py:321
  51.9 0.7 select_reduce_fusion
  52.6 0.1 iota_compare_fusion.1
  52.7 0.1 broadcast_and_fusion
  52.7 0.9 select_bitcast_fusion.weights
  53.7 0.0 collective-permute-done.refs_1_
  53.7 0.0 collective-permute-done.1.refs_2_
  53.7 0.0 copy-start.4
  53.7 0.8 collective-permute-done.5.refs_6_
  54.5 0.2 copy-done.2
  54.7 0.3 copy-done.4
  55.0 0.5 copy-done.5
  55.5 9.4 %metric_units.3 = (f32[8,2,32,256]{3,2,1,0:T(8,128)}, bf16[512,2048]{1,0:T(8,128)(2,1)}) custom-call(s32[1]{0:T(128)} %bitcast.where, s32[2,2]{1,0:T(2,128)} %dynamic-slice_bitcast_fusion.ids, bf16[64,2048]{1,0:T(8,128)(2,1)} %select_bitcast_fusion.weights, f32[64,64]{1,0:T(8,128)} %select_n.54.coefs, bf16[2048,512]{1,0:T(8,128)(2,1)} %refs_0_.3, ...), custom_call_target="tpu_custom_call" | custom-call | flops 536870912 | bytes 8388608 | tf_op jit(solution)/shard_map/metric_units/pallas_call | solution.py:182
  64.9 21.2 %all_to_all.30.got = f32[8,2,32,256]{3,2,1,0:T(8,128)} all-to-all(f32[8,2,32,256]{3,2,1,0:T(8,128)} %get-tuple-element.20), channel_id=1, replica_groups=mesh['band'=4,'grid'=8] {'grid'}, dimensions={0} | all-to-all | bytes 1048576 | tf_op jit(solution)/shard_map/all_to_all | solution.py:370
  86.0 1.9 sum_units.4
  87.9 3.6 all-to-all-start.3
  91.6 0.7 dynamic-slice_bitcast_fusion.1
  92.3 0.1 pad_add_fusion
  92.3 0.7 copy.26.ids
  93.0 12.5 %metric_units.2 = (f32[8,4,32,256]{3,2,1,0:T(8,128)}, f32[8,4,32,256]{3,2,1,0:T(8,128)}) custom-call(s32[1]{0:T(128)} %bitcast.where, s32[8,2]{1,0:T(8,128)} %copy.26.ids, bf16[64,2048]{1,0:T(8,128)(2,1)} %select_bitcast_fusion.weights, f32[64,64]{1,0:T(8,128)} %select_n.54.coefs, bf16[2048,512]{1,0:T(8,128)(2,1)} %refs_0_.3, bf16[1024,512]{1,0:T(8,128)(2,1)} %copy-done.2, ...), custom_call_target="tpu_custom_call" | custom-call | flops 2147483648 | bytes 8388608 | tf_op jit(solution)/shard_map/metric_units/pallas_call | solution.py:182
  105.5 0.6 all-to-all-done.3.refs_0_
  106.1 30.8 %all_to_all.31.got = f32[8,4,32,256]{3,2,1,0:T(8,128)} all-to-all(f32[8,4,32,256]{3,2,1,0:T(8,128)} %get-tuple-element.24), channel_id=1, replica_groups=mesh['band'=4,'grid'=8] {'grid'}, dimensions={0} | all-to-all | bytes 2097152 | tf_op jit(solution)/shard_map/all_to_all | solution.py:370
  137.0 3.6 all-to-all-start
  140.5 2.3 sum_units.5
  142.8 23.2 %all-to-all-done.got = f32[8,4,32,256]{3,2,1,0:T(8,128)S(1)} async-done(((f32[8,4,32,256]{3,2,1,0:T(8,128)}), f32[8,4,32,256]{3,2,1,0:T(8,128)S(1)}, u32[]{:S(2)}, u32[]{:S(2)}) %all-to-all-start) | async-done | bytes 1048608 | tf_op jit(solution)/shard_map/all_to_all | solution.py:370
  166.1 3.6 all-to-all-start.5
  169.6 2.3 sum_units.3
  171.9 23.5 %all-to-all-done.5.refs_0_ = f32[8,4,32,256]{3,2,1,0:T(8,128)S(1)} async-done(((f32[8,4,32,256]{3,2,1,0:T(8,128)}), f32[8,4,32,256]{3,2,1,0:T(8,128)S(1)}, u32[]{:S(2)}, u32[]{:S(2)}) %all-to-all-start.5) | async-done | bytes 1048608 | tf_op jit(solution)/shard_map/all_to_all | solution.py:372
  195.4 3.7 all-to-all-start.1
  199.2 1.6 collective-permute-start.13
  200.7 0.5 collective-permute-start.10
  201.3 0.0 collective-permute-start.9
  201.3 33.8 %collective-permute-done.10.refs_2_ = f32[8,2,32,256]{3,2,1,0:T(8,128)S(1)} collective-permute-done((f32[8,2,32,256]{3,2,1,0:T(8,128)S(1)}, f32[8,2,32,256]{3,2,1,0:T(8,128)S(1)}, u32[]{:S(2)}, u32[]{:S(2)}) %collective-permute-start.10) | collective-permute-done | bytes 524320 | tf_op jit(solution)/shard_map/ppermute | solution.py:321
  235.1 0.0 collective-permute-start.11
  235.1 0.0 all-to-all-done.1.refs_0_
  235.1 1.6 collective-permute-start.7
  236.7 0.2 collective-permute-start.12
  236.8 0.0 collective-permute-done.13.refs_2_
  236.8 0.4 collective-permute-start.14
  237.2 0.0 collective-permute-done.9.refs_1_
  237.2 16.1 %solve_group.4 = (bf16[2048,256]{1,0:T(8,128)(2,1)}, bf16[2048,256]{1,0:T(8,128)(2,1)}, bf16[512,256]{1,0:T(8,128)(2,1)}) custom-call(s32[1]{0:T(128)} %bitcast.where, s32[8,2]{1,0:T(8,128)} %constant.57.clone.spots, f32[8,2,32,256]{3,2,1,0:T(8,128)} %copy-done.8, f32[8,2,32,256]{3,2,1,0:T(8,128)} %collective-permute-done.9.refs_1_, ...), custom_call_target="tpu_custom_call" | custom-call | flops 10000000000 | bytes 8388608 | tf_op jit(solution)/shard_map/solve_group/pallas_call | solution.py:294
  253.3 0.2 collective-permute-start.6
  253.5 7.1 %collective-permute-done.7.refs_2_ = f32[8,4,32,256]{3,2,1,0:T(8,128)S(1)} collective-permute-done((f32[8,4,32,256]{3,2,1,0:T(8,128)S(1)}, f32[8,4,32,256]{3,2,1,0:T(8,128)S(1)}, u32[]{:S(2)}, u32[]{:S(2)}) %collective-permute-start.7) | collective-permute-done | bytes 1048608 | tf_op jit(solution)/shard_map/ppermute | solution.py:321
  260.7 1.0 copy-done.13
  261.7 0.4 copy-done.14
  262.1 19.9 %solve_group.5 = (bf16[2048,256]{1,0:T(8,128)(2,1)}, bf16[2048,256]{1,0:T(8,128)(2,1)}, bf16[512,256]{1,0:T(8,128)(2,1)}) custom-call(s32[1]{0:T(128)} %bitcast.where, s32[7,2]{1,0:T(8,128)} %constant.58.clone.spots, f32[8,4,32,256]{3,2,1,0:T(8,128)} %copy-done.7, f32[8,4,32,256]{3,2,1,0:T(8,128)} %copy-done.13, ...), custom_call_target="tpu_custom_call" | custom-call | flops 10000000000 | bytes 8388608 | tf_op jit(solution)/shard_map/solve_group/pallas_call | solution.py:294
  282.1 20.6 %solve_group.6 = (bf16[2048,256]{1,0:T(8,128)(2,1)}, bf16[2048,256]{1,0:T(8,128)(2,1)}, bf16[512,256]{1,0:T(8,128)(2,1)}) custom-call(s32[1]{0:T(128)} %bitcast.where, s32[6,2]{1,0:T(8,128)} %constant.59.clone.spots, f32[8,4,32,256]{3,2,1,0:T(8,128)} %copy-done.7, f32[8,4,32,256]{3,2,1,0:T(8,128)} %copy-done.13, ...), custom_call_target="tpu_custom_call" | custom-call | flops 10000000000 | bytes 8388608 | tf_op jit(solution)/shard_map/solve_group/pallas_call | solution.py:294
  302.7 1.0 copy-done.15
  303.7 0.4 copy-done.16
  304.1 74.1 %solve_group.7 = bf16[512,2048]{1,0:T(8,128)(2,1)} custom-call(s32[1]{0:T(128)} %bitcast.where, s32[15,2]{1,0:T(8,128)} %constant.60.clone.spots, f32[8,4,32,256]{3,2,1,0:T(8,128)} %copy-done.6, f32[8,4,32,256]{3,2,1,0:T(8,128)} %copy-done.15, f32[8,4,32,256]{3,2,1,0:T(8,128)} %copy-done.12, f32[8,4,32,256]{3,2,1,0:T(8,128)} %copy-done.16, ...), custom_call_target="tpu_custom_call" | custom-call | flops 49999998976 | bytes 8388608 | tf_op jit(solution)/shard_map/solve_group/pallas_call | solution.py:294
  (42 shorter events, 0.1 us)
Async XLA Ops:
  0.0 6.5 %copy-start.11 = (s32[64]{0:T(128)S(1)}, s32[64]{0:T(128)}, u32[]{:S(2)}) copy-start(s32[64]{0:T(128)} %param.17) | copy-start | bytes 772
  0.0 6.9 %copy-start.10 = (f32[64,8,8]{0,2,1:T(8,128)S(1)}, f32[64,8,8]{0,2,1:T(8,128)}, u32[]{:S(2)}) copy-start(f32[64,8,8]{0,2,1:T(8,128)} %param.18) | copy-start | bytes 49156
  0.0 51.9 %copy-start.9 = (bf16[64,8,128]{2,1,0:T(8,128)(2,1)S(1)}, bf16[64,8,128]{2,1,0:T(8,128)(2,1)}, u32[]{:S(2)}) copy-start(bf16[64,8,128]{2,1,0:T(8,128)(2,1)} %param.14) | copy-start | bytes 393220
  3.0 27.2 %collective-permute-start.2 = (bf16[1024,512]{1,0:T(8,128)(2,1)}, bf16[1024,512]{1,0:T(8,128)(2,1)S(1)}, u32[]{:S(2)}, u32[]{:S(2)}) collective-permute-start(bf16[1024,512]{1,0:T(8,128)(2,1)} %get-tuple-element.36), channel_id=1, source_target_pairs={{0,16},{8,24},{16,0},{24,8},{1,17},{9,25},{17,1},{25,9},{2,18},{10... | collective-permute-start | bytes 3145736 | tf_op jit(solution)/shard_map/ppermute | solution.py:321
  6.0 47.7 %collective-permute-start = (bf16[1024,512]{1,0:T(8,128)(2,1)}, bf16[1024,512]{1,0:T(8,128)(2,1)S(1)}, u32[]{:S(2)}, u32[]{:S(2)}) collective-permute-start(bf16[1024,512]{1,0:T(8,128)(2,1)} %get-tuple-element.36), channel_id=1, source_target_pairs={{0,8},{8,0},{16,24},{24,16},{1,9},{9,1},{17,25},{25,17},{2,10},{10... | collective-permute-start | bytes 3145736 | tf_op jit(solution)/shard_map/ppermute | solution.py:321
  6.0 45.8 %collective-permute-start.3 = (bf16[1024,512]{1,0:T(8,128)(2,1)}, bf16[1024,512]{1,0:T(8,128)(2,1)S(1)}, u32[]{:S(2)}, u32[]{:S(2)}) collective-permute-start(bf16[1024,512]{1,0:T(8,128)(2,1)} %get-tuple-element.35), channel_id=1, source_target_pairs={{0,16},{8,24},{16,0},{24,8},{1,17},{9,25},{17,1},{25,9},{2,18},{10... | collective-permute-start | bytes 3145736 | tf_op jit(solution)/shard_map/ppermute | solution.py:321
  6.1 47.6 %collective-permute-start.1 = (bf16[1024,512]{1,0:T(8,128)(2,1)}, bf16[1024,512]{1,0:T(8,128)(2,1)}, u32[]{:S(2)}, u32[]{:S(2)}) collective-permute-start(bf16[1024,512]{1,0:T(8,128)(2,1)} %get-tuple-element.35), channel_id=1, source_target_pairs={{0,8},{8,0},{16,24},{24,16},{1,9},{9,1},{17,25},{25,17},{2,10},{10... | collective-permute-start | bytes 3145736 | tf_op jit(solution)/shard_map/ppermute | solution.py:321
  30.2 24.3 %copy-start.1 = (bf16[1024,512]{1,0:T(8,128)(2,1)}, bf16[1024,512]{1,0:T(8,128)(2,1)S(1)}, u32[]{:S(2)}) copy-start(bf16[1024,512]{1,0:T(8,128)(2,1)S(1)} %collective-permute-done.2.refs_3_) | copy-start | bytes 3145732
  30.2 23.5 %collective-permute-start.4 = (bf16[1024,512]{1,0:T(8,128)(2,1)S(1)}, bf16[1024,512]{1,0:T(8,128)(2,1)S(1)}, u32[]{:S(2)}, u32[]{:S(2)}) collective-permute-start(bf16[1024,512]{1,0:T(8,128)(2,1)S(1)} %collective-permute-done.2.refs_3_), channel_id=1, source_target_pairs={{0,8},{8,0},{16,24},{24,16},{1,9},{9,1},{17,25},{25,17},{2,10},{10... | collective-permute-start | bytes 3145736 | tf_op jit(solution)/shard_map/ppermute | solution.py:321
  51.9 2.7 copy-start.3
  51.9 2.7 collective-permute-start.5
  53.7 1.0 copy-start.2
  53.7 1.3 copy-start.4
  54.5 1.0 copy-start.5
  87.9 18.2 %all-to-all-start.3 = ((f32[8,2,32,256]{3,2,1,0:T(8,128)}), f32[8,2,32,256]{3,2,1,0:T(8,128)S(1)}, u32[]{:S(2)}, u32[]{:S(2)}) async-start(f32[8,2,32,256]{3,2,1,0:T(8,128)} %sum_units.4), calls=%async_computation.3 | async-start | bytes 1048576 | tf_op jit(solution)/shard_map/all_to_all | solution.py:372
  106.1 95.1 %copy-start.8 = (f32[8,2,32,256]{3,2,1,0:T(8,128)}, f32[8,2,32,256]{3,2,1,0:T(8,128)S(1)}, u32[]{:S(2)}) copy-start(f32[8,2,32,256]{3,2,1,0:T(8,128)S(1)} %all-to-all-done.3.refs_0_) | copy-start | bytes 1572868
  137.0 29.1 %all-to-all-start = ((f32[8,4,32,256]{3,2,1,0:T(8,128)}), f32[8,4,32,256]{3,2,1,0:T(8,128)S(1)}, u32[]{:S(2)}, u32[]{:S(2)}) async-start(f32[8,4,32,256]{3,2,1,0:T(8,128)} %get-tuple-element.18), calls=%async_computation | async-start | bytes 2097152 | tf_op jit(solution)/shard_map/all_to_all | solution.py:370
  166.0 3.6 copy-start
  166.1 29.4 %all-to-all-start.5 = ((f32[8,4,32,256]{3,2,1,0:T(8,128)}), f32[8,4,32,256]{3,2,1,0:T(8,128)S(1)}, u32[]{:S(2)}, u32[]{:S(2)}) async-start(f32[8,4,32,256]{3,2,1,0:T(8,128)} %sum_units.5), calls=%async_computation.5 | async-start | bytes 2097152 | tf_op jit(solution)/shard_map/all_to_all | solution.py:372
  195.4 57.9 %copy-start.7 = (f32[8,4,32,256]{3,2,1,0:T(8,128)}, f32[8,4,32,256]{3,2,1,0:T(8,128)S(1)}, u32[]{:S(2)}) copy-start(f32[8,4,32,256]{3,2,1,0:T(8,128)S(1)} %all-to-all-done.5.refs_0_) | copy-start | bytes 3145732
  195.4 39.7 %all-to-all-start.1 = ((f32[8,4,32,256]{3,2,1,0:T(8,128)}), f32[8,4,32,256]{3,2,1,0:T(8,128)S(1)}, u32[]{:S(2)}, u32[]{:S(2)}) async-start(f32[8,4,32,256]{3,2,1,0:T(8,128)} %sum_units.3), calls=%async_computation.1 | async-start | bytes 2097152 | tf_op jit(solution)/shard_map/all_to_all | solution.py:372
  199.2 37.7 %collective-permute-start.13 = (f32[8,4,32,256]{3,2,1,0:T(8,128)S(1)}, f32[8,4,32,256]{3,2,1,0:T(8,128)}, u32[]{:S(2)}, u32[]{:S(2)}) collective-permute-start(f32[8,4,32,256]{3,2,1,0:T(8,128)S(1)} %all-to-all-done.5.refs_0_), channel_id=1, source_target_pairs={{0,16},{8,24},{16,0},{24,8},{1,17},{9,25},{17,1},{25,9},{2,18},{10... | collective-permute-start | bytes 3145736 | tf_op jit(solution)/shard_map/ppermute | solution.py:321
  200.7 34.3 %collective-permute-start.10 = (f32[8,2,32,256]{3,2,1,0:T(8,128)S(1)}, f32[8,2,32,256]{3,2,1,0:T(8,128)S(1)}, u32[]{:S(2)}, u32[]{:S(2)}) collective-permute-start(f32[8,2,32,256]{3,2,1,0:T(8,128)S(1)} %all-to-all-done.3.refs_0_), channel_id=1, source_target_pairs={{0,16},{8,24},{16,0},{24,8},{1,17},{9,25},{17,1},{25,9},{2,18},{10... | collective-permute-start | bytes 1572872 | tf_op jit(solution)/shard_map/ppermute | solution.py:321
  201.3 35.9 %collective-permute-start.9 = (f32[8,2,32,256]{3,2,1,0:T(8,128)S(1)}, f32[8,2,32,256]{3,2,1,0:T(8,128)}, u32[]{:S(2)}, u32[]{:S(2)}) collective-permute-start(f32[8,2,32,256]{3,2,1,0:T(8,128)S(1)} %all-to-all-done.3.refs_0_), channel_id=1, source_target_pairs={{0,8},{8,0},{16,24},{24,16},{1,9},{9,1},{17,25},{25,17},{2,10},{10... | collective-permute-start | bytes 1572872 | tf_op jit(solution)/shard_map/ppermute | solution.py:321
  235.1 2.1 copy-start.17
  235.1 2.1 collective-permute-start.11
  235.1 18.2 %copy-start.6 = (f32[8,4,32,256]{3,2,1,0:T(8,128)}, f32[8,4,32,256]{3,2,1,0:T(8,128)S(1)}, u32[]{:S(2)}) copy-start(f32[8,4,32,256]{3,2,1,0:T(8,128)S(1)} %all-to-all-done.1.refs_0_) | copy-start | bytes 3145732
  235.1 25.6 %collective-permute-start.7 = (f32[8,4,32,256]{3,2,1,0:T(8,128)S(1)}, f32[8,4,32,256]{3,2,1,0:T(8,128)S(1)}, u32[]{:S(2)}, u32[]{:S(2)}) collective-permute-start(f32[8,4,32,256]{3,2,1,0:T(8,128)S(1)} %all-to-all-done.1.refs_0_), channel_id=1, source_target_pairs={{0,16},{8,24},{16,0},{24,8},{1,17},{9,25},{17,1},{25,9},{2,18},{10... | collective-permute-start | bytes 3145736 | tf_op jit(solution)/shard_map/ppermute | solution.py:321
  236.7 24.0 %collective-permute-start.12 = (f32[8,4,32,256]{3,2,1,0:T(8,128)S(1)}, f32[8,4,32,256]{3,2,1,0:T(8,128)S(1)}, u32[]{:S(2)}, u32[]{:S(2)}) collective-permute-start(f32[8,4,32,256]{3,2,1,0:T(8,128)S(1)} %all-to-all-done.5.refs_0_), channel_id=1, source_target_pairs={{0,8},{8,0},{16,24},{24,16},{1,9},{9,1},{17,25},{25,17},{2,10},{10... | collective-permute-start | bytes 3145736 | tf_op jit(solution)/shard_map/ppermute | solution.py:321
  236.8 23.9 %collective-permute-start.14 = (f32[8,4,32,256]{3,2,1,0:T(8,128)}, f32[8,4,32,256]{3,2,1,0:T(8,128)S(1)}, u32[]{:S(2)}, u32[]{:S(2)}) collective-permute-start(f32[8,4,32,256]{3,2,1,0:T(8,128)} %collective-permute-done.13.refs_2_), channel_id=1, source_target_pairs={{0,8},{8,0},{16,24},{24,16},{1,9},{9,1},{17,25},{25,17},{2,10},{10... | collective-permute-start | bytes 3145736 | tf_op jit(solution)/shard_map/ppermute | solution.py:321
  253.3 49.4 %collective-permute-start.6 = (f32[8,4,32,256]{3,2,1,0:T(8,128)S(1)}, f32[8,4,32,256]{3,2,1,0:T(8,128)S(1)}, u32[]{:S(2)}, u32[]{:S(2)}) collective-permute-start(f32[8,4,32,256]{3,2,1,0:T(8,128)S(1)} %all-to-all-done.1.refs_0_), channel_id=1, source_target_pairs={{0,8},{8,0},{16,24},{24,16},{1,9},{9,1},{17,25},{25,17},{2,10},{10... | collective-permute-start | bytes 3145736 | tf_op jit(solution)/shard_map/ppermute | solution.py:321
  260.7 21.4 %copy-start.12 = (f32[8,4,32,256]{3,2,1,0:T(8,128)}, f32[8,4,32,256]{3,2,1,0:T(8,128)S(1)}, u32[]{:S(2)}) copy-start(f32[8,4,32,256]{3,2,1,0:T(8,128)S(1)} %collective-permute-done.7.refs_2_) | copy-start | bytes 3145732
  260.7 42.0 %collective-permute-start.8 = (f32[8,4,32,256]{3,2,1,0:T(8,128)S(1)}, f32[8,4,32,256]{3,2,1,0:T(8,128)S(1)}, u32[]{:S(2)}, u32[]{:S(2)}) collective-permute-start(f32[8,4,32,256]{3,2,1,0:T(8,128)S(1)} %collective-permute-done.7.refs_2_), channel_id=1, source_target_pairs={{0,8},{8,0},{16,24},{24,16},{1,9},{9,1},{17,25},{25,17},{2,10},{10... | collective-permute-start | bytes 3145736 | tf_op jit(solution)/shard_map/ppermute | solution.py:321
  260.7 1.1 copy-start.13
  260.7 1.4 copy-start.14
  302.7 1.0 copy-start.15
  302.7 1.4 copy-start.16

commit v3 on v2

--- a/solution.py
+++ b/solution.py
@@ -187,10 +187,52 @@
         scratch_shapes=[pltpu.VMEM((len(pieces), grid_rows, bands // len(pieces)), bf16)]
         + [pltpu.VMEM((terms, bands), bf16)] * 4
         + [pltpu.SemaphoreType.DMA((len(flat),))],
-        compiler_params=pltpu.CompilerParams(vmem_limit_bytes=56 * 2**20),
+        compiler_params=pltpu.CompilerParams(vmem_limit_bytes=28 * 2**20),
         cost_estimate=pl.CostEstimate(flops=sum(sizes) * 2 * grid_rows * BLOCK * BLOCK, bytes_accessed=2**23, transcendentals=0),
         name="metric_units",
     )(band, ids, weights, coefs, *flat)
+
+
+def lead_kernel(scale, own, lead, weights, coefs, out, high, low, whigh, wlow):
+    slabs, size, part, _ = out.shape
+    corr = jnp.dot(weights[...], own[...], preferred_element_type=f32)
+    whigh[...], wlow[...] = split(dot3(coefs[...], corr) * (1.0 / scale))
+    high[...], low[...] = split(jnp.dot(weights[...], lead[...], preferred_element_type=f32))
+    for n in range(size):
+        rows = slice(n * BLOCK, (n + 1) * BLOCK)
+        total = dotg(own[:, rows], lead[...], 0, 0)
+        paw = dotg(whigh[:, rows], high[...], 0, 0)
+        paw = paw + dotg(whigh[:, rows], low[...], 0, 0)
+        paw = paw + dotg(wlow[:, rows], high[...], 0, 0)
+        out[:, n] = ((total + paw) * scale).reshape(slabs, part, BLOCK)
+
+
+def lead_units(slabs, weights, coefs, own, lead, scale):
+    rows, width = own.shape
+    terms = weights.shape[0]
+    size = width // BLOCK
+    vmem = pl.BlockSpec(memory_space=pltpu.VMEM)
+    return pl.pallas_call(
+        functools.partial(lead_kernel, scale),
+        out_shape=jax.ShapeDtypeStruct((slabs, size, BLOCK // slabs, BLOCK), f32),
+        in_specs=[vmem] * 4,
+        out_specs=vmem,
+        scratch_shapes=[pltpu.VMEM((terms, BLOCK), bf16)] * 2 + [pltpu.VMEM((terms, width), bf16)] * 2,
+        compiler_params=pltpu.CompilerParams(vmem_limit_bytes=40 * 2**20),
+        cost_estimate=pl.CostEstimate(flops=2 * rows * width * BLOCK, bytes_accessed=2**22, transcendentals=0),
+        name="lead_units",
+    )(own, lead, weights, coefs)
+
+
+def spread_lead(value, index, size):
+    held = jnp.where(index == 0, value, jnp.zeros_like(value))
+    bit = size // 2
+    while bit:
+        pairs = [(d, d | bit) for d in range(0, size, 2 * bit)]
+        got = lax.ppermute(held, "band", pairs)
+        held = jnp.where(index & bit == 0, held, got)
+        bit //= 2
+    return held
 
 
 def sum_kernel(got, out):
@@ -306,7 +348,7 @@
             pltpu.SemaphoreType.DMA((len(pieces),)),
         ]
         + more,
-        compiler_params=pltpu.CompilerParams(vmem_limit_bytes=56 * 2**20),
+        compiler_params=pltpu.CompilerParams(vmem_limit_bytes=36 * 2**20),
         cost_estimate=pl.CostEstimate(flops=flops, bytes_accessed=2**23, transcendentals=0),
         name="solve_group",
     )(band, spots, *pieces, rows, *flat)
@@ -318,7 +360,10 @@
     while bit:
         swap = [(d, d ^ bit) for d in range(size)]
         for r in list(held):
-            held[r | bit] = [lax.ppermute(x, "band", swap) for x in held[r]]
+            got = []
+            for x in held[r]:
+                got.append(lax.ppermute(x, "band", swap))
+            held[r | bit] = got
         bit //= 2
     return [held[r] for r in range(size)]
 
@@ -355,6 +400,7 @@
     band_index = lax.axis_index("band")
     band = band_index.reshape(1)
     half = grid_rows // 2
+    lead = spread_lead(orbitals[:, :BLOCK], band_index, devices)
     pieces = gather_bands([orbitals[:half], orbitals[half:]], devices)
     pieces[0] = [orbitals]
     weights, coefs = atom_rows(projectors, sphere_start, proj_count, owner_slab, correlation_coef, grid_rows)
@@ -362,11 +408,14 @@
     groups = panel_groups(count)
     plans = [place_units(panels, count, devices) for panels in groups]
     tables = [jnp.asarray(held, jnp.int32)[band_index] for _, held, _ in plans]
+    assert plans[0][0] == width // BLOCK
     sizes = [size for size, _, _ in plans]
-    lead, rows = metric_units(band, tables[0], sizes[:1], slabs, weights, coefs, pieces, scale, height)
-    rest = metric_units(band, jnp.concatenate(tables[1:]), sizes[1:], slabs, weights, coefs, pieces, scale, 0)
+    first = lead_units(slabs, weights, coefs, orbitals, lead, scale)
+    second, rows = metric_units(band, tables[1], sizes[1:2], slabs, weights, coefs, pieces, scale, height)
+    ids = jnp.concatenate(tables[2:])
+    rest = metric_units(band, ids, sizes[2:], slabs, weights, coefs, pieces, scale, 0)
     olds = []
-    for panels, (_, _, where), units in zip(groups, plans, [lead] + list(rest)):
+    for panels, (_, _, where), units in zip(groups, plans, [first, second] + list(rest)):
         got = lax.all_to_all(units, "grid", split_axis=0, concat_axis=0, tiled=True)
         part = sum_units(got)
         part = lax.all_to_all(part, "grid", split_axis=0, concat_axis=0, tiled=True)

time: 379 us -> 347 us (0.916)
  blocking collectives: 52 us -> 0 us
  starting transfers between devices: 22.4 us -> 42.5 us
  Pallas kernels: 159 us -> 140 us
  waiting for transfers between devices: 131 us -> 147 us
    all_to_all x2 -> x0, blocking collectives: 52 us -> none  [shards(): got = lax.all_to_all(units, 'grid', split_axis=0, concat_axis=0, tiled=True)]
    all_to_all x1 -> x3, waiting for transfers between devices: 23.2 us -> 40.2 us  [shards(): got = lax.all_to_all(units, 'grid', split_axis=0, concat_axis=0, tiled=True)]
    pallas_call x4, Pallas kernels: 131 us -> 116 us  [solve_group(): pl.pallas_call(functools.partial(group_kernel, list(panels), len(pieces),...]
    all_to_all x1 -> x3, starting transfers between devices: 3.56 us -> 13.6 us  [shards(): got = lax.all_to_all(units, 'grid', split_axis=0, concat_axis=0, tiled=True)]
    ppermute x15 -> x17, starting transfers between devices: 7.88 us -> 15.1 us  [the longest x15 7.72 us: gather_bands(): got.append(lax.ppermute(x, 'band', swap))]
    pallas_call x2, Pallas kernels: 21.9 us -> 16 us  [metric_units(): pl.pallas_call(functools.partial(metric_kernel, scale, [len(p) for p in p...]
    unnamed x36 -> x40, local copies, waits for them, and re-layouts: 3.75 us -> 9.33 us
    ppermute x15 -> x17, waiting for transfers between devices: 83.7 us -> 79.3 us  [the longest x15 59.9 us: gather_bands(): got.append(lax.ppermute(x, 'band', swap))]
  transfers between devices with their start and end apart: 19 -> 23, of which waited for: 8 -> 10; matrix products, arithmetic and copies ran while one was open for 2% -> 1% of each run, Pallas kernels for 19% -> 20%
where the time goes in v3:
time: 347 us; the launch traced here: 346 us
  waiting for transfers between devices  147 us (42%)
  Pallas kernels  140 us (40%)
  starting transfers between devices  42.5 us (12%)
  local copies, waits for them, and re-layouts  11.9 us (3%)
  other arithmetic  4.39 us (1%)
    pallas_call x4, Pallas kernels, solve_group(): pl.pallas_call(functools.partial(group_kernel, list(panels), len(pieces),...  116 us
    ppermute x15, waiting for transfers between devices, gather_bands(): got.append(lax.ppermute(x, 'band', swap))  59.9 us
    all_to_all x3, waiting for transfers between devices, shards(): got = lax.all_to_all(units, 'grid', split_axis=0, concat_axis=0, tiled=True)  40.2 us
    all_to_all x3, waiting for transfers between devices, shards(): part = lax.all_to_all(part, 'grid', split_axis=0, concat_axis=0, tiled=True)  27.4 us
    ppermute x2, waiting for transfers between devices, spread_lead(): got = lax.ppermute(held, 'band', pairs)  19.4 us
    pallas_call x2, Pallas kernels, metric_units(): pl.pallas_call(functools.partial(metric_kernel, scale, [len(p) for p in p...  16 us
    all_to_all x3, starting transfers between devices, shards(): part = lax.all_to_all(part, 'grid', split_axis=0, concat_axis=0, tiled=True)  13.8 us
    all_to_all x3, starting transfers between devices, shards(): got = lax.all_to_all(units, 'grid', split_axis=0, concat_axis=0, tiled=True)  13.6 us
  transfers between devices with their start and end apart: 23, of which 10 were waited for; matrix products, arithmetic and copies ran while one was open for 1% of the time, Pallas kernels for 20%

profile of v3, /device:TPU:0, one launch (start us, length us, event | category | flops | bytes accessed | tf_op | source)
XLA Modules:
  0.0 346.4 jit_solution(7326781213444291388)
XLA Ops:
  0.0 2.4 slice_select_fusion
  2.4 6.0 %collective-permute-start.9 = (bf16[2048,256]{1,0:T(8,128)(2,1)}, bf16[2048,256]{1,0:T(8,128)(2,1)}, u32[]{:S(2)}, u32[]{:S(2)}) collective-permute-start(bf16[2048,256]{1,0:T(8,128)(2,1)} %slice_select_fusion), channel_id=1, source_target_pairs={{0,16},{1,17},{2,18},{3,19},{4,20},{5,21},{6,22},{7,23}} | collective-permute-start | bytes 3145736 | tf_op jit(solution)/shard_map/ppermute | solution.py:232
  8.4 1.5 fusion.1
  9.9 2.0 collective-permute-start.2
  11.9 0.1 copy.21
  12.0 0.1 reduce-window.8
  12.1 0.1 add_reduce_fusion
  12.3 0.1 select_reduce_fusion.1
  12.4 0.1 broadcast_select_fusion.2
  12.5 0.1 select_n.73.coefs
  12.7 0.1 select_reduce_fusion.3
  12.9 0.1 iota_compare_fusion.2
  12.9 18.3 %collective-permute-done.9 = bf16[2048,256]{1,0:T(8,128)(2,1)} collective-permute-done((bf16[2048,256]{1,0:T(8,128)(2,1)}, bf16[2048,256]{1,0:T(8,128)(2,1)}, u32[]{:S(2)}, u32[]{:S(2)}) %collective-permute-start.9) | collective-permute-done | bytes 1048608 | tf_op jit(solution)/shard_map/ppermute | solution.py:232
  31.2 0.1 broadcast_select_fusion
  31.3 1.4 collective-permute-start.10
  32.7 0.7 select_reduce_fusion
  33.5 0.1 broadcast_and_fusion
  33.6 0.2 select_bitcast_fusion.weights
  33.8 1.1 collective-permute-done.10
  34.9 0.1 broadcast_select_fusion.1.lead
  35.0 1.9 lead_units.1
  36.9 0.8 copy-done.2
  37.7 5.8 %all-to-all-start.2 = ((f32[8,2,32,256]{3,2,1,0:T(8,128)}), f32[8,2,32,256]{3,2,1,0:T(8,128)}, u32[]{:S(2)}, u32[]{:S(2)}) async-start(f32[8,2,32,256]{3,2,1,0:T(8,128)} %copy-done.2), calls=%async_computation.2 | async-start | bytes 1048576 | tf_op jit(solution)/shard_map/all_to_all | solution.py:419
  43.5 0.1 collective-permute-start.1
  43.6 0.4 collective-permute-start
  44.1 9.6 %collective-permute-done.3.refs_4_ = bf16[1024,512]{1,0:T(8,128)(2,1)S(1)} collective-permute-done((bf16[1024,512]{1,0:T(8,128)(2,1)}, bf16[1024,512]{1,0:T(8,128)(2,1)S(1)}, u32[]{:S(2)}, u32[]{:S(2)}) %collective-permute-start.3) | collective-permute-done | bytes 1048608 | tf_op jit(solution)/shard_map/ppermute | solution.py:365
  53.7 11.3 %collective-permute-done.2.refs_3_ = bf16[1024,512]{1,0:T(8,128)(2,1)} collective-permute-done((bf16[1024,512]{1,0:T(8,128)(2,1)}, bf16[1024,512]{1,0:T(8,128)(2,1)}, u32[]{:S(2)}, u32[]{:S(2)}) %collective-permute-start.2) | collective-permute-done | bytes 1048608 | tf_op jit(solution)/shard_map/ppermute | solution.py:365
  65.0 1.9 sum_units.4
  66.9 5.8 %all-to-all-start.3 = ((f32[8,2,32,256]{3,2,1,0:T(8,128)}), f32[8,2,32,256]{3,2,1,0:T(8,128)}, u32[]{:S(2)}, u32[]{:S(2)}) async-start(f32[8,2,32,256]{3,2,1,0:T(8,128)} %sum_units.4), calls=%async_computation.3 | async-start | bytes 1048576 | tf_op jit(solution)/shard_map/all_to_all | solution.py:421
  72.8 0.7 dynamic-slice_bitcast_fusion
  73.5 0.1 copy.23.ids
  73.6 8.1 %metric_units.3 = (f32[8,4,32,256]{3,2,1,0:T(8,128)S(1)}, bf16[512,2048]{1,0:T(8,128)(2,1)S(1)}) custom-call(s32[1]{0:T(128)} %bitcast.where, s32[4,2]{1,0:T(4,128)S(1)} %copy.23.ids, bf16[64,2048]{1,0:T(8,128)(2,1)S(1)} %select_bitcast_fusion.weights, f32[64,64]{1,0:T(8,128)S(1)} %select_n.73.coefs, bf16[2048,512]{1,0:T(8,128)(2,1)S(1)} %copy-done, ...), custom_call_target="tpu_custom_call" | custom-call | flops 1073741824 | bytes 8388608 | tf_op jit(solution)/shard_map/metric_units/pallas_call | solution.py:182
  81.7 1.0 copy-done.3
  82.7 1.3 copy-done.4
  84.0 4.1 %all-to-all-done.3.refs_0_ = f32[8,2,32,256]{3,2,1,0:T(8,128)} async-done(((f32[8,2,32,256]{3,2,1,0:T(8,128)}), f32[8,2,32,256]{3,2,1,0:T(8,128)}, u32[]{:S(2)}, u32[]{:S(2)}) %all-to-all-start.3) | async-done | bytes 524320 | tf_op jit(solution)/shard_map/all_to_all | solution.py:421
  88.0 4.2 %all-to-all-start.4 = ((f32[8,4,32,256]{3,2,1,0:T(8,128)}), f32[8,4,32,256]{3,2,1,0:T(8,128)}, u32[]{:S(2)}, u32[]{:S(2)}) async-start(f32[8,4,32,256]{3,2,1,0:T(8,128)} %copy-done.3), calls=%async_computation.4 | async-start | bytes 2097152 | tf_op jit(solution)/shard_map/all_to_all | solution.py:419
  92.3 0.1 copy.22.ids
  92.4 7.9 %metric_units.2 = f32[8,4,32,256]{3,2,1,0:T(8,128)S(1)} custom-call(s32[1]{0:T(128)} %bitcast.where, s32[4,2]{1,0:T(4,128)S(1)} %copy.22.ids, bf16[64,2048]{1,0:T(8,128)(2,1)S(1)} %select_bitcast_fusion.weights, f32[64,64]{1,0:T(8,128)S(1)} %select_n.73.coefs, bf16[2048,512]{1,0:T(8,128)(2,1)S(1)} %copy-done, ...), custom_call_target="tpu_custom_call" | custom-call | flops 1073741824 | bytes 8388608 | tf_op jit(solution)/shard_map/metric_units/pallas_call | solution.py:182
  100.3 1.0 copy-done.1
  101.3 16.6 %all-to-all-done.4.got = f32[8,4,32,256]{3,2,1,0:T(8,128)} async-done(((f32[8,4,32,256]{3,2,1,0:T(8,128)}), f32[8,4,32,256]{3,2,1,0:T(8,128)}, u32[]{:S(2)}, u32[]{:S(2)}) %all-to-all-start.4) | async-done | bytes 1048608 | tf_op jit(solution)/shard_map/all_to_all | solution.py:419
  117.9 3.6 %all-to-all-start = ((f32[8,4,32,256]{3,2,1,0:T(8,128)}), f32[8,4,32,256]{3,2,1,0:T(8,128)S(1)}, u32[]{:S(2)}, u32[]{:S(2)}) async-start(f32[8,4,32,256]{3,2,1,0:T(8,128)} %copy-done.1), calls=%async_computation | async-start | bytes 2097152 | tf_op jit(solution)/shard_map/all_to_all | solution.py:419
  121.5 2.3 sum_units.5
  123.7 23.6 %all-to-all-done.got = f32[8,4,32,256]{3,2,1,0:T(8,128)S(1)} async-done(((f32[8,4,32,256]{3,2,1,0:T(8,128)}), f32[8,4,32,256]{3,2,1,0:T(8,128)S(1)}, u32[]{:S(2)}, u32[]{:S(2)}) %all-to-all-start) | async-done | bytes 1048608 | tf_op jit(solution)/shard_map/all_to_all | solution.py:419
  147.3 4.2 %all-to-all-start.5 = ((f32[8,4,32,256]{3,2,1,0:T(8,128)}), f32[8,4,32,256]{3,2,1,0:T(8,128)}, u32[]{:S(2)}, u32[]{:S(2)}) async-start(f32[8,4,32,256]{3,2,1,0:T(8,128)} %sum_units.5), calls=%async_computation.5 | async-start | bytes 2097152 | tf_op jit(solution)/shard_map/all_to_all | solution.py:421
  151.6 2.3 sum_units.3
  153.9 23.3 %all-to-all-done.5.refs_0_ = f32[8,4,32,256]{3,2,1,0:T(8,128)} async-done(((f32[8,4,32,256]{3,2,1,0:T(8,128)}), f32[8,4,32,256]{3,2,1,0:T(8,128)}, u32[]{:S(2)}, u32[]{:S(2)}) %all-to-all-start.5) | async-done | bytes 1048608 | tf_op jit(solution)/shard_map/all_to_all | solution.py:421
  177.1 3.7 %all-to-all-start.1 = ((f32[8,4,32,256]{3,2,1,0:T(8,128)}), f32[8,4,32,256]{3,2,1,0:T(8,128)S(1)}, u32[]{:S(2)}, u32[]{:S(2)}) async-start(f32[8,4,32,256]{3,2,1,0:T(8,128)} %sum_units.3), calls=%async_computation.1 | async-start | bytes 2097152 | tf_op jit(solution)/shard_map/all_to_all | solution.py:421
  180.9 2.5 collective-permute-start.15
  183.4 0.1 collective-permute-start.12
  183.5 34.1 %collective-permute-done.12.refs_2_ = f32[8,2,32,256]{3,2,1,0:T(8,128)S(1)} collective-permute-done((f32[8,2,32,256]{3,2,1,0:T(8,128)}, f32[8,2,32,256]{3,2,1,0:T(8,128)S(1)}, u32[]{:S(2)}, u32[]{:S(2)}) %collective-permute-start.12) | collective-permute-done | bytes 524320 | tf_op jit(solution)/shard_map/ppermute | solution.py:365
  217.6 0.8 copy-done.6
  218.4 1.7 collective-permute-start.7
  220.1 0.2 collective-permute-start.14
  220.3 0.3 collective-permute-start.16
  220.6 0.8 copy-done.8
  221.4 1.6 copy-done.5
  223.0 1.0 copy-done.7
  224.1 1.0 copy-done.9
  225.1 13.6 %solve_group.4 = (bf16[2048,256]{1,0:T(8,128)(2,1)S(1)}, bf16[2048,256]{1,0:T(8,128)(2,1)S(1)}, bf16[512,256]{1,0:T(8,128)(2,1)S(1)}) custom-call(s32[1]{0:T(128)} %bitcast.where, s32[8,2]{1,0:T(8,128)S(1)} %copy-done.13, f32[8,2,32,256]{3,2,1,0:T(8,128)} %all-to-all-done.3.refs_0_, f32[8,2,32,256]{3,2,1,0:T(8,128)S(1)} %copy-done.9, ...), custom_call_target="tpu_custom_call" | custom-call | flops 10000000000 | bytes 8388608 | tf_op jit(solution)/shard_map/solve_group/pallas_call | solution.py:336
  238.7 0.3 collective-permute-start.6
  239.0 4.9 %collective-permute-done.7.refs_2_ = f32[8,4,32,256]{3,2,1,0:T(8,128)S(1)} collective-permute-done((f32[8,4,32,256]{3,2,1,0:T(8,128)S(1)}, f32[8,4,32,256]{3,2,1,0:T(8,128)S(1)}, u32[]{:S(2)}, u32[]{:S(2)}) %collective-permute-start.7) | collective-permute-done | bytes 1048608 | tf_op jit(solution)/shard_map/ppermute | solution.py:365
  244.0 16.3 %solve_group.5 = (bf16[2048,256]{1,0:T(8,128)(2,1)S(1)}, bf16[2048,256]{1,0:T(8,128)(2,1)S(1)}, bf16[512,256]{1,0:T(8,128)(2,1)S(1)}) custom-call(s32[1]{0:T(128)} %bitcast.where, s32[7,2]{1,0:T(8,128)S(1)} %copy-done.12, f32[8,4,32,256]{3,2,1,0:T(8,128)} %all-to-all-done.5.refs_0_, f32[8,4,32,256]{3,2,1,0:T(8,128)S(1)} %collective-permute-done.14.refs_1_, ...), custom_call_target="tpu_custom_call" | custom-call | flops 10000000000 | bytes 8388608 | tf_op jit(solution)/shard_map/solve_group/pallas_call | solution.py:336
  260.3 16.4 %solve_group.6 = (bf16[2048,256]{1,0:T(8,128)(2,1)S(1)}, bf16[2048,256]{1,0:T(8,128)(2,1)S(1)}, bf16[512,256]{1,0:T(8,128)(2,1)S(1)}) custom-call(s32[1]{0:T(128)} %bitcast.where, s32[6,2]{1,0:T(8,128)S(1)} %copy-done.11, f32[8,4,32,256]{3,2,1,0:T(8,128)} %all-to-all-done.5.refs_0_, f32[8,4,32,256]{3,2,1,0:T(8,128)S(1)} %collective-permute-done.14.refs_1_, ...), custom_call_target="tpu_custom_call" | custom-call | flops 10000000000 | bytes 8388608 | tf_op jit(solution)/shard_map/solve_group/pallas_call | solution.py:336
  276.8 69.4 %solve_group.7 = bf16[512,2048]{1,0:T(8,128)(2,1)} custom-call(s32[1]{0:T(128)} %bitcast.where, s32[15,2]{1,0:T(8,128)S(1)} %copy-done.10, f32[8,4,32,256]{3,2,1,0:T(8,128)S(1)} %all-to-all-done.1.refs_0_, f32[8,4,32,256]{3,2,1,0:T(8,128)S(1)} %collective-permute-done.6.refs_1_, f32[8,4,32,256]{3,2,1,0:T(8,128)S(1)} %collective-permute-done.7.refs_2_, ...), custom_call_target="tpu_custom_call" | custom-call | flops 49999998976 | bytes 8388608 | tf_op jit(solution)/shard_map/solve_group/pallas_call | solution.py:336
  (55 shorter events, 0.2 us)
Async XLA Ops:
  0.0 8.4 %copy-start = (bf16[2048,512]{1,0:T(8,128)(2,1)S(1)}, bf16[2048,512]{1,0:T(8,128)(2,1)}, u32[]{:S(2)}) copy-start(bf16[2048,512]{1,0:T(8,128)(2,1)} %own.1) | copy-start | bytes 6291460
  2.4 9.5 %copy-start.17 = (s32[64]{0:T(128)S(1)}, s32[64]{0:T(128)}, u32[]{:S(2)}) copy-start(s32[64]{0:T(128)} %param.16) | copy-start | bytes 772
  2.4 9.8 %copy-start.16 = (f32[64,8,8]{0,2,1:T(8,128)S(1)}, f32[64,8,8]{0,2,1:T(8,128)}, u32[]{:S(2)}) copy-start(f32[64,8,8]{0,2,1:T(8,128)} %param.17) | copy-start | bytes 49156
  2.4 10.2 %copy-start.18 = (s32[64]{0:T(128)S(1)}, s32[64]{0:T(128)}, u32[]{:S(2)}) copy-start(s32[64]{0:T(128)} %param.14) | copy-start | bytes 772
  2.4 10.2 %copy-start.19 = (s32[64]{0:T(128)S(1)}, s32[64]{0:T(128)}, u32[]{:S(2)}) copy-start(s32[64]{0:T(128)} %param.15) | copy-start | bytes 772
  2.4 28.8 %collective-permute-start.9 = (bf16[2048,256]{1,0:T(8,128)(2,1)}, bf16[2048,256]{1,0:T(8,128)(2,1)}, u32[]{:S(2)}, u32[]{:S(2)}) collective-permute-start(bf16[2048,256]{1,0:T(8,128)(2,1)} %slice_select_fusion), channel_id=1, source_target_pairs={{0,16},{1,17},{2,18},{3,19},{4,20},{5,21},{6,22},{7,23}} | collective-permute-start | bytes 3145736 | tf_op jit(solution)/shard_map/ppermute | solution.py:232
  9.9 43.8 %collective-permute-start.3 = (bf16[1024,512]{1,0:T(8,128)(2,1)}, bf16[1024,512]{1,0:T(8,128)(2,1)S(1)}, u32[]{:S(2)}, u32[]{:S(2)}) collective-permute-start(bf16[1024,512]{1,0:T(8,128)(2,1)} %get-tuple-element.31), channel_id=1, source_target_pairs={{0,16},{8,24},{16,0},{24,8},{1,17},{9,25},{17,1},{25,9},{2,18},{10... | collective-permute-start | bytes 3145736 | tf_op jit(solution)/shard_map/ppermute | solution.py:365
  9.9 55.1 %collective-permute-start.2 = (bf16[1024,512]{1,0:T(8,128)(2,1)}, bf16[1024,512]{1,0:T(8,128)(2,1)}, u32[]{:S(2)}, u32[]{:S(2)}) collective-permute-start(bf16[1024,512]{1,0:T(8,128)(2,1)} %get-tuple-element.32), channel_id=1, source_target_pairs={{0,16},{8,24},{16,0},{24,8},{1,17},{9,25},{17,1},{25,9},{2,18},{10... | collective-permute-start | bytes 3145736 | tf_op jit(solution)/shard_map/ppermute | solution.py:365
  12.7 20.0 %copy-start.15 = (bf16[64,8,128]{2,1,0:T(8,128)(2,1)S(1)}, bf16[64,8,128]{2,1,0:T(8,128)(2,1)}, u32[]{:S(2)}) copy-start(bf16[64,8,128]{2,1,0:T(8,128)(2,1)} %param.13) | copy-start | bytes 393220
  31.3 3.6 %collective-permute-start.10 = (bf16[2048,256]{1,0:T(8,128)(2,1)S(1)}, bf16[2048,256]{1,0:T(8,128)(2,1)S(1)}, u32[]{:S(2)}, u32[]{:S(2)}) collective-permute-start(bf16[2048,256]{1,0:T(8,128)(2,1)S(1)} %broadcast_select_fusion), channel_id=1, source_target_pairs={{0,8},{16,24},{1,9},{17,25},{2,10},{18,26},{3,11},{19,27},{4,12},{... | collective-permute-start | bytes 3145736 | tf_op jit(solution)/shard_map/ppermute | solution.py:232
  36.9 0.8 copy-start.2
  37.7 27.3 %all-to-all-start.2 = ((f32[8,2,32,256]{3,2,1,0:T(8,128)}), f32[8,2,32,256]{3,2,1,0:T(8,128)}, u32[]{:S(2)}, u32[]{:S(2)}) async-start(f32[8,2,32,256]{3,2,1,0:T(8,128)} %copy-done.2), calls=%async_computation.2 | async-start | bytes 1048576 | tf_op jit(solution)/shard_map/all_to_all | solution.py:419
  43.5 30.0 %collective-permute-start.1 = (bf16[1024,512]{1,0:T(8,128)(2,1)}, bf16[1024,512]{1,0:T(8,128)(2,1)}, u32[]{:S(2)}, u32[]{:S(2)}) collective-permute-start(bf16[1024,512]{1,0:T(8,128)(2,1)} %get-tuple-element.31), channel_id=1, source_target_pairs={{0,8},{8,0},{16,24},{24,16},{1,9},{9,1},{17,25},{25,17},{2,10},{10... | collective-permute-start | bytes 3145736 | tf_op jit(solution)/shard_map/ppermute | solution.py:365
  43.6 29.9 %collective-permute-start = (bf16[1024,512]{1,0:T(8,128)(2,1)}, bf16[1024,512]{1,0:T(8,128)(2,1)}, u32[]{:S(2)}, u32[]{:S(2)}) collective-permute-start(bf16[1024,512]{1,0:T(8,128)(2,1)} %get-tuple-element.32), channel_id=1, source_target_pairs={{0,8},{8,0},{16,24},{24,16},{1,9},{9,1},{17,25},{25,17},{2,10},{10... | collective-permute-start | bytes 3145736 | tf_op jit(solution)/shard_map/ppermute | solution.py:365
  53.7 19.9 %collective-permute-start.5 = (bf16[1024,512]{1,0:T(8,128)(2,1)S(1)}, bf16[1024,512]{1,0:T(8,128)(2,1)}, u32[]{:S(2)}, u32[]{:S(2)}) collective-permute-start(bf16[1024,512]{1,0:T(8,128)(2,1)S(1)} %collective-permute-done.3.refs_4_), channel_id=1, source_target_pairs={{0,8},{8,0},{16,24},{24,16},{1,9},{9,1},{17,25},{25,17},{2,10},{10... | collective-permute-start | bytes 3145736 | tf_op jit(solution)/shard_map/ppermute | solution.py:365
  65.0 8.6 %collective-permute-start.4 = (bf16[1024,512]{1,0:T(8,128)(2,1)}, bf16[1024,512]{1,0:T(8,128)(2,1)}, u32[]{:S(2)}, u32[]{:S(2)}) collective-permute-start(bf16[1024,512]{1,0:T(8,128)(2,1)} %collective-permute-done.2.refs_3_), channel_id=1, source_target_pairs={{0,8},{8,0},{16,24},{24,16},{1,9},{9,1},{17,25},{25,17},{2,10},{10... | collective-permute-start | bytes 3145736 | tf_op jit(solution)/shard_map/ppermute | solution.py:365
  66.9 21.1 %all-to-all-start.3 = ((f32[8,2,32,256]{3,2,1,0:T(8,128)}), f32[8,2,32,256]{3,2,1,0:T(8,128)}, u32[]{:S(2)}, u32[]{:S(2)}) async-start(f32[8,2,32,256]{3,2,1,0:T(8,128)} %sum_units.4), calls=%async_computation.3 | async-start | bytes 1048576 | tf_op jit(solution)/shard_map/all_to_all | solution.py:421
  81.7 1.0 copy-start.3
  82.7 1.3 copy-start.4
  88.0 29.9 %all-to-all-start.4 = ((f32[8,4,32,256]{3,2,1,0:T(8,128)}), f32[8,4,32,256]{3,2,1,0:T(8,128)}, u32[]{:S(2)}, u32[]{:S(2)}) async-start(f32[8,4,32,256]{3,2,1,0:T(8,128)} %copy-done.3), calls=%async_computation.4 | async-start | bytes 2097152 | tf_op jit(solution)/shard_map/all_to_all | solution.py:419
  100.3 1.0 copy-start.1
  117.9 29.4 %all-to-all-start = ((f32[8,4,32,256]{3,2,1,0:T(8,128)}), f32[8,4,32,256]{3,2,1,0:T(8,128)S(1)}, u32[]{:S(2)}, u32[]{:S(2)}) async-start(f32[8,4,32,256]{3,2,1,0:T(8,128)} %copy-done.1), calls=%async_computation | async-start | bytes 2097152 | tf_op jit(solution)/shard_map/all_to_all | solution.py:419
  147.3 4.2 %copy-start.14 = (f32[8,4,32,256]{3,2,1,0:T(8,128)}, f32[8,4,32,256]{3,2,1,0:T(8,128)S(1)}, u32[]{:S(2)}) copy-start(f32[8,4,32,256]{3,2,1,0:T(8,128)S(1)} %all-to-all-done.got) | copy-start | bytes 3145732
  147.3 29.8 %all-to-all-start.5 = ((f32[8,4,32,256]{3,2,1,0:T(8,128)}), f32[8,4,32,256]{3,2,1,0:T(8,128)}, u32[]{:S(2)}, u32[]{:S(2)}) async-start(f32[8,4,32,256]{3,2,1,0:T(8,128)} %sum_units.5), calls=%async_computation.5 | async-start | bytes 2097152 | tf_op jit(solution)/shard_map/all_to_all | solution.py:421
  151.6 69.9 %copy-start.13 = (s32[8,2]{1,0:T(8,128)S(1)}, s32[8,2]{1,0:T(8,128)}, u32[]{:S(2)}) copy-start(s32[8,2]{1,0:T(8,128)} %constant.58.clone.spots) | copy-start | bytes 196
  177.1 41.2 %all-to-all-start.1 = ((f32[8,4,32,256]{3,2,1,0:T(8,128)}), f32[8,4,32,256]{3,2,1,0:T(8,128)S(1)}, u32[]{:S(2)}, u32[]{:S(2)}) async-start(f32[8,4,32,256]{3,2,1,0:T(8,128)} %sum_units.3), calls=%async_computation.1 | async-start | bytes 2097152 | tf_op jit(solution)/shard_map/all_to_all | solution.py:421
  180.9 39.5 %collective-permute-start.15 = (f32[8,4,32,256]{3,2,1,0:T(8,128)}, f32[8,4,32,256]{3,2,1,0:T(8,128)S(1)}, u32[]{:S(2)}, u32[]{:S(2)}) collective-permute-start(f32[8,4,32,256]{3,2,1,0:T(8,128)} %all-to-all-done.5.refs_0_), channel_id=1, source_target_pairs={{0,16},{8,24},{16,0},{24,8},{1,17},{9,25},{17,1},{25,9},{2,18},{10... | collective-permute-start | bytes 3145736 | tf_op jit(solution)/shard_map/ppermute | solution.py:365
  183.4 34.1 %collective-permute-start.12 = (f32[8,2,32,256]{3,2,1,0:T(8,128)}, f32[8,2,32,256]{3,2,1,0:T(8,128)S(1)}, u32[]{:S(2)}, u32[]{:S(2)}) collective-permute-start(f32[8,2,32,256]{3,2,1,0:T(8,128)} %all-to-all-done.3.refs_0_), channel_id=1, source_target_pairs={{0,16},{8,24},{16,0},{24,8},{1,17},{9,25},{17,1},{25,9},{2,18},{10... | collective-permute-start | bytes 1572872 | tf_op jit(solution)/shard_map/ppermute | solution.py:365
  183.5 37.1 %collective-permute-start.11 = (f32[8,2,32,256]{3,2,1,0:T(8,128)}, f32[8,2,32,256]{3,2,1,0:T(8,128)S(1)}, u32[]{:S(2)}, u32[]{:S(2)}) collective-permute-start(f32[8,2,32,256]{3,2,1,0:T(8,128)} %all-to-all-done.3.refs_0_), channel_id=1, source_target_pairs={{0,8},{8,0},{16,24},{24,16},{1,9},{9,1},{17,25},{25,17},{2,10},{10... | collective-permute-start | bytes 1572872 | tf_op jit(solution)/shard_map/ppermute | solution.py:365
  217.6 3.9 %collective-permute-start.13 = (f32[8,2,32,256]{3,2,1,0:T(8,128)S(1)}, f32[8,2,32,256]{3,2,1,0:T(8,128)}, u32[]{:S(2)}, u32[]{:S(2)}) collective-permute-start(f32[8,2,32,256]{3,2,1,0:T(8,128)S(1)} %collective-permute-done.12.refs_2_), channel_id=1, source_target_pairs={{0,8},{8,0},{16,24},{24,16},{1,9},{9,1},{17,25},{25,17},{2,10},{10... | collective-permute-start | bytes 1572872 | tf_op jit(solution)/shard_map/ppermute | solution.py:365
  217.6 0.8 copy-start.6
  218.4 25.6 %collective-permute-start.7 = (f32[8,4,32,256]{3,2,1,0:T(8,128)S(1)}, f32[8,4,32,256]{3,2,1,0:T(8,128)S(1)}, u32[]{:S(2)}, u32[]{:S(2)}) collective-permute-start(f32[8,4,32,256]{3,2,1,0:T(8,128)S(1)} %all-to-all-done.1.refs_0_), channel_id=1, source_target_pairs={{0,16},{8,24},{16,0},{24,8},{1,17},{9,25},{17,1},{25,9},{2,18},{10... | collective-permute-start | bytes 3145736 | tf_op jit(solution)/shard_map/ppermute | solution.py:365
  220.1 23.8 %collective-permute-start.14 = (f32[8,4,32,256]{3,2,1,0:T(8,128)}, f32[8,4,32,256]{3,2,1,0:T(8,128)S(1)}, u32[]{:S(2)}, u32[]{:S(2)}) collective-permute-start(f32[8,4,32,256]{3,2,1,0:T(8,128)} %all-to-all-done.5.refs_0_), channel_id=1, source_target_pairs={{0,8},{8,0},{16,24},{24,16},{1,9},{9,1},{17,25},{25,17},{2,10},{10... | collective-permute-start | bytes 3145736 | tf_op jit(solution)/shard_map/ppermute | solution.py:365
  220.3 23.6 %collective-permute-start.16 = (f32[8,4,32,256]{3,2,1,0:T(8,128)S(1)}, f32[8,4,32,256]{3,2,1,0:T(8,128)S(1)}, u32[]{:S(2)}, u32[]{:S(2)}) collective-permute-start(f32[8,4,32,256]{3,2,1,0:T(8,128)S(1)} %collective-permute-done.15.refs_2_), channel_id=1, source_target_pairs={{0,8},{8,0},{16,24},{24,16},{1,9},{9,1},{17,25},{25,17},{2,10},{10... | collective-permute-start | bytes 3145736 | tf_op jit(solution)/shard_map/ppermute | solution.py:365
  220.6 0.8 copy-start.8
  221.4 1.6 copy-start.5
  223.0 1.0 copy-start.7
  224.1 1.0 copy-start.9
  225.1 18.8 %copy-start.12 = (s32[7,2]{1,0:T(8,128)S(1)}, s32[7,2]{1,0:T(8,128)}, u32[]{:S(2)}) copy-start(s32[7,2]{1,0:T(8,128)} %constant.59.clone.spots) | copy-start | bytes 172
  238.7 38.0 %collective-permute-start.6 = (f32[8,4,32,256]{3,2,1,0:T(8,128)S(1)}, f32[8,4,32,256]{3,2,1,0:T(8,128)S(1)}, u32[]{:S(2)}, u32[]{:S(2)}) collective-permute-start(f32[8,4,32,256]{3,2,1,0:T(8,128)S(1)} %all-to-all-done.1.refs_0_), channel_id=1, source_target_pairs={{0,8},{8,0},{16,24},{24,16},{1,9},{9,1},{17,25},{25,17},{2,10},{10... | collective-permute-start | bytes 3145736 | tf_op jit(solution)/shard_map/ppermute | solution.py:365
  243.9 32.9 %collective-permute-start.8 = (f32[8,4,32,256]{3,2,1,0:T(8,128)S(1)}, f32[8,4,32,256]{3,2,1,0:T(8,128)S(1)}, u32[]{:S(2)}, u32[]{:S(2)}) collective-permute-start(f32[8,4,32,256]{3,2,1,0:T(8,128)S(1)} %collective-permute-done.7.refs_2_), channel_id=1, source_target_pairs={{0,8},{8,0},{16,24},{24,16},{1,9},{9,1},{17,25},{25,17},{2,10},{10... | collective-permute-start | bytes 3145736 | tf_op jit(solution)/shard_map/ppermute | solution.py:365
  244.0 16.4 %copy-start.11 = (s32[6,2]{1,0:T(8,128)S(1)}, s32[6,2]{1,0:T(8,128)}, u32[]{:S(2)}) copy-start(s32[6,2]{1,0:T(8,128)} %constant.60.clone.spots) | copy-start | bytes 148
  260.3 16.5 %copy-start.10 = (s32[15,2]{1,0:T(8,128)S(1)}, s32[15,2]{1,0:T(8,128)}, u32[]{:S(2)}) copy-start(s32[15,2]{1,0:T(8,128)} %constant.61.clone.spots) | copy-start | bytes 364

commit v4 on v3

--- a/solution.py
+++ b/solution.py
@@ -97,10 +97,20 @@
     return [range(a, min(b, count)) for a, b in zip(GROUPS, ends) if a < count]
 
 
-def place_units(panels, count, devices):
-    blocks = [(i, p) for p in panels for i in range(p, count)]
+def group_blocks(groups, count, devices):
+    listed, late = [], []
+    for panels in groups:
+        blocks = late + [(i, p) for p in panels for i in range(p, count)]
+        late = []
+        if panels[-1] + 2 < count and len(blocks) % devices == 1:
+            late = [blocks.pop()]
+        listed.append((blocks, late))
+    return listed
+
+
+def place_units(blocks, devices):
     size = -(-len(blocks) // devices)
-    blocks += [blocks[-1]] * (size * devices - len(blocks))
+    blocks = blocks + [blocks[-1]] * (size * devices - len(blocks))
     held = [blocks[d * size : (d + 1) * size] for d in range(devices)]
     where = {}
     for k, block in enumerate(blocks):
@@ -253,14 +263,20 @@
     )(got)
 
 
-def group_kernel(panels, npieces, earlier, last, where, spots, *refs):
+def group_kernel(panels, npieces, earlier, last, owed, owing, where, spots, *refs):
     pieces = [[r] for r in refs[:npieces]]
     o_ref = refs[npieces]
     refs = refs[npieces + 1 :]
     olds = [refs[3 * q : 3 * q + 3] for q in range(earlier)]
     refs = refs[3 * earlier :]
-    nout = 1 if last else 3
+    if owed:
+        t_old, refs = refs[0], refs[1:]
+    nout = (1 if last else 3) + owing
     outs, (buf, m, t, s, c, pv, sem) = refs[:nout], refs[nout : nout + 7]
+    if owing:
+        t_out, outs = outs[-1], outs[:-1]
+    if owed:
+        refs, (h_old, l_old) = refs[:-2], refs[-2:]
     if last:
         y_out, (hi, lo) = outs[0], refs[nout + 7 :]
         base = panels[0] * BLOCK
@@ -278,6 +294,20 @@
     def block(k):
         return buf[spots[k, 0], :, spots[k, 1]].reshape(BLOCK, BLOCK)
 
+    if owed:
+        end = slice((count - 1) * BLOCK, count * BLOCK)
+        used = slice(panels[0] * BLOCK, (count - 1) * BLOCK)
+        before = slice((panels[0] - 1) * BLOCK, panels[0] * BLOCK)
+        h_old[used, :] = olds[-1][0][used, :]
+        l_old[used, :] = olds[-1][1][used, :]
+        x = block(0)
+        for h, l, _ in olds[:-1]:
+            x = x - dotg(h[end, :], h[before, :], 1, 1)
+            x = x - (dotg(h[end, :], l[before, :], 1, 1) + dotg(l[end, :], h[before, :], 1, 1))
+        h_old[end, :], l_old[end, :] = split(dot3(x, t_old[...]))
+        olds = list(olds[:-1]) + [(h_old, l_old, olds[-1][2])]
+        first = 1
+
     for step, p in enumerate(panels):
         K = step * BLOCK
         mine = slice(K, K + BLOCK)
@@ -303,7 +333,7 @@
             hi[ri, mine], lo[ri, mine] = split(r)
             return 0
 
-        lax.fori_loop(0, count - 1 - p, rows_below, 0)
+        lax.fori_loop(0, count - 1 - p - owing, rows_below, 0)
 
         def rows_orbital(n, _):
             ri = pl.ds(pl.multiple_of(n * BLOCK, BLOCK), BLOCK)
@@ -317,9 +347,11 @@
 
         lax.fori_loop(0, height // BLOCK, rows_orbital, 0)
         first += count - p
-
-
-def solve_group(panels, band, spots, pieces, rows, olds):
+    if owing:
+        t_out[...] = t[...]
+
+
+def solve_group(panels, band, spots, pieces, rows, olds, t_old, owing):
     height, bands = rows.shape
     width = len(panels) * BLOCK
     last = panels[-1] + 1 == bands // BLOCK
@@ -332,9 +364,14 @@
     else:
         outs = [jax.ShapeDtypeStruct((bands, width), bf16)] * 2 + [jax.ShapeDtypeStruct((height, width), bf16)]
         more = []
+    if owing:
+        outs.append(jax.ShapeDtypeStruct((BLOCK, BLOCK), f32))
+    if t_old is not None:
+        flat.append(t_old)
+        more = more + [pltpu.VMEM((bands, BLOCK), bf16)] * 2
     flops = len(panels) * 10 * 10**9
     return pl.pallas_call(
-        functools.partial(group_kernel, list(panels), len(pieces), len(olds), last),
+        functools.partial(group_kernel, list(panels), len(pieces), len(olds), last, t_old is not None, owing),
         out_shape=outs,
         in_specs=[smem, smem] + [pl.BlockSpec(memory_space=pl.ANY)] * len(pieces) + [vmem] * (1 + len(flat)),
         out_specs=[vmem] * len(outs),
@@ -406,7 +443,8 @@
     weights, coefs = atom_rows(projectors, sphere_start, proj_count, owner_slab, correlation_coef, grid_rows)
 
     groups = panel_groups(count)
-    plans = [place_units(panels, count, devices) for panels in groups]
+    listed = group_blocks(groups, count, devices)
+    plans = [place_units(blocks, devices) for blocks, _ in listed]
     tables = [jnp.asarray(held, jnp.int32)[band_index] for _, held, _ in plans]
     assert plans[0][0] == width // BLOCK
     sizes = [size for size, _, _ in plans]
@@ -414,16 +452,24 @@
     second, rows = metric_units(band, tables[1], sizes[1:2], slabs, weights, coefs, pieces, scale, height)
     ids = jnp.concatenate(tables[2:])
     rest = metric_units(band, ids, sizes[2:], slabs, weights, coefs, pieces, scale, 0)
-    olds = []
-    for panels, (_, _, where), units in zip(groups, plans, [first, second] + list(rest)):
+    olds, t_old, late = [], None, []
+    for g, (panels, (_, _, where), units) in enumerate(zip(groups, plans, [first, second] + list(rest))):
         got = lax.all_to_all(units, "grid", split_axis=0, concat_axis=0, tiled=True)
         part = sum_units(got)
         part = lax.all_to_all(part, "grid", split_axis=0, concat_axis=0, tiled=True)
         all_parts = [x[0] for x in gather_bands([part], devices)]
         runs = [list(panels)] if panels[-1] + 1 == count else [[p] for p in panels]
         for run in runs:
-            order = [where[i, p] for p in run for i in range(p, count)]
-            olds.append(solve_group(run, band, jnp.asarray(order, jnp.int32), all_parts, rows, olds))
+            order = [where[block] for block in late]
+            missing = listed[g][1] if run[-1] == panels[-1] else []
+            order += [where[i, p] for p in run for i in range(p, count) if (i, p) not in missing]
+            spots = jnp.asarray(order, jnp.int32)
+            got = solve_group(run, band, spots, all_parts, rows, olds, t_old, len(missing))
+            late, t_old = [], None
+            if missing:
+                late, t_old = missing, got[-1]
+                got = got[:-1]
+            olds.append(got)
     return olds[-1][0]
 
 

time: 347 us -> 349 us (level)
    ppermute x15, waiting for transfers between devices: 59.9 us -> 20.9 us  [gather_bands(): got.append(lax.ppermute(x, 'band', swap))]
    ppermute x2, waiting for transfers between devices: 19.4 us -> 49.7 us  [spread_lead(): got = lax.ppermute(held, 'band', pairs)]
    all_to_all x3, waiting for transfers between devices: 40.2 us -> 46.3 us  [shards(): got = lax.all_to_all(units, 'grid', split_axis=0, concat_axis=0, tiled=True)]
    ppermute x15, starting transfers between devices: 7.72 us -> 12.2 us  [gather_bands(): got.append(lax.ppermute(x, 'band', swap))]
  transfers between devices with their start and end apart: 23 -> 23, of which waited for: 10 -> 11; matrix products, arithmetic and copies ran while one was open for 1% -> 1% of each run, Pallas kernels for 20% -> 20%
where the time goes in v4:
time: 349 us; the launch traced here: 348 us
  waiting for transfers between devices  147 us (42%)
  Pallas kernels  141 us (40%)
  starting transfers between devices  44.7 us (13%)
  local copies, waits for them, and re-layouts  12.6 us (4%)
    pallas_call x4, Pallas kernels, solve_group(): pl.pallas_call(functools.partial(group_kernel, list(panels), len(pieces),...  117 us
    ppermute x2, waiting for transfers between devices, spread_lead(): got = lax.ppermute(held, 'band', pairs)  49.7 us
    all_to_all x3, waiting for transfers between devices, shards(): got = lax.all_to_all(units, 'grid', split_axis=0, concat_axis=0, tiled=True)  46.3 us
    all_to_all x3, waiting for transfers between devices, shards(): part = lax.all_to_all(part, 'grid', split_axis=0, concat_axis=0, tiled=True)  29.7 us
    ppermute x15, waiting for transfers between devices, gather_bands(): got.append(lax.ppermute(x, 'band', swap))  20.9 us
    pallas_call x2, Pallas kernels, metric_units(): pl.pallas_call(functools.partial(metric_kernel, scale, [len(p) for p in p...  15.4 us
    all_to_all x3, starting transfers between devices, shards(): got = lax.all_to_all(units, 'grid', split_axis=0, concat_axis=0, tiled=True)  13.7 us
    all_to_all x3, starting transfers between devices, shards(): part = lax.all_to_all(part, 'grid', split_axis=0, concat_axis=0, tiled=True)  12.8 us
  transfers between devices with their start and end apart: 23, of which 11 were waited for; matrix products, arithmetic and copies ran while one was open for 1% of the time, Pallas kernels for 20%

profile of v4, /device:TPU:0, one launch (start us, length us, event | category | flops | bytes accessed | tf_op | source)
XLA Modules:
  0.0 348.2 jit_solution(8458853112380524044)
XLA Ops:
  0.0 3.2 fusion.1
  3.2 3.0 collective-permute-start.3
  6.2 0.2 collective-permute-start.2
  6.4 0.4 collective-permute-start
  6.7 1.1 slice_select_fusion
  7.8 4.7 %collective-permute-start.9 = (bf16[2048,256]{1,0:T(8,128)(2,1)}, bf16[2048,256]{1,0:T(8,128)(2,1)}, u32[]{:S(2)}, u32[]{:S(2)}) collective-permute-start(bf16[2048,256]{1,0:T(8,128)(2,1)} %slice_select_fusion), channel_id=1, source_target_pairs={{0,16},{1,17},{2,18},{3,19},{4,20},{5,21},{6,22},{7,23}} | collective-permute-start | bytes 3145736 | tf_op jit(solution)/shard_map/ppermute | solution.py:242
  12.5 0.1 copy.21
  12.6 0.1 reduce-window.8
  12.6 0.1 add_reduce_fusion
  12.8 0.1 select_reduce_fusion.1
  13.0 0.1 broadcast_select_fusion.2
  13.0 0.1 select_n.73.coefs
  13.2 0.1 select_reduce_fusion.3
  13.4 0.1 iota_compare_fusion.2
  13.4 49.2 %collective-permute-done.9 = bf16[2048,256]{1,0:T(8,128)(2,1)} collective-permute-done((bf16[2048,256]{1,0:T(8,128)(2,1)}, bf16[2048,256]{1,0:T(8,128)(2,1)}, u32[]{:S(2)}, u32[]{:S(2)}) %collective-permute-start.9) | collective-permute-done | bytes 1048608 | tf_op jit(solution)/shard_map/ppermute | solution.py:242
  62.7 0.1 broadcast_select_fusion
  62.8 1.4 collective-permute-start.10
  64.1 0.7 select_reduce_fusion
  64.9 0.1 broadcast_and_fusion
  65.0 0.2 select_bitcast_fusion.weights
  65.3 0.5 collective-permute-start.4
  65.8 0.5 collective-permute-done.10
  66.3 0.1 broadcast_select_fusion.1.lead
  66.4 1.9 lead_units.1
  68.4 0.8 copy-done.2
  69.2 5.8 %all-to-all-start.2 = ((f32[8,2,32,256]{3,2,1,0:T(8,128)}), f32[8,2,32,256]{3,2,1,0:T(8,128)}, u32[]{:S(2)}, u32[]{:S(2)}) async-start(f32[8,2,32,256]{3,2,1,0:T(8,128)} %copy-done.2), calls=%async_computation.2 | async-start | bytes 1048576 | tf_op jit(solution)/shard_map/all_to_all | solution.py:457
  75.0 0.7 dynamic-slice_bitcast_fusion
  75.7 0.1 copy.23.ids
  75.8 7.5 %metric_units.3 = (f32[8,3,32,256]{3,2,1,0:T(8,128)S(1)}, bf16[512,2048]{1,0:T(8,128)(2,1)S(1)}) custom-call(s32[1]{0:T(128)} %bitcast.where, s32[3,2]{1,0:T(4,128)S(1)} %copy.23.ids, bf16[64,2048]{1,0:T(8,128)(2,1)S(1)} %select_bitcast_fusion.weights, f32[64,64]{1,0:T(8,128)S(1)} %select_n.73.coefs, bf16[2048,512]{1,0:T(8,128)(2,1)S(1)} %copy-done, ...), custom_call_target="tpu_custom_call" | custom-call | flops 805306368 | bytes 8388608 | tf_op jit(solution)/shard_map/metric_units/pallas_call | solution.py:192
  83.3 0.9 copy-done.3
  84.2 1.3 copy-done.4
  85.5 4.6 %all-to-all-done.2.got = f32[8,2,32,256]{3,2,1,0:T(8,128)} async-done(((f32[8,2,32,256]{3,2,1,0:T(8,128)}), f32[8,2,32,256]{3,2,1,0:T(8,128)}, u32[]{:S(2)}, u32[]{:S(2)}) %all-to-all-start.2) | async-done | bytes 524320 | tf_op jit(solution)/shard_map/all_to_all | solution.py:457
  90.1 4.2 %all-to-all-start.4 = ((f32[8,3,32,256]{3,2,1,0:T(8,128)}), f32[8,3,32,256]{3,2,1,0:T(8,128)}, u32[]{:S(2)}, u32[]{:S(2)}) async-start(f32[8,3,32,256]{3,2,1,0:T(8,128)} %copy-done.3), calls=%async_computation.4 | async-start | bytes 1572864 | tf_op jit(solution)/shard_map/all_to_all | solution.py:457
  94.4 1.9 sum_units.4
  96.2 18.1 %all-to-all-done.4.got = f32[8,3,32,256]{3,2,1,0:T(8,128)} async-done(((f32[8,3,32,256]{3,2,1,0:T(8,128)}), f32[8,3,32,256]{3,2,1,0:T(8,128)}, u32[]{:S(2)}, u32[]{:S(2)}) %all-to-all-start.4) | async-done | bytes 786464 | tf_op jit(solution)/shard_map/all_to_all | solution.py:457
  114.3 4.1 %all-to-all-start.3 = ((f32[8,2,32,256]{3,2,1,0:T(8,128)}), f32[8,2,32,256]{3,2,1,0:T(8,128)}, u32[]{:S(2)}, u32[]{:S(2)}) async-start(f32[8,2,32,256]{3,2,1,0:T(8,128)} %sum_units.4), calls=%async_computation.3 | async-start | bytes 1048576 | tf_op jit(solution)/shard_map/all_to_all | solution.py:459
  118.5 0.7 dynamic-slice_bitcast_fusion.1
  119.2 0.1 copy.22.ids
  119.2 7.9 %metric_units.2 = f32[8,4,32,256]{3,2,1,0:T(8,128)S(1)} custom-call(s32[1]{0:T(128)} %bitcast.where, s32[4,2]{1,0:T(4,128)S(1)} %copy.22.ids, bf16[64,2048]{1,0:T(8,128)(2,1)S(1)} %select_bitcast_fusion.weights, f32[64,64]{1,0:T(8,128)S(1)} %select_n.73.coefs, bf16[2048,512]{1,0:T(8,128)(2,1)S(1)} %copy-done, ...), custom_call_target="tpu_custom_call" | custom-call | flops 1073741824 | bytes 8388608 | tf_op jit(solution)/shard_map/metric_units/pallas_call | solution.py:192
  127.2 1.0 copy-done.1
  128.2 4.5 %all-to-all-done.3.refs_0_ = f32[8,2,32,256]{3,2,1,0:T(8,128)} async-done(((f32[8,2,32,256]{3,2,1,0:T(8,128)}), f32[8,2,32,256]{3,2,1,0:T(8,128)}, u32[]{:S(2)}, u32[]{:S(2)}) %all-to-all-start.3) | async-done | bytes 524320 | tf_op jit(solution)/shard_map/all_to_all | solution.py:459
  132.6 3.6 %all-to-all-start = ((f32[8,4,32,256]{3,2,1,0:T(8,128)}), f32[8,4,32,256]{3,2,1,0:T(8,128)S(1)}, u32[]{:S(2)}, u32[]{:S(2)}) async-start(f32[8,4,32,256]{3,2,1,0:T(8,128)} %copy-done.1), calls=%async_computation | async-start | bytes 2097152 | tf_op jit(solution)/shard_map/all_to_all | solution.py:457
  136.3 2.1 sum_units.5
  138.3 23.6 %all-to-all-done.got = f32[8,4,32,256]{3,2,1,0:T(8,128)S(1)} async-done(((f32[8,4,32,256]{3,2,1,0:T(8,128)}), f32[8,4,32,256]{3,2,1,0:T(8,128)S(1)}, u32[]{:S(2)}, u32[]{:S(2)}) %all-to-all-start) | async-done | bytes 1048608 | tf_op jit(solution)/shard_map/all_to_all | solution.py:457
  162.0 4.2 %all-to-all-start.5 = ((f32[8,3,32,256]{3,2,1,0:T(8,128)}), f32[8,3,32,256]{3,2,1,0:T(8,128)}, u32[]{:S(2)}, u32[]{:S(2)}) async-start(f32[8,3,32,256]{3,2,1,0:T(8,128)} %sum_units.5), calls=%async_computation.5 | async-start | bytes 1572864 | tf_op jit(solution)/shard_map/all_to_all | solution.py:459
  166.2 2.4 sum_units.3
  168.7 17.4 %all-to-all-done.5.refs_0_ = f32[8,3,32,256]{3,2,1,0:T(8,128)} async-done(((f32[8,3,32,256]{3,2,1,0:T(8,128)}), f32[8,3,32,256]{3,2,1,0:T(8,128)}, u32[]{:S(2)}, u32[]{:S(2)}) %all-to-all-start.5) | async-done | bytes 786464 | tf_op jit(solution)/shard_map/all_to_all | solution.py:459
  186.1 4.4 %all-to-all-start.1 = ((f32[8,4,32,256]{3,2,1,0:T(8,128)}), f32[8,4,32,256]{3,2,1,0:T(8,128)}, u32[]{:S(2)}, u32[]{:S(2)}) async-start(f32[8,4,32,256]{3,2,1,0:T(8,128)} %sum_units.3), calls=%async_computation.1 | async-start | bytes 2097152 | tf_op jit(solution)/shard_map/all_to_all | solution.py:459
  190.5 3.8 %collective-permute-start.12 = (f32[8,2,32,256]{3,2,1,0:T(8,128)}, f32[8,2,32,256]{3,2,1,0:T(8,128)S(1)}, u32[]{:S(2)}, u32[]{:S(2)}) collective-permute-start(f32[8,2,32,256]{3,2,1,0:T(8,128)} %all-to-all-done.3.refs_0_), channel_id=1, source_target_pairs={{0,16},{8,24},{16,0},{24,8},{1,17},{9,25},{17,1},{25,9},{2,18},{10... | collective-permute-start | bytes 1572872 | tf_op jit(solution)/shard_map/ppermute | solution.py:402
  194.3 0.1 collective-permute-start.15
  194.4 12.9 %collective-permute-done.12.refs_2_ = f32[8,2,32,256]{3,2,1,0:T(8,128)S(1)} collective-permute-done((f32[8,2,32,256]{3,2,1,0:T(8,128)}, f32[8,2,32,256]{3,2,1,0:T(8,128)S(1)}, u32[]{:S(2)}, u32[]{:S(2)}) %collective-permute-start.12) | collective-permute-done | bytes 524320 | tf_op jit(solution)/shard_map/ppermute | solution.py:402
  207.3 0.8 copy-done.6
  208.1 7.8 %all-to-all-done.1.refs_0_ = f32[8,4,32,256]{3,2,1,0:T(8,128)} async-done(((f32[8,4,32,256]{3,2,1,0:T(8,128)}), f32[8,4,32,256]{3,2,1,0:T(8,128)}, u32[]{:S(2)}, u32[]{:S(2)}) %all-to-all-start.1) | async-done | bytes 1048608 | tf_op jit(solution)/shard_map/all_to_all | solution.py:459
  215.9 3.7 %collective-permute-start.7 = (f32[8,4,32,256]{3,2,1,0:T(8,128)}, f32[8,4,32,256]{3,2,1,0:T(8,128)S(1)}, u32[]{:S(2)}, u32[]{:S(2)}) collective-permute-start(f32[8,4,32,256]{3,2,1,0:T(8,128)} %all-to-all-done.1.refs_0_), channel_id=1, source_target_pairs={{0,16},{8,24},{16,0},{24,8},{1,17},{9,25},{17,1},{25,9},{2,18},{10... | collective-permute-start | bytes 3145736 | tf_op jit(solution)/shard_map/ppermute | solution.py:402
  219.6 4.7 %collective-permute-done.15.refs_2_ = f32[8,3,32,256]{3,2,1,0:T(8,128)} collective-permute-done((f32[8,3,32,256]{3,2,1,0:T(8,128)}, f32[8,3,32,256]{3,2,1,0:T(8,128)}, u32[]{:S(2)}, u32[]{:S(2)}) %collective-permute-start.15) | collective-permute-done | bytes 786464 | tf_op jit(solution)/shard_map/ppermute | solution.py:402
  224.2 0.8 copy-done.8
  225.1 1.0 copy-done.7
  226.1 1.0 copy-done.9
  227.1 13.6 %solve_group.4 = (bf16[2048,256]{1,0:T(8,128)(2,1)S(1)}, bf16[2048,256]{1,0:T(8,128)(2,1)S(1)}, bf16[512,256]{1,0:T(8,128)(2,1)S(1)}) custom-call(s32[1]{0:T(128)} %bitcast.where, s32[8,2]{1,0:T(8,128)S(1)} %copy-done.13, f32[8,2,32,256]{3,2,1,0:T(8,128)} %all-to-all-done.3.refs_0_, f32[8,2,32,256]{3,2,1,0:T(8,128)S(1)} %copy-done.9, ...), custom_call_target="tpu_custom_call" | custom-call | flops 10000000000 | bytes 8388608 | tf_op jit(solution)/shard_map/solve_group/pallas_call | solution.py:373
  240.8 0.6 collective-permute-start.6
  241.4 3.3 collective-permute-done.7.refs_2_
  244.7 16.5 %solve_group.5 = (bf16[2048,256]{1,0:T(8,128)(2,1)S(1)}, bf16[2048,256]{1,0:T(8,128)(2,1)S(1)}, bf16[512,256]{1,0:T(8,128)(2,1)S(1)}) custom-call(s32[1]{0:T(128)} %bitcast.where, s32[7,2]{1,0:T(8,128)S(1)} %copy-done.12, f32[8,3,32,256]{3,2,1,0:T(8,128)} %all-to-all-done.5.refs_0_, f32[8,3,32,256]{3,2,1,0:T(8,128)S(1)} %collective-permute-done.14.refs_1_, ...), custom_call_target="tpu_custom_call" | custom-call | flops 10000000000 | bytes 8388608 | tf_op jit(solution)/shard_map/solve_group/pallas_call | solution.py:373
  261.2 15.9 %solve_group.6 = (bf16[2048,256]{1,0:T(8,128)(2,1)S(1)}, bf16[2048,256]{1,0:T(8,128)(2,1)S(1)}, bf16[512,256]{1,0:T(8,128)(2,1)S(1)}, f32[256,256]{1,0:T(8,128)S(1)}) custom-call(s32[1]{0:T(128)} %bitcast.where, s32[5,2]{1,0:T(8,128)S(1)} %copy-done.11, f32[8,3,32,256]{3,2,1,0:T(8,128)} %all-to-all-done.5.refs_0_, ...), custom_call_target="tpu_custom_call" | custom-call | flops 10000000000 | bytes 8388608 | tf_op jit(solution)/shard_map/solve_group/pallas_call | solution.py:373
  277.2 70.8 %solve_group.7 = bf16[512,2048]{1,0:T(8,128)(2,1)} custom-call(s32[1]{0:T(128)} %bitcast.where, s32[16,2]{1,0:T(8,128)S(1)} %copy-done.10, f32[8,4,32,256]{3,2,1,0:T(8,128)} %all-to-all-done.1.refs_0_, f32[8,4,32,256]{3,2,1,0:T(8,128)S(1)} %collective-permute-done.6.refs_1_, f32[8,4,32,256]{3,2,1,0:T(8,128)S(1)} %collective-permute-done.7.refs_2_, ...), custom_call_target="tpu_custom_call" | custom-call | flops 49999998976 | bytes 8388608 | tf_op jit(solution)/shard_map/solve_group/pallas_call | solution.py:373
  (56 shorter events, 0.3 us)
Async XLA Ops:
  0.0 6.7 %copy-start = (bf16[2048,512]{1,0:T(8,128)(2,1)S(1)}, bf16[2048,512]{1,0:T(8,128)(2,1)}, u32[]{:S(2)}) copy-start(bf16[2048,512]{1,0:T(8,128)(2,1)} %own.1) | copy-start | bytes 6291460
  3.2 9.3 %copy-start.17 = (s32[64]{0:T(128)S(1)}, s32[64]{0:T(128)}, u32[]{:S(2)}) copy-start(s32[64]{0:T(128)} %param.16) | copy-start | bytes 772
  3.2 9.6 %copy-start.16 = (f32[64,8,8]{0,2,1:T(8,128)S(1)}, f32[64,8,8]{0,2,1:T(8,128)}, u32[]{:S(2)}) copy-start(f32[64,8,8]{0,2,1:T(8,128)} %param.17) | copy-start | bytes 49156
  3.2 10.0 %copy-start.18 = (s32[64]{0:T(128)S(1)}, s32[64]{0:T(128)}, u32[]{:S(2)}) copy-start(s32[64]{0:T(128)} %param.14) | copy-start | bytes 772
  3.2 10.0 %copy-start.19 = (s32[64]{0:T(128)S(1)}, s32[64]{0:T(128)}, u32[]{:S(2)}) copy-start(s32[64]{0:T(128)} %param.15) | copy-start | bytes 772
  3.2 62.1 %collective-permute-start.3 = (bf16[1024,512]{1,0:T(8,128)(2,1)}, bf16[1024,512]{1,0:T(8,128)(2,1)S(1)}, u32[]{:S(2)}, u32[]{:S(2)}) collective-permute-start(bf16[1024,512]{1,0:T(8,128)(2,1)} %get-tuple-element.33), channel_id=1, source_target_pairs={{0,16},{8,24},{16,0},{24,8},{1,17},{9,25},{17,1},{25,9},{2,18},{10... | collective-permute-start | bytes 3145736 | tf_op jit(solution)/shard_map/ppermute | solution.py:402
  6.2 69.6 %collective-permute-start.1 = (bf16[1024,512]{1,0:T(8,128)(2,1)}, bf16[1024,512]{1,0:T(8,128)(2,1)}, u32[]{:S(2)}, u32[]{:S(2)}) collective-permute-start(bf16[1024,512]{1,0:T(8,128)(2,1)} %get-tuple-element.33), channel_id=1, source_target_pairs={{0,8},{8,0},{16,24},{24,16},{1,9},{9,1},{17,25},{25,17},{2,10},{10... | collective-permute-start | bytes 3145736 | tf_op jit(solution)/shard_map/ppermute | solution.py:402
  6.2 59.1 %collective-permute-start.2 = (bf16[1024,512]{1,0:T(8,128)(2,1)}, bf16[1024,512]{1,0:T(8,128)(2,1)}, u32[]{:S(2)}, u32[]{:S(2)}) collective-permute-start(bf16[1024,512]{1,0:T(8,128)(2,1)} %get-tuple-element.34), channel_id=1, source_target_pairs={{0,16},{8,24},{16,0},{24,8},{1,17},{9,25},{17,1},{25,9},{2,18},{10... | collective-permute-start | bytes 3145736 | tf_op jit(solution)/shard_map/ppermute | solution.py:402
  6.4 69.4 %collective-permute-start = (bf16[1024,512]{1,0:T(8,128)(2,1)}, bf16[1024,512]{1,0:T(8,128)(2,1)}, u32[]{:S(2)}, u32[]{:S(2)}) collective-permute-start(bf16[1024,512]{1,0:T(8,128)(2,1)} %get-tuple-element.34), channel_id=1, source_target_pairs={{0,8},{8,0},{16,24},{24,16},{1,9},{9,1},{17,25},{25,17},{2,10},{10... | collective-permute-start | bytes 3145736 | tf_op jit(solution)/shard_map/ppermute | solution.py:402
  7.8 54.9 %collective-permute-start.9 = (bf16[2048,256]{1,0:T(8,128)(2,1)}, bf16[2048,256]{1,0:T(8,128)(2,1)}, u32[]{:S(2)}, u32[]{:S(2)}) collective-permute-start(bf16[2048,256]{1,0:T(8,128)(2,1)} %slice_select_fusion), channel_id=1, source_target_pairs={{0,16},{1,17},{2,18},{3,19},{4,20},{5,21},{6,22},{7,23}} | collective-permute-start | bytes 3145736 | tf_op jit(solution)/shard_map/ppermute | solution.py:242
  13.2 50.9 %copy-start.15 = (bf16[64,8,128]{2,1,0:T(8,128)(2,1)S(1)}, bf16[64,8,128]{2,1,0:T(8,128)(2,1)}, u32[]{:S(2)}) copy-start(bf16[64,8,128]{2,1,0:T(8,128)(2,1)} %param.13) | copy-start | bytes 393220
  62.8 3.6 %collective-permute-start.10 = (bf16[2048,256]{1,0:T(8,128)(2,1)S(1)}, bf16[2048,256]{1,0:T(8,128)(2,1)S(1)}, u32[]{:S(2)}, u32[]{:S(2)}) collective-permute-start(bf16[2048,256]{1,0:T(8,128)(2,1)S(1)} %broadcast_select_fusion), channel_id=1, source_target_pairs={{0,8},{16,24},{1,9},{17,25},{2,10},{18,26},{3,11},{19,27},{4,12},{... | collective-permute-start | bytes 3145736 | tf_op jit(solution)/shard_map/ppermute | solution.py:242
  65.2 10.5 %collective-permute-start.5 = (bf16[1024,512]{1,0:T(8,128)(2,1)S(1)}, bf16[1024,512]{1,0:T(8,128)(2,1)}, u32[]{:S(2)}, u32[]{:S(2)}) collective-permute-start(bf16[1024,512]{1,0:T(8,128)(2,1)S(1)} %collective-permute-done.3.refs_4_), channel_id=1, source_target_pairs={{0,8},{8,0},{16,24},{24,16},{1,9},{9,1},{17,25},{25,17},{2,10},{10... | collective-permute-start | bytes 3145736 | tf_op jit(solution)/shard_map/ppermute | solution.py:402
  65.3 10.5 %collective-permute-start.4 = (bf16[1024,512]{1,0:T(8,128)(2,1)}, bf16[1024,512]{1,0:T(8,128)(2,1)}, u32[]{:S(2)}, u32[]{:S(2)}) collective-permute-start(bf16[1024,512]{1,0:T(8,128)(2,1)} %collective-permute-done.2.refs_3_), channel_id=1, source_target_pairs={{0,8},{8,0},{16,24},{24,16},{1,9},{9,1},{17,25},{25,17},{2,10},{10... | collective-permute-start | bytes 3145736 | tf_op jit(solution)/shard_map/ppermute | solution.py:402
  68.4 0.8 copy-start.2
  69.2 21.0 %all-to-all-start.2 = ((f32[8,2,32,256]{3,2,1,0:T(8,128)}), f32[8,2,32,256]{3,2,1,0:T(8,128)}, u32[]{:S(2)}, u32[]{:S(2)}) async-start(f32[8,2,32,256]{3,2,1,0:T(8,128)} %copy-done.2), calls=%async_computation.2 | async-start | bytes 1048576 | tf_op jit(solution)/shard_map/all_to_all | solution.py:457
  83.3 0.9 copy-start.3
  84.2 1.3 copy-start.4
  90.1 24.2 %all-to-all-start.4 = ((f32[8,3,32,256]{3,2,1,0:T(8,128)}), f32[8,3,32,256]{3,2,1,0:T(8,128)}, u32[]{:S(2)}, u32[]{:S(2)}) async-start(f32[8,3,32,256]{3,2,1,0:T(8,128)} %copy-done.3), calls=%async_computation.4 | async-start | bytes 1572864 | tf_op jit(solution)/shard_map/all_to_all | solution.py:457
  114.3 18.3 %all-to-all-start.3 = ((f32[8,2,32,256]{3,2,1,0:T(8,128)}), f32[8,2,32,256]{3,2,1,0:T(8,128)}, u32[]{:S(2)}, u32[]{:S(2)}) async-start(f32[8,2,32,256]{3,2,1,0:T(8,128)} %sum_units.4), calls=%async_computation.3 | async-start | bytes 1048576 | tf_op jit(solution)/shard_map/all_to_all | solution.py:459
  127.2 1.0 copy-start.1
  132.6 29.3 %all-to-all-start = ((f32[8,4,32,256]{3,2,1,0:T(8,128)}), f32[8,4,32,256]{3,2,1,0:T(8,128)S(1)}, u32[]{:S(2)}, u32[]{:S(2)}) async-start(f32[8,4,32,256]{3,2,1,0:T(8,128)} %copy-done.1), calls=%async_computation | async-start | bytes 2097152 | tf_op jit(solution)/shard_map/all_to_all | solution.py:457
  162.0 4.2 %copy-start.14 = (f32[8,4,32,256]{3,2,1,0:T(8,128)}, f32[8,4,32,256]{3,2,1,0:T(8,128)S(1)}, u32[]{:S(2)}) copy-start(f32[8,4,32,256]{3,2,1,0:T(8,128)S(1)} %all-to-all-done.got) | copy-start | bytes 3145732
  162.0 24.1 %all-to-all-start.5 = ((f32[8,3,32,256]{3,2,1,0:T(8,128)}), f32[8,3,32,256]{3,2,1,0:T(8,128)}, u32[]{:S(2)}, u32[]{:S(2)}) async-start(f32[8,3,32,256]{3,2,1,0:T(8,128)} %sum_units.5), calls=%async_computation.5 | async-start | bytes 1572864 | tf_op jit(solution)/shard_map/all_to_all | solution.py:459
  166.2 58.8 %copy-start.5 = (bf16[512,2048]{1,0:T(8,128)(2,1)S(1)}, bf16[512,2048]{1,0:T(8,128)(2,1)}, u32[]{:S(2)}) copy-start(bf16[512,2048]{1,0:T(8,128)(2,1)} %copy-done.4) | copy-start | bytes 6291460
  166.2 58.8 %copy-start.13 = (s32[8,2]{1,0:T(8,128)S(1)}, s32[8,2]{1,0:T(8,128)}, u32[]{:S(2)}) copy-start(s32[8,2]{1,0:T(8,128)} %constant.58.clone.spots) | copy-start | bytes 196
  186.1 29.8 %all-to-all-start.1 = ((f32[8,4,32,256]{3,2,1,0:T(8,128)}), f32[8,4,32,256]{3,2,1,0:T(8,128)}, u32[]{:S(2)}, u32[]{:S(2)}) async-start(f32[8,4,32,256]{3,2,1,0:T(8,128)} %sum_units.3), calls=%async_computation.1 | async-start | bytes 2097152 | tf_op jit(solution)/shard_map/all_to_all | solution.py:459
  190.5 16.8 %collective-permute-start.12 = (f32[8,2,32,256]{3,2,1,0:T(8,128)}, f32[8,2,32,256]{3,2,1,0:T(8,128)S(1)}, u32[]{:S(2)}, u32[]{:S(2)}) collective-permute-start(f32[8,2,32,256]{3,2,1,0:T(8,128)} %all-to-all-done.3.refs_0_), channel_id=1, source_target_pairs={{0,16},{8,24},{16,0},{24,8},{1,17},{9,25},{17,1},{25,9},{2,18},{10... | collective-permute-start | bytes 1572872 | tf_op jit(solution)/shard_map/ppermute | solution.py:402
  194.3 29.9 %collective-permute-start.15 = (f32[8,3,32,256]{3,2,1,0:T(8,128)}, f32[8,3,32,256]{3,2,1,0:T(8,128)}, u32[]{:S(2)}, u32[]{:S(2)}) collective-permute-start(f32[8,3,32,256]{3,2,1,0:T(8,128)} %all-to-all-done.5.refs_0_), channel_id=1, source_target_pairs={{0,16},{8,24},{16,0},{24,8},{1,17},{9,25},{17,1},{25,9},{2,18},{10... | collective-permute-start | bytes 2359304 | tf_op jit(solution)/shard_map/ppermute | solution.py:402
  194.4 29.9 %collective-permute-start.11 = (f32[8,2,32,256]{3,2,1,0:T(8,128)}, f32[8,2,32,256]{3,2,1,0:T(8,128)S(1)}, u32[]{:S(2)}, u32[]{:S(2)}) collective-permute-start(f32[8,2,32,256]{3,2,1,0:T(8,128)} %all-to-all-done.3.refs_0_), channel_id=1, source_target_pairs={{0,8},{8,0},{16,24},{24,16},{1,9},{9,1},{17,25},{25,17},{2,10},{10... | collective-permute-start | bytes 1572872 | tf_op jit(solution)/shard_map/ppermute | solution.py:402
  207.3 17.8 %collective-permute-start.13 = (f32[8,2,32,256]{3,2,1,0:T(8,128)S(1)}, f32[8,2,32,256]{3,2,1,0:T(8,128)}, u32[]{:S(2)}, u32[]{:S(2)}) collective-permute-start(f32[8,2,32,256]{3,2,1,0:T(8,128)S(1)} %collective-permute-done.12.refs_2_), channel_id=1, source_target_pairs={{0,8},{8,0},{16,24},{24,16},{1,9},{9,1},{17,25},{25,17},{2,10},{10... | collective-permute-start | bytes 1572872 | tf_op jit(solution)/shard_map/ppermute | solution.py:402
  207.3 0.8 copy-start.6
  215.9 28.8 %collective-permute-start.7 = (f32[8,4,32,256]{3,2,1,0:T(8,128)}, f32[8,4,32,256]{3,2,1,0:T(8,128)S(1)}, u32[]{:S(2)}, u32[]{:S(2)}) collective-permute-start(f32[8,4,32,256]{3,2,1,0:T(8,128)} %all-to-all-done.1.refs_0_), channel_id=1, source_target_pairs={{0,16},{8,24},{16,0},{24,8},{1,17},{9,25},{17,1},{25,9},{2,18},{10... | collective-permute-start | bytes 3145736 | tf_op jit(solution)/shard_map/ppermute | solution.py:402
  219.6 25.1 %collective-permute-start.14 = (f32[8,3,32,256]{3,2,1,0:T(8,128)}, f32[8,3,32,256]{3,2,1,0:T(8,128)S(1)}, u32[]{:S(2)}, u32[]{:S(2)}) collective-permute-start(f32[8,3,32,256]{3,2,1,0:T(8,128)} %all-to-all-done.5.refs_0_), channel_id=1, source_target_pairs={{0,8},{8,0},{16,24},{24,16},{1,9},{9,1},{17,25},{25,17},{2,10},{10... | collective-permute-start | bytes 2359304 | tf_op jit(solution)/shard_map/ppermute | solution.py:402
  224.2 20.4 %collective-permute-start.16 = (f32[8,3,32,256]{3,2,1,0:T(8,128)}, f32[8,3,32,256]{3,2,1,0:T(8,128)S(1)}, u32[]{:S(2)}, u32[]{:S(2)}) collective-permute-start(f32[8,3,32,256]{3,2,1,0:T(8,128)} %collective-permute-done.15.refs_2_), channel_id=1, source_target_pairs={{0,8},{8,0},{16,24},{24,16},{1,9},{9,1},{17,25},{25,17},{2,10},{10... | collective-permute-start | bytes 2359304 | tf_op jit(solution)/shard_map/ppermute | solution.py:402
  224.2 0.8 copy-start.8
  225.1 1.0 copy-start.7
  226.1 1.0 copy-start.9
  227.1 17.5 %copy-start.12 = (s32[7,2]{1,0:T(8,128)S(1)}, s32[7,2]{1,0:T(8,128)}, u32[]{:S(2)}) copy-start(s32[7,2]{1,0:T(8,128)} %constant.59.clone.spots) | copy-start | bytes 172
  240.8 36.4 %collective-permute-start.6 = (f32[8,4,32,256]{3,2,1,0:T(8,128)}, f32[8,4,32,256]{3,2,1,0:T(8,128)S(1)}, u32[]{:S(2)}, u32[]{:S(2)}) collective-permute-start(f32[8,4,32,256]{3,2,1,0:T(8,128)} %all-to-all-done.1.refs_0_), channel_id=1, source_target_pairs={{0,8},{8,0},{16,24},{24,16},{1,9},{9,1},{17,25},{25,17},{2,10},{10... | collective-permute-start | bytes 3145736 | tf_op jit(solution)/shard_map/ppermute | solution.py:402
  244.7 32.5 %collective-permute-start.8 = (f32[8,4,32,256]{3,2,1,0:T(8,128)S(1)}, f32[8,4,32,256]{3,2,1,0:T(8,128)S(1)}, u32[]{:S(2)}, u32[]{:S(2)}) collective-permute-start(f32[8,4,32,256]{3,2,1,0:T(8,128)S(1)} %collective-permute-done.7.refs_2_), channel_id=1, source_target_pairs={{0,8},{8,0},{16,24},{24,16},{1,9},{9,1},{17,25},{25,17},{2,10},{10... | collective-permute-start | bytes 3145736 | tf_op jit(solution)/shard_map/ppermute | solution.py:402
  244.7 16.5 %copy-start.11 = (s32[5,2]{1,0:T(8,128)S(1)}, s32[5,2]{1,0:T(8,128)}, u32[]{:S(2)}) copy-start(s32[5,2]{1,0:T(8,128)} %constant.60.clone.spots) | copy-start | bytes 124
  261.2 16.0 %copy-start.10 = (s32[16,2]{1,0:T(8,128)S(1)}, s32[16,2]{1,0:T(8,128)}, u32[]{:S(2)}) copy-start(s32[16,2]{1,0:T(8,128)} %constant.61.clone.spots) | copy-start | bytes 388

commit v5 on v4

--- a/solution.py
+++ b/solution.py
@@ -288,7 +288,6 @@
         base = 0
     fetch(where[0], pieces, buf, sem)
     count = o_ref.shape[1] // BLOCK
-    height = o_ref.shape[0]
     first = 0
 
     def block(k):
@@ -314,38 +313,40 @@
         cp = slice(p * BLOCK, (p + 1) * BLOCK)
         stores = [(oh, ol, oy, oy.shape[1], 0) for oh, ol, oy in olds] + ([(hi, lo, y_out, K, base)] if K else [])
 
-        def reduce_block(i, x):
-            ri = pl.ds(pl.multiple_of(i * BLOCK, BLOCK), BLOCK)
+        def reduce_rows(ri, x):
             for h, l, _, k, _b in stores:
                 x = x - dotg(h[ri, :k], h[cp, :k], 1, 1)
                 x = x - (dotg(h[ri, :k], l[cp, :k], 1, 1) + dotg(l[ri, :k], h[cp, :k], 1, 1))
             return x
 
-        s[...] = reduce_block(p, block(first))
+        s[...] = reduce_rows(cp, block(first))
         invert_block(s[...], m, t, c, pv)
         th, tl = split(t[...])
 
-        def rows_below(n, _):
-            i = p + 1 + n
-            xh, xl = split(reduce_block(i, block(first + 1 + n)))
+        def rows_below(n, high):
+            ri = pl.ds(pl.multiple_of((p + 1 + n) * BLOCK, BLOCK), high * BLOCK)
+            x = jnp.concatenate([block(first + 1 + n + k) for k in range(high)], axis=0)
+            xh, xl = split(reduce_rows(ri, x))
             r = dotg(xh, th, 1, 0) + (dotg(xh, tl, 1, 0) + dotg(xl, th, 1, 0))
-            ri = pl.ds(pl.multiple_of(i * BLOCK, BLOCK), BLOCK)
             hi[ri, mine], lo[ri, mine] = split(r)
+
+        below = count - 1 - p - owing
+
+        def two_below(n, _):
+            rows_below(2 * n, 2)
             return 0
 
-        lax.fori_loop(0, count - 1 - p - owing, rows_below, 0)
-
-        def rows_orbital(n, _):
-            ri = pl.ds(pl.multiple_of(n * BLOCK, BLOCK), BLOCK)
-            x = o_ref[ri, cp].astype(f32)
-            for h, _l, y, k, b in stores:
-                x = x - dotg(y[ri, b : b + k], h[cp, :k], 1, 1)
-            xh, xl = split(x)
-            r = dotg(xh, th, 1, 0) + (dotg(xh, tl, 1, 0) + dotg(xl, th, 1, 0))
-            y_out[ri, base + K : base + K + BLOCK] = r.astype(bf16)
-            return 0
-
-        lax.fori_loop(0, height // BLOCK, rows_orbital, 0)
+        if below > 1:
+            lax.fori_loop(0, below // 2, two_below, 0)
+        if below % 2:
+            rows_below(below - 1, 1)
+
+        x = o_ref[:, cp].astype(f32)
+        for h, _l, y, k, b in stores:
+            x = x - dotg(y[:, b : b + k], h[cp, :k], 1, 1)
+        xh, xl = split(x)
+        r = dotg(xh, th, 1, 0) + (dotg(xh, tl, 1, 0) + dotg(xl, th, 1, 0))
+        y_out[:, base + K : base + K + BLOCK] = r.astype(bf16)
         first += count - p
     if owing:
         t_out[...] = t[...]

time: 349 us -> 340 us (0.974)
  Pallas kernels: 141 us -> 131 us
    pallas_call x4, Pallas kernels: 117 us -> 107 us  [solve_group(): pl.pallas_call(functools.partial(group_kernel, list(panels), len(pieces),...]
where the time goes in v5:
time: 340 us; the launch traced here: 339 us
  waiting for transfers between devices  147 us (43%)
  Pallas kernels  131 us (39%)
  starting transfers between devices  44.8 us (13%)
  local copies, waits for them, and re-layouts  12.6 us (4%)
    pallas_call x4, Pallas kernels, solve_group(): pl.pallas_call(functools.partial(group_kernel, list(panels), len(pieces),...  107 us
    ppermute x2, waiting for transfers between devices, spread_lead(): got = lax.ppermute(held, 'band', pairs)  49.7 us
    all_to_all x3, waiting for transfers between devices, shards(): got = lax.all_to_all(units, 'grid', split_axis=0, concat_axis=0, tiled=True)  46.3 us
    all_to_all x3, waiting for transfers between devices, shards(): part = lax.all_to_all(part, 'grid', split_axis=0, concat_axis=0, tiled=True)  29.7 us
    ppermute x15, waiting for transfers between devices, gather_bands(): got.append(lax.ppermute(x, 'band', swap))  21.7 us
    pallas_call x2, Pallas kernels, metric_units(): pl.pallas_call(functools.partial(metric_kernel, scale, [len(p) for p in p...  15.4 us
    all_to_all x3, starting transfers between devices, shards(): got = lax.all_to_all(units, 'grid', split_axis=0, concat_axis=0, tiled=True)  13.7 us
    all_to_all x3, starting transfers between devices, shards(): part = lax.all_to_all(part, 'grid', split_axis=0, concat_axis=0, tiled=True)  12.8 us
  transfers between devices with their start and end apart: 23, of which 11 were waited for; matrix products, arithmetic and copies ran while one was open for 1% of the time, Pallas kernels for 20%

profile of v5, /device:TPU:0, one launch (start us, length us, event | category | flops | bytes accessed | tf_op | source)
XLA Modules:
  0.0 339.0 jit_solution(17834052025526634861)
XLA Ops:
  0.0 3.2 fusion.1
  3.2 3.0 collective-permute-start.3
  6.2 0.2 collective-permute-start.2
  6.4 0.4 collective-permute-start
  6.7 1.1 slice_select_fusion
  7.8 4.7 %collective-permute-start.9 = (bf16[2048,256]{1,0:T(8,128)(2,1)}, bf16[2048,256]{1,0:T(8,128)(2,1)}, u32[]{:S(2)}, u32[]{:S(2)}) collective-permute-start(bf16[2048,256]{1,0:T(8,128)(2,1)} %slice_select_fusion), channel_id=1, source_target_pairs={{0,16},{1,17},{2,18},{3,19},{4,20},{5,21},{6,22},{7,23}} | collective-permute-start | bytes 3145736 | tf_op jit(solution)/shard_map/ppermute | solution.py:242
  12.5 0.1 copy.21
  12.6 0.1 reduce-window.8
  12.6 0.1 add_reduce_fusion
  12.8 0.1 select_reduce_fusion.1
  13.0 0.1 broadcast_select_fusion.2
  13.0 0.1 select_n.73.coefs
  13.2 0.1 select_reduce_fusion.3
  13.4 0.1 iota_compare_fusion.2
  13.4 49.2 %collective-permute-done.9 = bf16[2048,256]{1,0:T(8,128)(2,1)} collective-permute-done((bf16[2048,256]{1,0:T(8,128)(2,1)}, bf16[2048,256]{1,0:T(8,128)(2,1)}, u32[]{:S(2)}, u32[]{:S(2)}) %collective-permute-start.9) | collective-permute-done | bytes 1048608 | tf_op jit(solution)/shard_map/ppermute | solution.py:242
  62.7 0.1 broadcast_select_fusion
  62.8 1.4 collective-permute-start.10
  64.1 0.7 select_reduce_fusion
  64.9 0.1 broadcast_and_fusion
  65.0 0.2 select_bitcast_fusion.weights
  65.3 0.5 collective-permute-start.4
  65.8 0.5 collective-permute-done.10
  66.3 0.1 broadcast_select_fusion.1.lead
  66.4 1.9 lead_units.1
  68.4 0.8 copy-done.2
  69.2 5.8 %all-to-all-start.2 = ((f32[8,2,32,256]{3,2,1,0:T(8,128)}), f32[8,2,32,256]{3,2,1,0:T(8,128)}, u32[]{:S(2)}, u32[]{:S(2)}) async-start(f32[8,2,32,256]{3,2,1,0:T(8,128)} %copy-done.2), calls=%async_computation.2 | async-start | bytes 1048576 | tf_op jit(solution)/shard_map/all_to_all | solution.py:458
  75.0 0.7 dynamic-slice_bitcast_fusion
  75.7 0.1 copy.23.ids
  75.8 7.5 %metric_units.3 = (f32[8,3,32,256]{3,2,1,0:T(8,128)S(1)}, bf16[512,2048]{1,0:T(8,128)(2,1)S(1)}) custom-call(s32[1]{0:T(128)} %bitcast.where, s32[3,2]{1,0:T(4,128)S(1)} %copy.23.ids, bf16[64,2048]{1,0:T(8,128)(2,1)S(1)} %select_bitcast_fusion.weights, f32[64,64]{1,0:T(8,128)S(1)} %select_n.73.coefs, bf16[2048,512]{1,0:T(8,128)(2,1)S(1)} %copy-done, ...), custom_call_target="tpu_custom_call" | custom-call | flops 805306368 | bytes 8388608 | tf_op jit(solution)/shard_map/metric_units/pallas_call | solution.py:192
  83.3 0.9 copy-done.3
  84.2 1.3 copy-done.4
  85.5 4.6 %all-to-all-done.2.got = f32[8,2,32,256]{3,2,1,0:T(8,128)} async-done(((f32[8,2,32,256]{3,2,1,0:T(8,128)}), f32[8,2,32,256]{3,2,1,0:T(8,128)}, u32[]{:S(2)}, u32[]{:S(2)}) %all-to-all-start.2) | async-done | bytes 524320 | tf_op jit(solution)/shard_map/all_to_all | solution.py:458
  90.1 4.2 %all-to-all-start.4 = ((f32[8,3,32,256]{3,2,1,0:T(8,128)}), f32[8,3,32,256]{3,2,1,0:T(8,128)}, u32[]{:S(2)}, u32[]{:S(2)}) async-start(f32[8,3,32,256]{3,2,1,0:T(8,128)} %copy-done.3), calls=%async_computation.4 | async-start | bytes 1572864 | tf_op jit(solution)/shard_map/all_to_all | solution.py:458
  94.4 1.9 sum_units.4
  96.2 18.1 %all-to-all-done.4.got = f32[8,3,32,256]{3,2,1,0:T(8,128)} async-done(((f32[8,3,32,256]{3,2,1,0:T(8,128)}), f32[8,3,32,256]{3,2,1,0:T(8,128)}, u32[]{:S(2)}, u32[]{:S(2)}) %all-to-all-start.4) | async-done | bytes 786464 | tf_op jit(solution)/shard_map/all_to_all | solution.py:458
  114.3 4.1 %all-to-all-start.3 = ((f32[8,2,32,256]{3,2,1,0:T(8,128)}), f32[8,2,32,256]{3,2,1,0:T(8,128)}, u32[]{:S(2)}, u32[]{:S(2)}) async-start(f32[8,2,32,256]{3,2,1,0:T(8,128)} %sum_units.4), calls=%async_computation.3 | async-start | bytes 1048576 | tf_op jit(solution)/shard_map/all_to_all | solution.py:460
  118.5 0.7 dynamic-slice_bitcast_fusion.1
  119.2 0.1 copy.22.ids
  119.2 7.9 %metric_units.2 = f32[8,4,32,256]{3,2,1,0:T(8,128)S(1)} custom-call(s32[1]{0:T(128)} %bitcast.where, s32[4,2]{1,0:T(4,128)S(1)} %copy.22.ids, bf16[64,2048]{1,0:T(8,128)(2,1)S(1)} %select_bitcast_fusion.weights, f32[64,64]{1,0:T(8,128)S(1)} %select_n.73.coefs, bf16[2048,512]{1,0:T(8,128)(2,1)S(1)} %copy-done, ...), custom_call_target="tpu_custom_call" | custom-call | flops 1073741824 | bytes 8388608 | tf_op jit(solution)/shard_map/metric_units/pallas_call | solution.py:192
  127.2 1.0 copy-done.1
  128.2 4.5 %all-to-all-done.3.refs_0_ = f32[8,2,32,256]{3,2,1,0:T(8,128)} async-done(((f32[8,2,32,256]{3,2,1,0:T(8,128)}), f32[8,2,32,256]{3,2,1,0:T(8,128)}, u32[]{:S(2)}, u32[]{:S(2)}) %all-to-all-start.3) | async-done | bytes 524320 | tf_op jit(solution)/shard_map/all_to_all | solution.py:460
  132.6 3.6 %all-to-all-start = ((f32[8,4,32,256]{3,2,1,0:T(8,128)}), f32[8,4,32,256]{3,2,1,0:T(8,128)S(1)}, u32[]{:S(2)}, u32[]{:S(2)}) async-start(f32[8,4,32,256]{3,2,1,0:T(8,128)} %copy-done.1), calls=%async_computation | async-start | bytes 2097152 | tf_op jit(solution)/shard_map/all_to_all | solution.py:458
  136.3 2.1 sum_units.5
  138.3 23.6 %all-to-all-done.got = f32[8,4,32,256]{3,2,1,0:T(8,128)S(1)} async-done(((f32[8,4,32,256]{3,2,1,0:T(8,128)}), f32[8,4,32,256]{3,2,1,0:T(8,128)S(1)}, u32[]{:S(2)}, u32[]{:S(2)}) %all-to-all-start) | async-done | bytes 1048608 | tf_op jit(solution)/shard_map/all_to_all | solution.py:458
  162.0 4.2 %all-to-all-start.5 = ((f32[8,3,32,256]{3,2,1,0:T(8,128)}), f32[8,3,32,256]{3,2,1,0:T(8,128)}, u32[]{:S(2)}, u32[]{:S(2)}) async-start(f32[8,3,32,256]{3,2,1,0:T(8,128)} %sum_units.5), calls=%async_computation.5 | async-start | bytes 1572864 | tf_op jit(solution)/shard_map/all_to_all | solution.py:460
  166.2 2.4 sum_units.3
  168.7 17.4 %all-to-all-done.5.refs_0_ = f32[8,3,32,256]{3,2,1,0:T(8,128)} async-done(((f32[8,3,32,256]{3,2,1,0:T(8,128)}), f32[8,3,32,256]{3,2,1,0:T(8,128)}, u32[]{:S(2)}, u32[]{:S(2)}) %all-to-all-start.5) | async-done | bytes 786464 | tf_op jit(solution)/shard_map/all_to_all | solution.py:460
  186.1 4.4 %all-to-all-start.1 = ((f32[8,4,32,256]{3,2,1,0:T(8,128)}), f32[8,4,32,256]{3,2,1,0:T(8,128)}, u32[]{:S(2)}, u32[]{:S(2)}) async-start(f32[8,4,32,256]{3,2,1,0:T(8,128)} %sum_units.3), calls=%async_computation.1 | async-start | bytes 2097152 | tf_op jit(solution)/shard_map/all_to_all | solution.py:460
  190.5 3.8 %collective-permute-start.12 = (f32[8,2,32,256]{3,2,1,0:T(8,128)}, f32[8,2,32,256]{3,2,1,0:T(8,128)S(1)}, u32[]{:S(2)}, u32[]{:S(2)}) collective-permute-start(f32[8,2,32,256]{3,2,1,0:T(8,128)} %all-to-all-done.3.refs_0_), channel_id=1, source_target_pairs={{0,16},{8,24},{16,0},{24,8},{1,17},{9,25},{17,1},{25,9},{2,18},{10... | collective-permute-start | bytes 1572872 | tf_op jit(solution)/shard_map/ppermute | solution.py:403
  194.3 0.1 collective-permute-start.15
  194.4 12.9 %collective-permute-done.12.refs_2_ = f32[8,2,32,256]{3,2,1,0:T(8,128)S(1)} collective-permute-done((f32[8,2,32,256]{3,2,1,0:T(8,128)}, f32[8,2,32,256]{3,2,1,0:T(8,128)S(1)}, u32[]{:S(2)}, u32[]{:S(2)}) %collective-permute-start.12) | collective-permute-done | bytes 524320 | tf_op jit(solution)/shard_map/ppermute | solution.py:403
  207.3 0.8 copy-done.6
  208.1 7.8 %all-to-all-done.1.refs_0_ = f32[8,4,32,256]{3,2,1,0:T(8,128)} async-done(((f32[8,4,32,256]{3,2,1,0:T(8,128)}), f32[8,4,32,256]{3,2,1,0:T(8,128)}, u32[]{:S(2)}, u32[]{:S(2)}) %all-to-all-start.1) | async-done | bytes 1048608 | tf_op jit(solution)/shard_map/all_to_all | solution.py:460
  215.9 3.7 %collective-permute-start.7 = (f32[8,4,32,256]{3,2,1,0:T(8,128)}, f32[8,4,32,256]{3,2,1,0:T(8,128)S(1)}, u32[]{:S(2)}, u32[]{:S(2)}) collective-permute-start(f32[8,4,32,256]{3,2,1,0:T(8,128)} %all-to-all-done.1.refs_0_), channel_id=1, source_target_pairs={{0,16},{8,24},{16,0},{24,8},{1,17},{9,25},{17,1},{25,9},{2,18},{10... | collective-permute-start | bytes 3145736 | tf_op jit(solution)/shard_map/ppermute | solution.py:403
  219.6 4.7 %collective-permute-done.15.refs_2_ = f32[8,3,32,256]{3,2,1,0:T(8,128)} collective-permute-done((f32[8,3,32,256]{3,2,1,0:T(8,128)}, f32[8,3,32,256]{3,2,1,0:T(8,128)}, u32[]{:S(2)}, u32[]{:S(2)}) %collective-permute-start.15) | collective-permute-done | bytes 786464 | tf_op jit(solution)/shard_map/ppermute | solution.py:403
  224.2 0.8 copy-done.8
  225.1 1.0 copy-done.7
  226.1 1.0 copy-done.9
  227.1 12.8 %solve_group.4 = (bf16[2048,256]{1,0:T(8,128)(2,1)S(1)}, bf16[2048,256]{1,0:T(8,128)(2,1)S(1)}, bf16[512,256]{1,0:T(8,128)(2,1)S(1)}) custom-call(s32[1]{0:T(128)} %bitcast.where, s32[8,2]{1,0:T(8,128)S(1)} %copy-done.13, f32[8,2,32,256]{3,2,1,0:T(8,128)} %all-to-all-done.3.refs_0_, f32[8,2,32,256]{3,2,1,0:T(8,128)S(1)} %copy-done.9, ...), custom_call_target="tpu_custom_call" | custom-call | flops 10000000000 | bytes 8388608 | tf_op jit(solution)/shard_map/solve_group/pallas_call | solution.py:374
  239.9 0.6 collective-permute-start.6
  240.5 4.1 %collective-permute-done.7.refs_2_ = f32[8,4,32,256]{3,2,1,0:T(8,128)S(1)} collective-permute-done((f32[8,4,32,256]{3,2,1,0:T(8,128)}, f32[8,4,32,256]{3,2,1,0:T(8,128)S(1)}, u32[]{:S(2)}, u32[]{:S(2)}) %collective-permute-start.7) | collective-permute-done | bytes 1048608 | tf_op jit(solution)/shard_map/ppermute | solution.py:403
  244.7 15.2 %solve_group.5 = (bf16[2048,256]{1,0:T(8,128)(2,1)S(1)}, bf16[2048,256]{1,0:T(8,128)(2,1)S(1)}, bf16[512,256]{1,0:T(8,128)(2,1)S(1)}) custom-call(s32[1]{0:T(128)} %bitcast.where, s32[7,2]{1,0:T(8,128)S(1)} %copy-done.12, f32[8,3,32,256]{3,2,1,0:T(8,128)} %all-to-all-done.5.refs_0_, f32[8,3,32,256]{3,2,1,0:T(8,128)S(1)} %collective-permute-done.14.refs_1_, ...), custom_call_target="tpu_custom_call" | custom-call | flops 10000000000 | bytes 8388608 | tf_op jit(solution)/shard_map/solve_group/pallas_call | solution.py:374
  259.9 15.0 %solve_group.6 = (bf16[2048,256]{1,0:T(8,128)(2,1)S(1)}, bf16[2048,256]{1,0:T(8,128)(2,1)S(1)}, bf16[512,256]{1,0:T(8,128)(2,1)S(1)}, f32[256,256]{1,0:T(8,128)S(1)}) custom-call(s32[1]{0:T(128)} %bitcast.where, s32[5,2]{1,0:T(8,128)S(1)} %copy-done.11, f32[8,3,32,256]{3,2,1,0:T(8,128)} %all-to-all-done.5.refs_0_, ...), custom_call_target="tpu_custom_call" | custom-call | flops 10000000000 | bytes 8388608 | tf_op jit(solution)/shard_map/solve_group/pallas_call | solution.py:374
  275.0 63.8 %solve_group.7 = bf16[512,2048]{1,0:T(8,128)(2,1)} custom-call(s32[1]{0:T(128)} %bitcast.where, s32[16,2]{1,0:T(8,128)S(1)} %copy-done.10, f32[8,4,32,256]{3,2,1,0:T(8,128)} %all-to-all-done.1.refs_0_, f32[8,4,32,256]{3,2,1,0:T(8,128)S(1)} %collective-permute-done.6.refs_1_, f32[8,4,32,256]{3,2,1,0:T(8,128)S(1)} %collective-permute-done.7.refs_2_, ...), custom_call_target="tpu_custom_call" | custom-call | flops 49999998976 | bytes 8388608 | tf_op jit(solution)/shard_map/solve_group/pallas_call | solution.py:374
  (56 shorter events, 0.3 us)
Async XLA Ops:
  0.0 6.7 %copy-start = (bf16[2048,512]{1,0:T(8,128)(2,1)S(1)}, bf16[2048,512]{1,0:T(8,128)(2,1)}, u32[]{:S(2)}) copy-start(bf16[2048,512]{1,0:T(8,128)(2,1)} %own.1) | copy-start | bytes 6291460
  3.2 9.3 %copy-start.17 = (s32[64]{0:T(128)S(1)}, s32[64]{0:T(128)}, u32[]{:S(2)}) copy-start(s32[64]{0:T(128)} %param.16) | copy-start | bytes 772
  3.2 9.6 %copy-start.16 = (f32[64,8,8]{0,2,1:T(8,128)S(1)}, f32[64,8,8]{0,2,1:T(8,128)}, u32[]{:S(2)}) copy-start(f32[64,8,8]{0,2,1:T(8,128)} %param.17) | copy-start | bytes 49156
  3.2 10.0 %copy-start.18 = (s32[64]{0:T(128)S(1)}, s32[64]{0:T(128)}, u32[]{:S(2)}) copy-start(s32[64]{0:T(128)} %param.14) | copy-start | bytes 772
  3.2 10.0 %copy-start.19 = (s32[64]{0:T(128)S(1)}, s32[64]{0:T(128)}, u32[]{:S(2)}) copy-start(s32[64]{0:T(128)} %param.15) | copy-start | bytes 772
  3.2 62.1 %collective-permute-start.3 = (bf16[1024,512]{1,0:T(8,128)(2,1)}, bf16[1024,512]{1,0:T(8,128)(2,1)S(1)}, u32[]{:S(2)}, u32[]{:S(2)}) collective-permute-start(bf16[1024,512]{1,0:T(8,128)(2,1)} %get-tuple-element.33), channel_id=1, source_target_pairs={{0,16},{8,24},{16,0},{24,8},{1,17},{9,25},{17,1},{25,9},{2,18},{10... | collective-permute-start | bytes 3145736 | tf_op jit(solution)/shard_map/ppermute | solution.py:403
  6.2 69.6 %collective-permute-start.1 = (bf16[1024,512]{1,0:T(8,128)(2,1)}, bf16[1024,512]{1,0:T(8,128)(2,1)}, u32[]{:S(2)}, u32[]{:S(2)}) collective-permute-start(bf16[1024,512]{1,0:T(8,128)(2,1)} %get-tuple-element.33), channel_id=1, source_target_pairs={{0,8},{8,0},{16,24},{24,16},{1,9},{9,1},{17,25},{25,17},{2,10},{10... | collective-permute-start | bytes 3145736 | tf_op jit(solution)/shard_map/ppermute | solution.py:403
  6.2 59.1 %collective-permute-start.2 = (bf16[1024,512]{1,0:T(8,128)(2,1)}, bf16[1024,512]{1,0:T(8,128)(2,1)}, u32[]{:S(2)}, u32[]{:S(2)}) collective-permute-start(bf16[1024,512]{1,0:T(8,128)(2,1)} %get-tuple-element.34), channel_id=1, source_target_pairs={{0,16},{8,24},{16,0},{24,8},{1,17},{9,25},{17,1},{25,9},{2,18},{10... | collective-permute-start | bytes 3145736 | tf_op jit(solution)/shard_map/ppermute | solution.py:403
  6.4 69.4 %collective-permute-start = (bf16[1024,512]{1,0:T(8,128)(2,1)}, bf16[1024,512]{1,0:T(8,128)(2,1)}, u32[]{:S(2)}, u32[]{:S(2)}) collective-permute-start(bf16[1024,512]{1,0:T(8,128)(2,1)} %get-tuple-element.34), channel_id=1, source_target_pairs={{0,8},{8,0},{16,24},{24,16},{1,9},{9,1},{17,25},{25,17},{2,10},{10... | collective-permute-start | bytes 3145736 | tf_op jit(solution)/shard_map/ppermute | solution.py:403
  7.8 54.9 %collective-permute-start.9 = (bf16[2048,256]{1,0:T(8,128)(2,1)}, bf16[2048,256]{1,0:T(8,128)(2,1)}, u32[]{:S(2)}, u32[]{:S(2)}) collective-permute-start(bf16[2048,256]{1,0:T(8,128)(2,1)} %slice_select_fusion), channel_id=1, source_target_pairs={{0,16},{1,17},{2,18},{3,19},{4,20},{5,21},{6,22},{7,23}} | collective-permute-start | bytes 3145736 | tf_op jit(solution)/shard_map/ppermute | solution.py:242
  13.2 50.9 %copy-start.15 = (bf16[64,8,128]{2,1,0:T(8,128)(2,1)S(1)}, bf16[64,8,128]{2,1,0:T(8,128)(2,1)}, u32[]{:S(2)}) copy-start(bf16[64,8,128]{2,1,0:T(8,128)(2,1)} %param.13) | copy-start | bytes 393220
  62.8 3.6 %collective-permute-start.10 = (bf16[2048,256]{1,0:T(8,128)(2,1)S(1)}, bf16[2048,256]{1,0:T(8,128)(2,1)S(1)}, u32[]{:S(2)}, u32[]{:S(2)}) collective-permute-start(bf16[2048,256]{1,0:T(8,128)(2,1)S(1)} %broadcast_select_fusion), channel_id=1, source_target_pairs={{0,8},{16,24},{1,9},{17,25},{2,10},{18,26},{3,11},{19,27},{4,12},{... | collective-permute-start | bytes 3145736 | tf_op jit(solution)/shard_map/ppermute | solution.py:242
  65.2 10.5 %collective-permute-start.5 = (bf16[1024,512]{1,0:T(8,128)(2,1)S(1)}, bf16[1024,512]{1,0:T(8,128)(2,1)}, u32[]{:S(2)}, u32[]{:S(2)}) collective-permute-start(bf16[1024,512]{1,0:T(8,128)(2,1)S(1)} %collective-permute-done.3.refs_4_), channel_id=1, source_target_pairs={{0,8},{8,0},{16,24},{24,16},{1,9},{9,1},{17,25},{25,17},{2,10},{10... | collective-permute-start | bytes 3145736 | tf_op jit(solution)/shard_map/ppermute | solution.py:403
  65.3 10.5 %collective-permute-start.4 = (bf16[1024,512]{1,0:T(8,128)(2,1)}, bf16[1024,512]{1,0:T(8,128)(2,1)}, u32[]{:S(2)}, u32[]{:S(2)}) collective-permute-start(bf16[1024,512]{1,0:T(8,128)(2,1)} %collective-permute-done.2.refs_3_), channel_id=1, source_target_pairs={{0,8},{8,0},{16,24},{24,16},{1,9},{9,1},{17,25},{25,17},{2,10},{10... | collective-permute-start | bytes 3145736 | tf_op jit(solution)/shard_map/ppermute | solution.py:403
  68.4 0.8 copy-start.2
  69.2 21.0 %all-to-all-start.2 = ((f32[8,2,32,256]{3,2,1,0:T(8,128)}), f32[8,2,32,256]{3,2,1,0:T(8,128)}, u32[]{:S(2)}, u32[]{:S(2)}) async-start(f32[8,2,32,256]{3,2,1,0:T(8,128)} %copy-done.2), calls=%async_computation.2 | async-start | bytes 1048576 | tf_op jit(solution)/shard_map/all_to_all | solution.py:458
  83.3 0.9 copy-start.3
  84.2 1.3 copy-start.4
  90.1 24.2 %all-to-all-start.4 = ((f32[8,3,32,256]{3,2,1,0:T(8,128)}), f32[8,3,32,256]{3,2,1,0:T(8,128)}, u32[]{:S(2)}, u32[]{:S(2)}) async-start(f32[8,3,32,256]{3,2,1,0:T(8,128)} %copy-done.3), calls=%async_computation.4 | async-start | bytes 1572864 | tf_op jit(solution)/shard_map/all_to_all | solution.py:458
  114.3 18.3 %all-to-all-start.3 = ((f32[8,2,32,256]{3,2,1,0:T(8,128)}), f32[8,2,32,256]{3,2,1,0:T(8,128)}, u32[]{:S(2)}, u32[]{:S(2)}) async-start(f32[8,2,32,256]{3,2,1,0:T(8,128)} %sum_units.4), calls=%async_computation.3 | async-start | bytes 1048576 | tf_op jit(solution)/shard_map/all_to_all | solution.py:460
  127.2 1.0 copy-start.1
  132.6 29.3 %all-to-all-start = ((f32[8,4,32,256]{3,2,1,0:T(8,128)}), f32[8,4,32,256]{3,2,1,0:T(8,128)S(1)}, u32[]{:S(2)}, u32[]{:S(2)}) async-start(f32[8,4,32,256]{3,2,1,0:T(8,128)} %copy-done.1), calls=%async_computation | async-start | bytes 2097152 | tf_op jit(solution)/shard_map/all_to_all | solution.py:458
  162.0 4.2 %copy-start.14 = (f32[8,4,32,256]{3,2,1,0:T(8,128)}, f32[8,4,32,256]{3,2,1,0:T(8,128)S(1)}, u32[]{:S(2)}) copy-start(f32[8,4,32,256]{3,2,1,0:T(8,128)S(1)} %all-to-all-done.got) | copy-start | bytes 3145732
  162.0 24.1 %all-to-all-start.5 = ((f32[8,3,32,256]{3,2,1,0:T(8,128)}), f32[8,3,32,256]{3,2,1,0:T(8,128)}, u32[]{:S(2)}, u32[]{:S(2)}) async-start(f32[8,3,32,256]{3,2,1,0:T(8,128)} %sum_units.5), calls=%async_computation.5 | async-start | bytes 1572864 | tf_op jit(solution)/shard_map/all_to_all | solution.py:460
  166.2 58.8 %copy-start.5 = (bf16[512,2048]{1,0:T(8,128)(2,1)S(1)}, bf16[512,2048]{1,0:T(8,128)(2,1)}, u32[]{:S(2)}) copy-start(bf16[512,2048]{1,0:T(8,128)(2,1)} %copy-done.4) | copy-start | bytes 6291460
  166.2 58.8 %copy-start.13 = (s32[8,2]{1,0:T(8,128)S(1)}, s32[8,2]{1,0:T(8,128)}, u32[]{:S(2)}) copy-start(s32[8,2]{1,0:T(8,128)} %constant.58.clone.spots) | copy-start | bytes 196
  186.1 29.8 %all-to-all-start.1 = ((f32[8,4,32,256]{3,2,1,0:T(8,128)}), f32[8,4,32,256]{3,2,1,0:T(8,128)}, u32[]{:S(2)}, u32[]{:S(2)}) async-start(f32[8,4,32,256]{3,2,1,0:T(8,128)} %sum_units.3), calls=%async_computation.1 | async-start | bytes 2097152 | tf_op jit(solution)/shard_map/all_to_all | solution.py:460
  190.5 16.8 %collective-permute-start.12 = (f32[8,2,32,256]{3,2,1,0:T(8,128)}, f32[8,2,32,256]{3,2,1,0:T(8,128)S(1)}, u32[]{:S(2)}, u32[]{:S(2)}) collective-permute-start(f32[8,2,32,256]{3,2,1,0:T(8,128)} %all-to-all-done.3.refs_0_), channel_id=1, source_target_pairs={{0,16},{8,24},{16,0},{24,8},{1,17},{9,25},{17,1},{25,9},{2,18},{10... | collective-permute-start | bytes 1572872 | tf_op jit(solution)/shard_map/ppermute | solution.py:403
  194.3 29.9 %collective-permute-start.15 = (f32[8,3,32,256]{3,2,1,0:T(8,128)}, f32[8,3,32,256]{3,2,1,0:T(8,128)}, u32[]{:S(2)}, u32[]{:S(2)}) collective-permute-start(f32[8,3,32,256]{3,2,1,0:T(8,128)} %all-to-all-done.5.refs_0_), channel_id=1, source_target_pairs={{0,16},{8,24},{16,0},{24,8},{1,17},{9,25},{17,1},{25,9},{2,18},{10... | collective-permute-start | bytes 2359304 | tf_op jit(solution)/shard_map/ppermute | solution.py:403
  194.4 29.9 %collective-permute-start.11 = (f32[8,2,32,256]{3,2,1,0:T(8,128)}, f32[8,2,32,256]{3,2,1,0:T(8,128)S(1)}, u32[]{:S(2)}, u32[]{:S(2)}) collective-permute-start(f32[8,2,32,256]{3,2,1,0:T(8,128)} %all-to-all-done.3.refs_0_), channel_id=1, source_target_pairs={{0,8},{8,0},{16,24},{24,16},{1,9},{9,1},{17,25},{25,17},{2,10},{10... | collective-permute-start | bytes 1572872 | tf_op jit(solution)/shard_map/ppermute | solution.py:403
  207.3 17.8 %collective-permute-start.13 = (f32[8,2,32,256]{3,2,1,0:T(8,128)S(1)}, f32[8,2,32,256]{3,2,1,0:T(8,128)}, u32[]{:S(2)}, u32[]{:S(2)}) collective-permute-start(f32[8,2,32,256]{3,2,1,0:T(8,128)S(1)} %collective-permute-done.12.refs_2_), channel_id=1, source_target_pairs={{0,8},{8,0},{16,24},{24,16},{1,9},{9,1},{17,25},{25,17},{2,10},{10... | collective-permute-start | bytes 1572872 | tf_op jit(solution)/shard_map/ppermute | solution.py:403
  207.3 0.8 copy-start.6
  215.9 28.8 %collective-permute-start.7 = (f32[8,4,32,256]{3,2,1,0:T(8,128)}, f32[8,4,32,256]{3,2,1,0:T(8,128)S(1)}, u32[]{:S(2)}, u32[]{:S(2)}) collective-permute-start(f32[8,4,32,256]{3,2,1,0:T(8,128)} %all-to-all-done.1.refs_0_), channel_id=1, source_target_pairs={{0,16},{8,24},{16,0},{24,8},{1,17},{9,25},{17,1},{25,9},{2,18},{10... | collective-permute-start | bytes 3145736 | tf_op jit(solution)/shard_map/ppermute | solution.py:403
  219.6 25.1 %collective-permute-start.14 = (f32[8,3,32,256]{3,2,1,0:T(8,128)}, f32[8,3,32,256]{3,2,1,0:T(8,128)S(1)}, u32[]{:S(2)}, u32[]{:S(2)}) collective-permute-start(f32[8,3,32,256]{3,2,1,0:T(8,128)} %all-to-all-done.5.refs_0_), channel_id=1, source_target_pairs={{0,8},{8,0},{16,24},{24,16},{1,9},{9,1},{17,25},{25,17},{2,10},{10... | collective-permute-start | bytes 2359304 | tf_op jit(solution)/shard_map/ppermute | solution.py:403
  224.2 20.4 %collective-permute-start.16 = (f32[8,3,32,256]{3,2,1,0:T(8,128)}, f32[8,3,32,256]{3,2,1,0:T(8,128)S(1)}, u32[]{:S(2)}, u32[]{:S(2)}) collective-permute-start(f32[8,3,32,256]{3,2,1,0:T(8,128)} %collective-permute-done.15.refs_2_), channel_id=1, source_target_pairs={{0,8},{8,0},{16,24},{24,16},{1,9},{9,1},{17,25},{25,17},{2,10},{10... | collective-permute-start | bytes 2359304 | tf_op jit(solution)/shard_map/ppermute | solution.py:403
  224.2 0.8 copy-start.8
  225.1 1.0 copy-start.7
  226.1 1.0 copy-start.9
  227.1 17.5 %copy-start.12 = (s32[7,2]{1,0:T(8,128)S(1)}, s32[7,2]{1,0:T(8,128)}, u32[]{:S(2)}) copy-start(s32[7,2]{1,0:T(8,128)} %constant.59.clone.spots) | copy-start | bytes 172
  239.9 35.1 %collective-permute-start.6 = (f32[8,4,32,256]{3,2,1,0:T(8,128)}, f32[8,4,32,256]{3,2,1,0:T(8,128)S(1)}, u32[]{:S(2)}, u32[]{:S(2)}) collective-permute-start(f32[8,4,32,256]{3,2,1,0:T(8,128)} %all-to-all-done.1.refs_0_), channel_id=1, source_target_pairs={{0,8},{8,0},{16,24},{24,16},{1,9},{9,1},{17,25},{25,17},{2,10},{10... | collective-permute-start | bytes 3145736 | tf_op jit(solution)/shard_map/ppermute | solution.py:403
  244.7 30.4 %collective-permute-start.8 = (f32[8,4,32,256]{3,2,1,0:T(8,128)S(1)}, f32[8,4,32,256]{3,2,1,0:T(8,128)S(1)}, u32[]{:S(2)}, u32[]{:S(2)}) collective-permute-start(f32[8,4,32,256]{3,2,1,0:T(8,128)S(1)} %collective-permute-done.7.refs_2_), channel_id=1, source_target_pairs={{0,8},{8,0},{16,24},{24,16},{1,9},{9,1},{17,25},{25,17},{2,10},{10... | collective-permute-start | bytes 3145736 | tf_op jit(solution)/shard_map/ppermute | solution.py:403
  244.7 15.2 %copy-start.11 = (s32[5,2]{1,0:T(8,128)S(1)}, s32[5,2]{1,0:T(8,128)}, u32[]{:S(2)}) copy-start(s32[5,2]{1,0:T(8,128)} %constant.60.clone.spots) | copy-start | bytes 124
  259.9 15.1 %copy-start.10 = (s32[16,2]{1,0:T(8,128)S(1)}, s32[16,2]{1,0:T(8,128)}, u32[]{:S(2)}) copy-start(s32[16,2]{1,0:T(8,128)} %constant.61.clone.spots) | copy-start | bytes 388
